TPU v7x, 128 devices: a whole 4x4x4 slice. The times are simulated.
128 devices in a mesh: proto: 64 (over z, y, x), data: 2 (over core).
Axes of the slice: x: 4, y: 4, z: 4, core: 2. Of those that a mesh axis runs over, the one named last changes fastest.
Arguments:
- emb_one: bfloat16 [4096, 256], P('data')
- emb_two: bfloat16 [4096, 256], P('data')
- protos: bfloat16 [16384, 256], P('proto')
Outputs:
- output 1: float32 [4096, 16384], P('data', 'proto')
- output 2: float32 [4096, 16384], P('data', 'proto')
- output 3: float32 [], replicated
- output 4: float32 [4096, 256], P('data')
- output 5: float32 [4096, 256], P('data')
- output 6: float32 [16384, 256], P('proto')
All inputs are finite; a program needn't handle non-finite values.
Results may differ from a plain program's by a relative error of at most 0.001.
Values are sent between devices in bfloat16 or wider.
A program may use at most 1 GiB of HBM per device.

v0:
```python
import jax
import jax.numpy as jnp
from jax import lax
from jax.sharding import PartitionSpec as P, NamedSharding

EPSILON = 0.05
TEMP_TAU = 0.1
value_a14 = 3


def solution(mesh):
    proto_size = mesh.shape['proto']
    data_size = mesh.shape['data']

    def local_step(emb_one, emb_two, protos):
        local_rows = emb_one.shape[0]
        total_rows = local_rows * data_size
        total_protos = protos.shape[0] * proto_size

        def view_terms(emb):
            scores = jnp.einsum('nd,kd->nk', emb, protos, preferred_element_type=jnp.float32)
            transport = jnp.exp(scores / EPSILON)
            for _ in range(value_a14):
                col_sum = lax.psum(jnp.sum(transport, axis=0), 'data')
                transport = transport / (total_protos * col_sum)
                row_sum = lax.psum(jnp.sum(transport, axis=1, keepdims=True), 'proto')
                transport = transport / (total_rows * row_sum)
            codes = total_rows * transport
            logits = scores / TEMP_TAU
            soft_denom = lax.psum(jnp.sum(jnp.exp(logits), axis=1, keepdims=True), 'proto')
            return codes, logits - jnp.log(soft_denom)

        codes_one, logp_one = view_terms(emb_one)
        codes_two, logp_two = view_terms(emb_two)
        part_loss = jnp.sum(codes_two * logp_one) + jnp.sum(codes_one * logp_two)
        loss_value = -lax.psum(part_loss, ('proto', 'data')) / (2 * total_rows)
        grad_scale = 2 * total_rows * TEMP_TAU
        logit_grad_one = ((jnp.exp(logp_one) - codes_two) / grad_scale).astype(jnp.bfloat16)
        logit_grad_two = ((jnp.exp(logp_two) - codes_one) / grad_scale).astype(jnp.bfloat16)
        grad_one = lax.psum(jnp.einsum('nk,kd->nd', logit_grad_one, protos, preferred_element_type=jnp.float32), 'proto')
        grad_two = lax.psum(jnp.einsum('nk,kd->nd', logit_grad_two, protos, preferred_element_type=jnp.float32), 'proto')
        proto_part = (jnp.einsum('nk,nd->kd', logit_grad_one, emb_one, preferred_element_type=jnp.float32)
                      + jnp.einsum('nk,nd->kd', logit_grad_two, emb_two, preferred_element_type=jnp.float32))
        grad_protos = lax.psum(proto_part, 'data')
        return codes_one, codes_two, loss_value, grad_one, grad_two, grad_protos

    return jax.shard_map(
        local_step, mesh=mesh,
        in_specs=(P('data', None), P('data', None), P('proto', None)),
        out_specs=(P('data', 'proto'), P('data', 'proto'), P(), P('data', None), P('data', None), P('proto', None)),
        check_vma=False)
```

profile of v0, /device:TPU:0, one launch (start us, length us, event | category | flops | bytes accessed | tf_op | source)
XLA Modules:
  0.0 1616.8 jit_solution(9126442925567049024)
XLA Ops:
  9.1 2.5 psum.126
  12.2 182.6 %psum.127 = f32[2048,1]{0,1:T(1,128)S(1)} all-reduce(f32[2048,1]{0,1:T(1,128)S(1)} %bitcast.52), channel_id=1, replica_groups=mesh['proto'=64,'data'=2] {'proto'}, use_global_device_ids=true, to_apply=%region_3.0 | all-reduce | flops 2048 | bytes 16384 | tf_op jit(solution)/shard_map/psum | solution.py:26
  195.5 2.5 psum.128
  198.6 173.8 %psum.129 = f32[2048,1]{0,1:T(1,128)S(1)} all-reduce(f32[2048,1]{0,1:T(1,128)S(1)} %bitcast.53), channel_id=1, replica_groups=mesh['proto'=64,'data'=2] {'proto'}, use_global_device_ids=true, to_apply=%region_7.0 | all-reduce | flops 2048 | bytes 16384 | tf_op jit(solution)/shard_map/psum | solution.py:26
  373.1 2.1 exponential_reduce_fusion
  375.2 2.4 all-reduce.3
  378.4 343.4 %all-reduce.1 = (f32[2048,1]{0,1:T(1,128)S(1)}, f32[2048,1]{0,1:T(1,128)S(1)}) all-reduce(f32[2048,1]{0,1:T(1,128)S(1)} %bitcast.50, f32[2048,1]{0,1:T(1,128)S(1)} %bitcast.57), channel_id=1, replica_groups=mesh['proto'=64,'data'=2] {'proto'}, use_global_device_ids=true, to_apply=%region_11.0 | all-reduce | flops 4096 | bytes 32768 | tf_op jit(solution)/shard_map/psum | solution.py:26
  721.9 4.3 multiply_convert_fusion
  727.6 173.8 %psum.133 = f32[2048,1]{0,1:T(1,128)S(1)} all-reduce(f32[2048,1]{0,1:T(1,128)S(1)} %bitcast.51), channel_id=1, replica_groups=mesh['proto'=64,'data'=2] {'proto'}, use_global_device_ids=true, to_apply=%region_15.0 | all-reduce | flops 2048 | bytes 16384 | tf_op jit(solution)/shard_map/psum | solution.py:26
  901.4 2.2 fusion.17
  903.7 2.5 psum.134
  906.1 2.2 fusion.18
  908.3 175.7 %psum.135 = f32[2048,1]{0,1:T(1,128)S(1)} all-reduce(f32[2048,1]{0,1:T(1,128)S(1)} %bitcast.54), channel_id=1, replica_groups=mesh['proto'=64,'data'=2] {'proto'}, use_global_device_ids=true, to_apply=%region_19.0 | all-reduce | flops 2048 | bytes 16384 | tf_op jit(solution)/shard_map/psum | solution.py:26
  1084.0 2.3 fusion.21
  1086.4 2.5 psum.136
  1088.8 2.4 fusion.22
  1091.3 341.8 %all-reduce = (f32[2048,1]{0,1:T(1,128)S(1)}, f32[2048,1]{0,1:T(1,128)S(1)}) all-reduce(f32[2048,1]{0,1:T(1,128)S(1)} %bitcast.49, f32[2048,1]{0,1:T(1,128)S(1)} %bitcast.48), channel_id=1, replica_groups=mesh['proto'=64,'data'=2] {'proto'}, use_global_device_ids=true, to_apply=%region_23.0 | all-reduce | flops 4096 | bytes 32768 | tf_op jit(solution)/shard_map/psum | solution.py:26
  1433.1 4.6 multiply_convert_fusion.1
  1440.5 3.1 fusion.29
  1445.5 2.7 multiply_reduce_fusion.1
  1449.5 63.0 %psum.140 = f32[]{:T(128)} all-reduce(f32[]{:T(128)S(6)} %add.42), channel_id=1, replica_groups=mesh['proto'=64,'data'=2] {'proto','data'}, use_global_device_ids=true, to_apply=%region_30.0 | all-reduce | flops 1 | bytes 8 | tf_op jit(solution)/shard_map/psum | solution.py:36
  1512.5 3.0 copy.11
  1518.0 85.6 %all-reduce.9.cloned.1.call-done = (f32[2048,256]{1,0:T(8,128)}, f32[2048,256]{1,0:T(8,128)}) async-done(((f32[2048,256]{1,0:T(8,128)}, f32[2048,256]{1,0:T(8,128)}), (f32[2048,256]{1,0:T(8,128)}, f32[2048,256]{1,0:T(8,128)})) %all-reduce.9.cloned.1.call-update) | async-done | bytes 4194320 | tf_op jit(solution)/shard_map/psum | solution.py:40
  1603.6 3.2 copy.16
  (53 shorter events, 15.4 us)
Async XLA Ops:
  7.2 365.9 %copy-start = (bf16[2048,256]{1,0:T(8,128)(2,1)S(1)}, bf16[2048,256]{1,0:T(8,128)(2,1)}, u32[]{:S(2)}) copy-start(bf16[2048,256]{1,0:T(8,128)(2,1)} %param.4) | copy-start | bytes 3145732
  7.2 1510.9 %all-reduce.7.cloned.1.call-start = ((), (), s32[]{:S(2)}) async-start(), calls=%async_computation | async-start | bytes 524288 | tf_op jit(solution)/shard_map/psum | solution.py:44
  198.0 175.1 %copy-start.9 = (bf16[256,256]{1,0:T(8,128)(2,1)S(1)}, bf16[256,256]{1,0:T(8,128)(2,1)}, u32[]{:S(2)}) copy-start(bf16[256,256]{1,0:T(8,128)(2,1)} %param.5) | copy-start | bytes 393220
  721.9 4.3 copy-start.1
  726.2 1.4 copy-start.2
  1433.1 5.5 copy-start.7
  1437.6 1.0 copy-start.5
  1437.7 1.6 copy-start.4
  1440.4 163.2 %all-reduce.9.cloned.1.call-start = ((), (), s32[]{:S(2)}) async-start(), calls=%async_computation.1 | async-start | bytes 8388608 | tf_op jit(solution)/shard_map/psum | solution.py:40
  1440.5 3.2 copy-start.6
  1512.5 3.0 copy-start.3
  1603.6 3.2 copy-start.8
  1606.8 1.3 copy-start.10
Sparse Core Ops, SparseCore 0:
  1440.5 16.9 all-reduce.6
  1462.7 140.8 all-reduce.8
where the time goes:
time: 1620 us
  blocking collectives  1470 us (91%)
  waiting for transfers between devices  85.6 us (5%)
  other arithmetic  25.6 us (2%)
  between operations  17.3 us (1%)
    psum x6, blocking collectives, view_terms(): row_sum = lax.psum(jnp.sum(transport, axis=1, keepdims=True), 'proto')  1390 us
    psum x1, waiting for transfers between devices, local_step(): lax.psum(jnp.einsum('nk,kd->nd', logit_grad_one, protos, preferred_elemen...  85.6 us
    psum x1, blocking collectives, local_step(): loss_value = -lax.psum(part_loss, ('proto', 'data')) / (2 * total_rows)  63 us
  transfers between devices with their start and end apart: 2, of which 1 were waited for; matrix products, arithmetic and copies ran while one was open for 1% of the time, Pallas kernels for 0%

commit v1 on v0

v1 whole, which is shorter than its diff:
```python
import functools

import jax
import jax.numpy as jnp
from jax import lax
from jax.experimental import pallas as pl
from jax.experimental.pallas import tpu as pltpu
from jax.sharding import PartitionSpec as P

EPSILON = 0.05
TEMP_TAU = 0.1
ITERS = 3
LINE = 4
AXES = 3
MESH = pl.DeviceIdType.MESH
F32 = jnp.float32
LANES = 128


def _nt(a, b):
    return lax.dot_general(a, b, (((1,), (1,)), ((), ())), preferred_element_type=F32)


def _eye():
    r = lax.broadcasted_iota(jnp.int32, (LANES, LANES), 0)
    c = lax.broadcasted_iota(jnp.int32, (LANES, LANES), 1)
    return r == c


def _parts(n):
    tiles = n // LANES
    cuts = [tiles * j // AXES * LANES for j in range(AXES + 1)]
    return [(cuts[j], cuts[j + 1]) for j in range(AXES)]


def sinkhorn_kernel(total_rows, total_protos, z1, z2, c_ref, r_out, v_out, d_out,
                    e_scr, cacc, vb, ub, stage, csend, crecv, first, later,
                    c_ssem, c_rsem, s_ssem, s_rsem):
    me = lax.axis_index('proto')
    core = lax.axis_index('data')
    rows = z1.shape[0]
    cols = c_ref.shape[0]
    parts = _parts(rows)
    pos = [lax.rem(me, LINE), lax.rem(me // LINE, LINE), me // (LINE * LINE)]
    stride = [1, LINE, LINE * LINE]

    def peer(axis, d):
        return me + (lax.rem(pos[axis] + d, LINE) - pos[axis]) * stride[axis]

    barrier = pltpu.get_barrier_semaphore()
    pl.semaphore_signal(barrier, inc=1, device_id=(me, 1 - core), device_id_type=MESH)
    for axis in range(AXES):
        for d in range(1, LINE):
            pl.semaphore_signal(barrier, inc=1, device_id=(peer(axis, d), core), device_id_type=MESH)

    cb = c_ref[...]
    for view, z in enumerate((z1, z2)):
        cacc[view] = jnp.zeros((cols, LANES), F32)

        def body(i, _, view=view, z=z):
            n0 = pl.multiple_of(i * 256, 256)
            s = _nt(cb, z[pl.ds(n0, 256), :])
            f = jnp.exp(s * (1.0 / TEMP_TAU))
            stage[0, 2 + view:3 + view, pl.ds(n0, 256)] = jnp.sum(f, axis=0, keepdims=True)
            e = f * f
            e_scr[view, :, pl.ds(n0, 256)] = e
            cacc[view] += e[:, :LANES] + e[:, LANES:]
            return 0
        lax.fori_loop(0, rows // 256, body, 0)

    pl.semaphore_wait(barrier, 1 + AXES * (LINE - 1))

    for it in range(ITERS):
        eye = _eye()
        for view in range(2):
            for h in range(2):
                s = jnp.sum(cacc[view, h * LANES:(h + 1) * LANES, :], axis=1, keepdims=True)
                csend[it, 2 * view + h:2 * view + h + 1, :] = jnp.sum(
                    jnp.where(eye, s, 0.0), axis=0, keepdims=True)
        cp = pltpu.make_async_remote_copy(csend.at[it], crecv.at[it], c_ssem.at[it], c_rsem.at[it],
                                          device_id=(me, 1 - core), device_id_type=MESH)
        cp.start()
        cp.wait()
        vrow = 1.0 / (float(total_protos) * (csend[it] + crecv[it]))
        if it == ITERS - 1:
            v_out[...] = vrow
        for view in range(2):
            for h in range(2):
                k = 2 * view + h
                col = jnp.sum(jnp.where(eye, vrow[k:k + 1, :], 0.0), axis=1, keepdims=True)
                vb[view, h * LANES:(h + 1) * LANES, :] = jnp.broadcast_to(col, (LANES, LANES))
        buf = first if it == 0 else later.at[it - 1]
        for view in range(2):
            def rbody(j, _, view=view):
                acc = [jnp.zeros((8, LANES), F32) for _ in range(4)]
                for g in range(cols // 8):
                    w = vb[view, 8 * g:8 * g + 8, :]
                    for t in range(4):
                        l0 = pl.multiple_of(j * 512 + t * LANES, LANES)
                        acc[t] = acc[t] + e_scr[view, 8 * g:8 * g + 8, pl.ds(l0, LANES)] * w
                for t in range(4):
                    l0 = pl.multiple_of(j * 512 + t * LANES, LANES)
                    stage[it, view:view + 1, pl.ds(l0, LANES)] = jnp.sum(acc[t], axis=0, keepdims=True)
                return 0
            lax.fori_loop(0, rows // 512, rbody, 0)
        for j, (l0, l1) in enumerate(parts):
            buf[0, pos[j], :, l0:l1] = stage[it, :buf.shape[2], l0:l1]
        for st in range(AXES):
            copies = []
            for d in (2, 1, 3):
                for j, (l0, l1) in enumerate(parts):
                    ax = (st + j) % AXES
                    idx = ((it * AXES + st) * AXES + j) * (LINE - 1) + d - 1
                    src = buf.at[st, pos[ax], :, l0:l1]
                    cp = pltpu.make_async_remote_copy(src, src, s_ssem.at[idx], s_rsem.at[idx],
                                                      device_id=(peer(ax, d), core), device_id_type=MESH)
                    cp.start()
                    copies.append(cp)
            for j, (l0, l1) in enumerate(parts):
                ax = (st + j) % AXES
                for d in range(1, LINE):
                    idx = ((it * AXES + st) * AXES + j) * (LINE - 1) + d - 1
                    dst = buf.at[st, lax.rem(pos[ax] + LINE - d, LINE), :, l0:l1]
                    pltpu.make_async_remote_copy(dst, dst, s_ssem.at[idx], s_rsem.at[idx],
                                                 device_id=(peer(ax, d), core), device_id_type=MESH).wait_recv()
                tot = (buf[st, 0, :, l0:l1] + buf[st, 1, :, l0:l1]) + (buf[st, 2, :, l0:l1] + buf[st, 3, :, l0:l1])
                if st < AXES - 1:
                    buf[st + 1, pos[(st + 1 + j) % AXES], :, l0:l1] = tot
                else:
                    if it == 0:
                        d_out[:, l0:l1] = tot[2:4]
                        tot = tot[0:2]
                    if it == ITERS - 1:
                        r_out[:, l0:l1] = tot
                    else:
                        u = 1.0 / (float(total_rows) * tot)
                        for view in range(2):
                            ub[view, :, l0:l1] = jnp.broadcast_to(u[view:view + 1], (8, l1 - l0))
            for cp in copies:
                cp.wait_send()
        if it < ITERS - 1:
            for view in range(2):
                def cbody(g, _, view=view):
                    for gg in range(4):
                        k0 = pl.multiple_of(g * 32 + gg * 8, 8)
                        acc = [None] * 4
                        for t in range(rows // LANES):
                            x = e_scr[view, pl.ds(k0, 8), t * LANES:(t + 1) * LANES] * ub[view, :, t * LANES:(t + 1) * LANES]
                            acc[t % 4] = x if acc[t % 4] is None else acc[t % 4] + x
                        cacc[view, pl.ds(k0, 8), :] = (acc[0] + acc[1]) + (acc[2] + acc[3])
                    return 0
                lax.fori_loop(0, cols // 32, cbody, 0)


def solution(mesh):
    proto_size = mesh.shape['proto']
    data_size = mesh.shape['data']

    def local_step(emb_one, emb_two, protos):
        rows, cols = emb_one.shape[0], protos.shape[0]
        total_rows = rows * data_size
        total_protos = cols * proto_size
        vm = pl.BlockSpec(memory_space=pltpu.VMEM)
        nsem = ITERS * AXES * AXES * (LINE - 1)
        r3, v3, den = pl.pallas_call(
            functools.partial(sinkhorn_kernel, total_rows, total_protos),
            out_shape=(jax.ShapeDtypeStruct((2, rows), F32),
                       jax.ShapeDtypeStruct((4, LANES), F32),
                       jax.ShapeDtypeStruct((2, rows), F32)),
            in_specs=[vm] * 3,
            out_specs=(vm,) * 3,
            scratch_shapes=[
                pltpu.VMEM((2, cols, rows), F32),
                pltpu.VMEM((2, cols, LANES), F32),
                pltpu.VMEM((2, cols, LANES), F32),
                pltpu.VMEM((2, 8, rows), F32),
                pltpu.VMEM((ITERS, 4, rows), F32),
                pltpu.VMEM((ITERS, 4, LANES), F32),
                pltpu.VMEM((ITERS, 4, LANES), F32),
                pltpu.VMEM((AXES, LINE, 4, rows), F32),
                pltpu.VMEM((ITERS - 1, AXES, LINE, 2, rows), F32),
                pltpu.SemaphoreType.DMA((ITERS,)),
                pltpu.SemaphoreType.DMA((ITERS,)),
                pltpu.SemaphoreType.DMA((nsem,)),
                pltpu.SemaphoreType.DMA((nsem,)),
            ],
            compiler_params=pltpu.CompilerParams(collective_id=0, has_side_effects=True),
        )(emb_one, emb_two, protos)
        vrow = v3.reshape(2, cols)

        def view_terms(emb, i):
            scores = jnp.einsum('nd,kd->nk', emb, protos, preferred_element_type=F32)
            logits = scores / TEMP_TAU
            codes = jnp.exp(scores / EPSILON) * vrow[i][None, :] / r3[i][:, None]
            return codes, logits - jnp.log(den[i])[:, None]

        codes_one, logp_one = view_terms(emb_one, 0)
        codes_two, logp_two = view_terms(emb_two, 1)
        part_loss = jnp.sum(codes_two * logp_one) + jnp.sum(codes_one * logp_two)
        loss_value = -lax.psum(part_loss, ('proto', 'data')) / (2 * total_rows)
        grad_scale = 2 * total_rows * TEMP_TAU
        hone = ((jnp.exp(logp_one) - codes_two) / grad_scale).astype(jnp.bfloat16)
        htwo = ((jnp.exp(logp_two) - codes_one) / grad_scale).astype(jnp.bfloat16)
        grad_one = lax.psum(jnp.einsum('nk,kd->nd', hone, protos, preferred_element_type=F32), 'proto')
        grad_two = lax.psum(jnp.einsum('nk,kd->nd', htwo, protos, preferred_element_type=F32), 'proto')
        proto_part = (jnp.einsum('nk,nd->kd', hone, emb_one, preferred_element_type=F32)
                      + jnp.einsum('nk,nd->kd', htwo, emb_two, preferred_element_type=F32))
        grad_protos = lax.psum(proto_part, 'data')
        return codes_one, codes_two, loss_value, grad_one, grad_two, grad_protos

    return jax.shard_map(
        local_step, mesh=mesh,
        in_specs=(P('data', None), P('data', None), P('proto', None)),
        out_specs=(P('data', 'proto'), P('data', 'proto'), P(), P('data', None), P('data', None), P('proto', None)),
        check_vma=False)
```

time: 1620 us -> 250 us (0.15)
  blocking collectives: 1470 us -> 62.8 us
  Pallas kernels: 0 us -> 50.2 us
  other arithmetic: 25.6 us -> 4.16 us
    psum x11 -> x0, blocking collectives: 1400 us -> none  [the longest x6 1390 us: view_terms(): row_sum = lax.psum(jnp.sum(transport, axis=1, keepdims=True), 'proto')]
    pallas_call x0 -> x1, Pallas kernels: none -> 50.2 us  [local_step(): pl.pallas_call(functools.partial(sinkhorn_kernel, total_rows, total_proto...]
  transfers between devices with their start and end apart: 2 -> 2, of which waited for: 1 -> 1; matrix products, arithmetic and copies ran while one was open for 1% -> 4% of each run, Pallas kernels for 0% -> 0%
where the time goes in v1:
time: 250 us; the launch traced here: 249 us
  waiting for transfers between devices  94 us (38%)
  blocking collectives  62.8 us (25%)
  Pallas kernels  50.2 us (20%)
  between operations  17.1 us (7%)
  matrix products  12.7 us (5%)
  local copies, waits for them, and re-layouts  7.95 us (3%)
  other arithmetic  4.16 us (2%)
    psum x1, waiting for transfers between devices, local_step(): lax.psum(jnp.einsum('nk,kd->nd', hone, protos, preferred_element_type=F32...  93.9 us
    psum x1, blocking collectives, local_step(): loss_value = -lax.psum(part_loss, ('proto', 'data')) / (2 * total_rows)  62.8 us
    pallas_call x1, Pallas kernels, local_step(): pl.pallas_call(functools.partial(sinkhorn_kernel, total_rows, total_proto...  50.2 us
    unnamed x19, local copies, waits for them, and re-layouts  6.36 us
    dot_general x2, matrix products, view_terms(): scores = jnp.einsum('nd,kd->nk', emb, protos, preferred_element_type=F32)  6.36 us
  transfers between devices with their start and end apart: 2, of which 1 were waited for; matrix products, arithmetic and copies ran while one was open for 4% of the time, Pallas kernels for 0%

profile of v1, /device:TPU:0, one launch (start us, length us, event | category | flops | bytes accessed | tf_op | source)
XLA Modules:
  0.0 249.1 jit_solution(11716446171638851617)
XLA Ops:
  7.2 0.0 all-reduce.4.cloned.1.call-start
  7.2 1.7 fusion.1
  8.9 50.2 %shard_map.82 = (f32[2,2048]{1,0:T(2,128)}, f32[4,128]{1,0:T(4,128)}, f32[2,2048]{1,0:T(2,128)}) custom-call(bf16[2048,256]{1,0:T(8,128)(2,1)} %z1.1, bf16[2048,256]{1,0:T(8,128)(2,1)} %z2.1, bf16[256,256]{1,0:T(8,128)(2,1)} %c_ref.1), custom_call_target="tpu_custom_call" | custom-call | tf_op jit(solution)/shard_map/pallas_call | solution.py:165
  59.2 0.8 slice_bitcast_fusion
  59.9 0.8 slice_log_fusion.1
  60.8 4.6 %multiply_convert_fusion.1 = (bf16[2048,256]{1,0:T(8,128)(2,1)S(1)}, f32[2048,256]{1,0:T(8,128)}, bf16[2048,256]{1,0:T(8,128)(2,1)S(1)}, f32[2048,256]{1,0:T(8,128)}, f32[2048,256]{1,0:T(8,128)}) fusion(f32[2048]{0:T(1024)S(1)} %bitcast.20, f32[2048]{0:T(1024)S(1)} %bitcast.25, f32[256]{0:T(256)S(1)} %get-tuple-element.24, f32[2048,256]{1,0:T(8,128)S(1)} %fusion.1, ...), kind=kOutput, calls=%fused_computation.1 | convolution fusion | flops 276824064 | bytes 11700224 | tf_op jit(solution)/shard_map/nd,kd->nk/dot_general | solution.py:192
  65.4 0.5 fusion.4
  65.9 0.5 copy-done.1
  66.4 0.6 copy-done
  67.0 1.2 convolution_add_fusion
  68.2 0.0 all-reduce.4.cloned.1.call-update
  68.2 0.0 all-reduce.6.cloned.1.call-start
  68.3 3.0 %fusion.3 = f32[2048,256]{1,0:T(8,128)} fusion(bf16[2048,256]{1,0:T(8,128)(2,1)} %copy-done.1, bf16[256,256]{1,0:T(8,128)(2,1)S(1)} %copy-done.3), kind=kOutput, calls=%fused_computation.16 | convolution fusion | flops 268435456 | bytes 3276800 | tf_op jit(solution)/shard_map/nk,kd->nd/dot_general | solution.py:205
  71.2 1.8 fusion.2
  73.0 0.0 all-reduce.6.cloned.1.call-update
  73.0 0.0 copy-start.4
  73.0 2.9 %multiply_reduce_fusion = f32[]{:T(128)} fusion(f32[2048,256]{1,0:T(8,128)} %get-tuple-element.29, f32[2048,256]{1,0:T(8,128)S(1)} %fusion.1, f32[2048]{0:T(1024)S(1)} %bitcast.23), kind=kLoop, calls=%fused_computation.2 | loop fusion | flops 2097151 | bytes 4202500 | tf_op jit(solution)/shard_map/reduce_sum | solution.py:199
  76.0 1.2 multiply_reduce_fusion.1
  78.4 62.8 %psum.28 = f32[]{:T(128)} all-reduce(f32[]{:T(128)S(6)} %add.14), channel_id=1, replica_groups=mesh['proto'=64,'data'=2] {'proto','data'}, use_global_device_ids=true, to_apply=%region_2.0 | all-reduce | flops 1 | bytes 8 | tf_op jit(solution)/shard_map/psum | solution.py:200
  141.9 0.0 all-reduce.4.cloned.1.call-done
  141.9 93.9 %all-reduce.6.cloned.1.call-done = (f32[2048,256]{1,0:T(8,128)}, f32[2048,256]{1,0:T(8,128)}) async-done(((f32[2048,256]{1,0:T(8,128)}, f32[2048,256]{1,0:T(8,128)}), (f32[2048,256]{1,0:T(8,128)}, f32[2048,256]{1,0:T(8,128)})) %all-reduce.6.cloned.1.call-update) | async-done | bytes 4194320 | tf_op jit(solution)/shard_map/psum | solution.py:204
  235.9 3.2 %copy.12 = f32[2048,256]{1,0:T(8,128)} copy(f32[2048,256]{1,0:T(8,128)} %get-tuple-element.32) | data formatting | bytes 4194304
  239.1 1.3 copy.13
  240.4 0.7 copy.14
  (13 shorter events, 0.0 us)
Async XLA Ops:
  7.2 53.6 %copy-start.3 = (bf16[256,256]{1,0:T(8,128)(2,1)S(1)}, bf16[256,256]{1,0:T(8,128)(2,1)}, u32[]{:S(2)}) copy-start(bf16[256,256]{1,0:T(8,128)(2,1)} %c_ref.1) | copy-start | bytes 393220
  7.2 134.8 %all-reduce.4.cloned.1.call-start = ((), (), s32[]{:S(2)}) async-start(), calls=%async_computation | async-start | bytes 524288 | tf_op jit(solution)/shard_map/psum | solution.py:208
  60.8 4.7 %copy-start.2 = (bf16[2048,256]{1,0:T(8,128)(2,1)S(1)}, bf16[2048,256]{1,0:T(8,128)(2,1)}, u32[]{:S(2)}) copy-start(bf16[2048,256]{1,0:T(8,128)(2,1)} %z1.1) | copy-start | bytes 3145732
  65.4 1.0 copy-start.1
  65.4 1.6 copy-start
  68.2 167.7 %all-reduce.6.cloned.1.call-start = ((), (), s32[]{:S(2)}) async-start(), calls=%async_computation.1 | async-start | bytes 8388608 | tf_op jit(solution)/shard_map/psum | solution.py:204
  73.0 3.0 %copy-start.4 = (f32[2048,256]{1,0:T(8,128)S(1)}, f32[2048,256]{1,0:T(8,128)}, u32[]{:S(2)}) copy-start(f32[2048,256]{1,0:T(8,128)} %get-tuple-element.30) | copy-start | bytes 6291460
  73.0 3.0 %copy-start.5 = (f32[2048,256]{1,0:T(8,128)S(1)}, f32[2048,256]{1,0:T(8,128)}, u32[]{:S(2)}) copy-start(f32[2048,256]{1,0:T(8,128)} %get-tuple-element.26) | copy-start | bytes 6291460
  235.9 3.2 %copy-start.6 = (f32[2048,256]{1,0:T(8,128)S(1)}, f32[2048,256]{1,0:T(8,128)}, u32[]{:S(2)}) copy-start(f32[2048,256]{1,0:T(8,128)} %get-tuple-element.33) | copy-start | bytes 6291460
  239.1 1.3 copy-start.7
Sparse Core Ops, SparseCore 0:
  68.3 20.7 all-reduce.3
  94.9 140.9 all-reduce.5

commit v2 on v1

v2 whole, which is shorter than its diff:
```python
import functools
import re

import jax
import jax.numpy as jnp
from jax import lax
from jax.experimental import pallas as pl
from jax.experimental.pallas import tpu as pltpu
from jax.sharding import PartitionSpec as P

EPSILON = 0.05
TEMP_TAU = 0.1
ITERS = 3
LINE = 4
AXES = 3
MESH = pl.DeviceIdType.MESH
F32 = jnp.float32
BF16 = jnp.bfloat16
LANES = 128
SUM_PARTS = ((0, 640), (640, 1280), (1280, 2048))
C_PARTS = ((0, 48), (48, 96), (96, 128))
G_PARTS = ((0, 24), (24, 48), (48, 64))
AG_SEMS = 27
SLOTS = (
    'S',
    'sA10A11A12A13',
    'a10B10a11B11a12B12a13B13A20T00T10T30',
    'A21b10b11b12b13T20a20B20T01T03',
    'A23a21B21T11T13b20T02',
    'A22a23B23T31T33b21T12',
    'a22B22T21T23b23T32',
    'b22T22UR0',
    'R1',
)


def _nt(a, b):
    return lax.dot_general(a, b, (((1,), (1,)), ((), ())), preferred_element_type=F32)


def _nn(a, b):
    return jnp.dot(a, b, preferred_element_type=F32)


def _col_to_row(s):
    r = lax.broadcasted_iota(jnp.int32, (LANES, LANES), 0)
    c = lax.broadcasted_iota(jnp.int32, (LANES, LANES), 1)
    return jnp.sum(jnp.where(r == c, s, 0.0), axis=0, keepdims=True)


def _row_to_col(row, n=LANES, shift=0):
    r = lax.broadcasted_iota(jnp.int32, (n, LANES), 0)
    c = lax.broadcasted_iota(jnp.int32, (n, LANES), 1)
    return jnp.sum(jnp.where(c == r + shift, row, 0.0), axis=1, keepdims=True)


class _Gather:
    def __init__(self, env, buf, row0, parts, ssem, rsem):
        self.env, self.buf, self.row0, self.parts = env, buf, row0, parts
        self.ssem, self.rsem = ssem, rsem

    def at(self, j, i0, i1, i2, row0=None):
        ids = [None] * AXES
        for axis, i in zip((j, j + 1, j + 2), (i0, i1, i2)):
            ids[axis % AXES] = slice(None) if i is None else i
        r0, r1 = self.parts[j]
        base = self.row0 if row0 is None else row0
        rows = pl.ds(base + r0, r1 - r0) if isinstance(base, int) else pl.ds(pl.multiple_of(base + r0, 16), r1 - r0)
        return self.buf.at[ids[2], ids[1], ids[0], rows, :]

    def p(self, j, level, d):
        return self.env.p((j + level) % AXES, d)

    def send(self, j, k, ref, level, d):
        env, i = self.env, j * AG_SEMS + k
        cp = pltpu.make_async_remote_copy(ref, ref, self.ssem.at[i], self.rsem.at[i],
                                          device_id=env.peer((j + level) % AXES, d), device_id_type=MESH)
        cp.start()
        env.pending.append(cp)

    def recv(self, j, k, ref):
        i = j * AG_SEMS + k
        pltpu.make_async_remote_copy(ref, ref, self.ssem.at[i], self.rsem.at[i],
                                     device_id=self.env.me2, device_id_type=MESH).wait_recv()

    def s1_send(self):
        for d in (2, 1, 3):
            for j in range(AXES):
                self.send(j, d - 1, self.at(j, self.p(j, 0, 0), self.p(j, 1, 0), self.p(j, 2, 0)), 0, d)

    def s1_recv(self):
        for d in (1, 3, 2):
            for j in range(AXES):
                self.recv(j, d - 1, self.at(j, self.p(j, 0, LINE - d), self.p(j, 1, 0), self.p(j, 2, 0)))

    def chunk(self, j, level, k, m):
        if level == 1:
            return self.at(j, self.p(j, 0, k), self.p(j, 1, m), self.p(j, 2, 0))
        return self.at(j, None, self.p(j, 1, k), self.p(j, 2, m))

    def a_send(self, level, k):
        base = 3 if level == 1 else 15
        for j in range(AXES):
            ref = self.chunk(j, level, k, 0)
            self.send(j, base + k, ref, level, 1)
            self.send(j, base + 4 + k, ref, level, 3)

    def a_recv(self, level, k):
        base = 3 if level == 1 else 15
        for j in range(AXES):
            self.recv(j, base + k, self.chunk(j, level, k, 3))
            self.recv(j, base + 4 + k, self.chunk(j, level, k, 1))

    def b_send(self, level, k):
        base = 11 if level == 1 else 23
        for j in range(AXES):
            if k < 2:
                self.send(j, base + k, self.chunk(j, level, k, 3), level, 1)
            else:
                self.send(j, base + k, self.chunk(j, level, k, 1), level, 3)

    def b_recv(self, level, k):
        base = 11 if level == 1 else 23
        for j in range(AXES):
            self.recv(j, base + k, self.chunk(j, level, k, 2))


class _Env:
    def __init__(self):
        self.me = lax.axis_index('proto')
        self.core = lax.axis_index('data')
        me = self.me
        self.pos = [lax.rem(me, LINE), lax.rem(lax.div(me, LINE), LINE), lax.div(me, LINE * LINE)]
        self.stride = [1, LINE, LINE * LINE]
        self.pending = []
        self.me2 = (me, 1 - self.core)

    def p(self, axis, d):
        return self.pos[axis] if d == 0 else lax.rem(self.pos[axis] + d, LINE)

    def peer(self, axis, d):
        return (self.me + (self.p(axis, d) - self.pos[axis]) * self.stride[axis], self.core)


def step_kernel(total_rows, total_protos, z1, z2, c_ref,
                code1, code2, loss_out, g1, g2, gp_out,
                f_scr, e_scr, cfull, lrow, frow, gfull, vall, zr, dvec,
                cacc, vb, ub, stage, csend, crecv, first, later, lossb, losst, dacc, drecv,
                lsem, c_ssem, c_rsem, s_ssem, s_rsem, a_ssem, a_rsem, t_ssem, t_rsem,
                v_ssem, v_rsem, g_ssem, g_rsem, l_ssem, l_rsem):
    env = _Env()
    me, core, pos = env.me, env.core, env.pos
    partner = env.me2
    rows, cols = z1.shape[0], c_ref.shape[0]
    half = cols // 2
    mine = zr.shape[0] // 2
    blocks = LINE ** AXES
    fscale = 1.0 / (2 * total_rows * TEMP_TAU)
    zs = (z1, z2)

    barrier = pltpu.get_barrier_semaphore()
    pl.semaphore_signal(barrier, inc=1, device_id=partner, device_id_type=MESH)
    for axis in range(AXES):
        for d in range(1, LINE):
            pl.semaphore_signal(barrier, inc=1, device_id=env.peer(axis, d), device_id_type=MESH)

    h0 = pl.multiple_of(core * half, half)
    own = pltpu.make_async_copy(c_ref.at[pl.ds(h0, half), :],
                                cfull.at[pos[2], pos[1], pos[0], pl.ds(h0, half), :], lsem.at[0])
    own.start()
    gc = _Gather(env, cfull, core * half, C_PARTS, a_ssem, a_rsem)
    gg = _Gather(env, gfull, 0, G_PARTS, g_ssem, g_rsem)

    def remote(src, dst, ss, rs, dev):
        cp = pltpu.make_async_remote_copy(src, dst, ss, rs, device_id=dev, device_id_type=MESH)
        cp.start()
        env.pending.append(cp)
        return cp

    def twin_send(k, m):
        for j in range(AXES):
            i = j * 16 + k * 4 + m
            ref = gc.chunk(j, 2, k, m)
            remote(ref, ref, t_ssem.at[i], t_rsem.at[i], partner)

    def twin_recv(k, m):
        for j in range(AXES):
            i = j * 16 + k * 4 + m
            ref = gc.at(j, None, gc.p(j, 1, k), gc.p(j, 2, m), row0=(1 - core) * half)
            pltpu.make_async_remote_copy(ref, ref, t_ssem.at[i], t_rsem.at[i],
                                         device_id=partner, device_id_type=MESH).wait_recv()

    cb = c_ref[...]
    for view, z in enumerate(zs):
        cacc[view] = jnp.zeros((cols, LANES), F32)

        def body(i, _, view=view, z=z):
            n0 = pl.multiple_of(i * 256, 256)
            s = _nt(cb, z[pl.ds(n0, 256), :])
            f = jnp.exp(s * (1.0 / TEMP_TAU))
            stage[0, 2 + view:3 + view, pl.ds(n0, 256)] = jnp.sum(f, axis=0, keepdims=True)
            e = f * f
            f_scr[view, :, pl.ds(n0, 256)] = f
            e_scr[view, :, pl.ds(n0, 256)] = e
            cacc[view] += e[:, :LANES] + e[:, LANES:]
            return 0
        lax.fori_loop(0, rows // 256, body, 0)
        zr[view * mine:(view + 1) * mine, :] = z[pl.ds(pl.multiple_of(me * mine, mine), mine), :]

    own.wait()
    pl.semaphore_wait(barrier, 1 + AXES * (LINE - 1))

    def gather_rows(lo, hi):
        def sbody(i, _):
            q = lax.div(i, 2)
            z_, y_, x_ = lax.div(q, 16), lax.rem(lax.div(q, 4), 4), lax.rem(q, 4)
            k0 = pl.multiple_of(lax.rem(i, 2) * half, half)
            l = _nt(zr[...], cfull[z_, y_, x_, pl.ds(k0, half), :]) * (1.0 / TEMP_TAU)
            lrow[q, :, pl.ds(k0, half)] = l
            frow[q, :, pl.ds(k0, half)] = jnp.exp(l)
            return 0
        lax.fori_loop(lo, hi, sbody, 0, unroll=4)

    def run(g, ops):
        for op in re.findall('[a-zA-Z][0-9]*', ops):
            args = [int(c) for c in op[1:]]
            {'S': g.s1_send, 's': g.s1_recv, 'A': g.a_send, 'a': g.a_recv, 'B': g.b_send, 'b': g.b_recv,
             'T': twin_send, 'U': twin_all, 'R': gather_half}[op[0]](*args)

    def twin_all():
        for k in range(LINE):
            for m in range(LINE):
                twin_recv(k, m)

    def gather_half(i):
        gather_rows(i * blocks, (i + 1) * blocks)

    for it in range(ITERS):
        for view in range(2):
            for h in range(2):
                s = jnp.sum(cacc[view, h * LANES:(h + 1) * LANES, :], axis=1, keepdims=True)
                k = 2 * view + h
                csend[it, k:k + 1, :] = _col_to_row(s)
        cp = remote(csend.at[it], crecv.at[it], c_ssem.at[it], c_rsem.at[it], partner)
        cp.wait_recv()
        vrow = 1.0 / (float(total_protos) * (csend[it] + crecv[it]))
        last = it == ITERS - 1
        if last:
            vall[pos[2], pos[1], pos[0]] = vrow
        for view in range(2):
            for h in range(2):
                k = 2 * view + h
                vb[view, h * LANES:(h + 1) * LANES, :] = jnp.broadcast_to(_row_to_col(vrow[k:k + 1, :]), (LANES, LANES))
        buf = first if it == 0 else later.at[it - 1]

        def vsend(st):
            ref = vall.at[(pos[2], pos[1], pos[0])[:AXES - st]]
            for d in (2, 1, 3):
                i = st * 3 + d - 1
                remote(ref, ref, v_ssem.at[i], v_rsem.at[i], env.peer(st, d))

        def vrecv(st):
            for d in (1, 3, 2):
                i = st * 3 + d - 1
                ids = [pos[2], pos[1], pos[0]][:AXES - st]
                ids[-1] = env.p(st, LINE - d)
                ref = vall.at[tuple(ids)]
                pltpu.make_async_remote_copy(ref, ref, v_ssem.at[i], v_rsem.at[i],
                                             device_id=partner, device_id_type=MESH).wait_recv()

        if last:
            vsend(0)
        for view in range(2):
            def rbody(j, _, view=view):
                acc = [jnp.zeros((8, LANES), F32) for _ in range(4)]
                for g in range(cols // 8):
                    w = vb[view, 8 * g:8 * g + 8, :]
                    for t in range(4):
                        l0 = pl.multiple_of(j * 512 + t * LANES, LANES)
                        acc[t] = acc[t] + e_scr[view, 8 * g:8 * g + 8, pl.ds(l0, LANES)] * w
                for t in range(4):
                    l0 = pl.multiple_of(j * 512 + t * LANES, LANES)
                    stage[it, view:view + 1, pl.ds(l0, LANES)] = jnp.sum(acc[t], axis=0, keepdims=True)
                return 0
            lax.fori_loop(0, rows // 512, rbody, 0)
        for j, (l0, l1) in enumerate(SUM_PARTS):
            buf[0, pos[j], :, l0:l1] = stage[it, :buf.shape[2], l0:l1]
        for st in range(AXES):
            for d in (2, 1, 3):
                for j, (l0, l1) in enumerate(SUM_PARTS):
                    ax = (st + j) % AXES
                    i = ((it * AXES + st) * AXES + j) * (LINE - 1) + d - 1
                    src = buf.at[st, pos[ax], :, l0:l1]
                    remote(src, src, s_ssem.at[i], s_rsem.at[i], env.peer(ax, d))
            run(gc, SLOTS[it * AXES + st])
            if last:
                vrecv(st)
                if st < AXES - 1:
                    vsend(st + 1)
            for j, (l0, l1) in enumerate(SUM_PARTS):
                ax = (st + j) % AXES
                for d in range(1, LINE):
                    i = ((it * AXES + st) * AXES + j) * (LINE - 1) + d - 1
                    dst = buf.at[st, env.p(ax, LINE - d), :, l0:l1]
                    pltpu.make_async_remote_copy(dst, dst, s_ssem.at[i], s_rsem.at[i],
                                                 device_id=partner, device_id_type=MESH).wait_recv()
                tot = (buf[st, 0, :, l0:l1] + buf[st, 1, :, l0:l1]) + (buf[st, 2, :, l0:l1] + buf[st, 3, :, l0:l1])
                if st < AXES - 1:
                    buf[st + 1, pos[(st + 1 + j) % AXES], :, l0:l1] = tot
                else:
                    if it == 0:
                        dvec[2:4, l0:l1] = tot[2:4]
                        tot = tot[0:2]
                    if last:
                        dvec[0:2, l0:l1] = tot
                    else:
                        u = 1.0 / (float(total_rows) * tot)
                        for view in range(2):
                            ub[view, :, l0:l1] = jnp.broadcast_to(u[view:view + 1], (8, l1 - l0))
        if not last:
            for view in range(2):
                def cbody(g, _, view=view):
                    for gi in range(4):
                        k0 = pl.multiple_of(g * 32 + gi * 8, 8)
                        acc = [None] * 4
                        for t in range(rows // LANES):
                            ls = slice(t * LANES, (t + 1) * LANES)
                            x = e_scr[view, pl.ds(k0, 8), ls] * ub[view, :, ls]
                            acc[t % 4] = x if acc[t % 4] is None else acc[t % 4] + x
                        cacc[view, pl.ds(k0, 8), :] = (acc[0] + acc[1]) + (acc[2] + acc[3])
                    return 0
                lax.fori_loop(0, cols // 32, cbody, 0)

    tile = pl.multiple_of(lax.div(me * mine, LANES) * LANES, LANES)
    shift = lax.rem(me * mine, LANES)
    dv = dvec[:, pl.ds(tile, LANES)]
    col = [_row_to_col(dv[i:i + 1, :], mine, shift) for i in range(4)]
    rc = jnp.broadcast_to(1.0 / jnp.concatenate(col[0:2], axis=0), (2 * mine, LANES))
    den = jnp.concatenate(col[2:4], axis=0)
    dc = jnp.broadcast_to(1.0 / den, (2 * mine, LANES))
    ld = jnp.broadcast_to(jnp.log(den), (2 * mine, LANES))

    def block(q):
        z_, y_, x_ = lax.div(q, 16), lax.rem(lax.div(q, 4), 4), lax.rem(q, 4)
        return z_, y_, x_

    def code_rows(q, h):
        z_, y_, x_ = block(q)
        f = frow[q, :, h * LANES:(h + 1) * LANES]
        v0 = jnp.broadcast_to(vall[z_, y_, x_, h:h + 1, :], (mine, LANES))
        v1 = jnp.broadcast_to(vall[z_, y_, x_, 2 + h:3 + h, :], (mine, LANES))
        return f, f * f * (rc * jnp.concatenate([v0, v1], axis=0))

    def dzbody(q, acc):
        z_, y_, x_ = block(q)
        hs = []
        for h in range(2):
            f, code = code_rows(q, h)
            other = jnp.concatenate([code[mine:], code[:mine]], axis=0)
            hs.append(((f * dc - other) * fscale).astype(BF16))
        return acc + _nn(jnp.concatenate(hs, axis=1), cfull[z_, y_, x_])

    gfull[pos[2], pos[1], pos[0]] = lax.fori_loop(0, blocks, dzbody, jnp.zeros((2 * mine, cols), F32), unroll=4)

    dacc[...] = jnp.zeros((cols, cols), F32)

    def columns(i):
        def body(i, _):
            n0 = pl.multiple_of(i * cols, cols)
            inv = 1.0 / dvec[:, pl.ds(n0, cols)]
            code, prob = [], []
            for view in range(2):
                w = jnp.concatenate([vb[view], vb[view]], axis=1)
                code.append(e_scr[view, :, pl.ds(n0, 256)] * w * inv[view:view + 1, :])
                prob.append(f_scr[view, :, pl.ds(n0, 256)] * inv[2 + view:3 + view, :])
            for view, out in enumerate((code1, code2)):
                h = ((prob[view] - code[1 - view]) * fscale).astype(BF16)
                dacc[...] += _nn(h, zs[view][pl.ds(n0, 256), :])
                out[pl.ds(n0, 256), :] = code[view].T
            return 0
        lax.fori_loop(i * 2, i * 2 + 2, body, 0)

    gg.s1_send()

    def lbody(q, acc):
        for h in range(2):
            f, code = code_rows(q, h)
            lp = lrow[q, :, h * LANES:(h + 1) * LANES] - ld
            other = jnp.concatenate([code[mine:], code[:mine]], axis=0)
            acc = acc + other * lp
        return acc
    part = lax.fori_loop(0, blocks, lbody, jnp.zeros((2 * mine, LANES), F32), unroll=2)
    lossb[0, pos[0]] = jnp.sum(part.reshape(2 * mine // 8, 8, LANES), axis=0)

    def loss_send(st):
        ref = lossb.at[st, pos[st]]
        for d in (2, 1, 3):
            i = st * 3 + d - 1
            remote(ref, ref, l_ssem.at[i], l_rsem.at[i], env.peer(st, d))

    def loss_recv(st):
        for d in (1, 3, 2):
            i = st * 3 + d - 1
            ref = lossb.at[st, env.p(st, LINE - d)]
            pltpu.make_async_remote_copy(ref, ref, l_ssem.at[i], l_rsem.at[i],
                                         device_id=partner, device_id_type=MESH).wait_recv()
        return (lossb[st, 0] + lossb[st, 1]) + (lossb[st, 2] + lossb[st, 3])

    run(gg, 'sA10A11A12A13')
    loss_send(0)
    run(gg, 'A20')
    columns(0)
    run(gg, 'a10B10a11B11a12B12a13B13A21A23')
    lossb[1, pos[1]] = loss_recv(0)
    loss_send(1)
    columns(1)
    run(gg, 'b10b11b12b13A22a20B20')
    lossb[2, pos[2]] = loss_recv(1)
    loss_send(2)
    columns(2)
    run(gg, 'a21B21a23B23')
    columns(3)
    losst[0] = loss_recv(2)
    lcp = remote(losst.at[0], losst.at[1], l_ssem.at[9], l_rsem.at[9], partner)
    dcp = remote(dacc, drecv, l_ssem.at[10], l_rsem.at[10], partner)
    run(gg, 'a22B22')
    lcp.wait_recv()
    loss_out[...] = jnp.sum(losst[0] + losst[1], keepdims=True) * (-1.0 / (2 * total_rows))
    dcp.wait_recv()
    gp_out[...] = dacc[...] + drecv[...]
    run(gg, 'b20b21b23b22')

    def obody(q, _):
        z_, y_, x_ = block(q)
        n0 = pl.multiple_of(q * mine, mine)
        g1[pl.ds(n0, mine), :] = gfull[z_, y_, x_, :mine, :]
        g2[pl.ds(n0, mine), :] = gfull[z_, y_, x_, mine:, :]
        return 0
    lax.fori_loop(0, blocks, obody, 0)
    for cp in env.pending:
        cp.wait_send()


def solution(mesh):
    proto_size = mesh.shape['proto']
    data_size = mesh.shape['data']

    def local_step(emb_one, emb_two, protos):
        rows, dim = emb_one.shape
        cols = protos.shape[0]
        total_rows = rows * data_size
        total_protos = cols * proto_size
        mine = rows // proto_size
        vm = pl.BlockSpec(memory_space=pltpu.VMEM)
        nsem = ITERS * AXES * AXES * (LINE - 1)
        dma = lambda n: pltpu.SemaphoreType.DMA((n,))
        grid3 = (LINE,) * AXES
        sds = jax.ShapeDtypeStruct
        code1, code2, loss, g1, g2, gp = pl.pallas_call(
            functools.partial(step_kernel, total_rows, total_protos),
            out_shape=(sds((rows, cols), F32), sds((rows, cols), F32), sds((1, 1), F32),
                       sds((rows, dim), F32), sds((rows, dim), F32), sds((cols, dim), F32)),
            in_specs=[vm] * 3,
            out_specs=(vm,) * 6,
            scratch_shapes=[
                pltpu.VMEM((2, cols, rows), F32),
                pltpu.VMEM((2, cols, rows), F32),
                pltpu.VMEM(grid3 + (cols, dim), BF16),
                pltpu.VMEM((proto_size, 2 * mine, cols), F32),
                pltpu.VMEM((proto_size, 2 * mine, cols), F32),
                pltpu.VMEM(grid3 + (2 * mine, dim), F32),
                pltpu.VMEM(grid3 + (4, LANES), F32),
                pltpu.VMEM((2 * mine, dim), BF16),
                pltpu.VMEM((4, rows), F32),
                pltpu.VMEM((2, cols, LANES), F32),
                pltpu.VMEM((2, cols, LANES), F32),
                pltpu.VMEM((2, 8, rows), F32),
                pltpu.VMEM((ITERS, 4, rows), F32),
                pltpu.VMEM((ITERS, 4, LANES), F32),
                pltpu.VMEM((ITERS, 4, LANES), F32),
                pltpu.VMEM((AXES, LINE, 4, rows), F32),
                pltpu.VMEM((ITERS - 1, AXES, LINE, 2, rows), F32),
                pltpu.VMEM((AXES, LINE, 8, LANES), F32),
                pltpu.VMEM((2, 8, LANES), F32),
                pltpu.VMEM((cols, dim), F32),
                pltpu.VMEM((cols, dim), F32),
                dma(1), dma(ITERS), dma(ITERS), dma(nsem), dma(nsem),
                dma(AXES * AG_SEMS), dma(AXES * AG_SEMS), dma(48), dma(48),
                dma(9), dma(9), dma(AXES * AG_SEMS), dma(AXES * AG_SEMS), dma(11), dma(11),
            ],
            compiler_params=pltpu.CompilerParams(collective_id=0, has_side_effects=True),
        )(emb_one, emb_two, protos)
        return code1, code2, loss[0, 0], g1, g2, gp

    return jax.shard_map(
        local_step, mesh=mesh,
        in_specs=(P('data', None), P('data', None), P('proto', None)),
        out_specs=(P('data', 'proto'), P('data', 'proto'), P(), P('data', None), P('data', None), P('proto', None)),
        check_vma=False)
```

time: 250 us -> 103 us (0.41)
  waiting for transfers between devices: 94 us -> 0 us
  blocking collectives: 62.8 us -> 0 us
  Pallas kernels: 50.2 us -> 90.8 us
  between operations: 17.1 us -> 2.48 us
  matrix products: 12.7 us -> 0 us
  other arithmetic: 4.16 us -> 0 us
    psum x2 -> x0, waiting for transfers between devices: 94 us -> none  [the longest x1 93.9 us: local_step(): lax.psum(jnp.einsum('nk,kd->nd', hone, protos, preferred_element_type=F32...]
    psum x1 -> x0, blocking collectives: 62.8 us -> none  [local_step(): loss_value = -lax.psum(part_loss, ('proto', 'data')) / (2 * total_rows)]
    pallas_call x1, Pallas kernels: 50.2 us -> 90.8 us  [local_step(): pl.pallas_call(functools.partial(step_kernel, total_rows, total_protos),...]
    dot_general x6 -> x0, matrix products: 12.7 us -> none  [the longest x2 6.36 us: view_terms(): scores = jnp.einsum('nd,kd->nk', emb, protos, preferred_element_type=F32)]
    reduce_sum x2 -> x0, other arithmetic: 4.16 us -> none  [local_step(): part_loss = jnp.sum(codes_two * logp_one) + jnp.sum(codes_one * logp_two)]
    unnamed x19 -> x13, local copies, waits for them, and re-layouts: 6.36 us -> 9.22 us
  transfers between devices with their start and end apart: 2 -> 0, of which waited for: 1 -> 0; matrix products, arithmetic and copies ran while one was open for 4% -> 0% of each run, Pallas kernels for 0% -> 0%
where the time goes in v2:
time: 103 us
  Pallas kernels  90.8 us (88%)
  local copies, waits for them, and re-layouts  9.22 us (9%)
  between operations  2.48 us (2%)
    pallas_call x1, Pallas kernels, local_step(): pl.pallas_call(functools.partial(step_kernel, total_rows, total_protos),...  90.8 us
    unnamed x13, local copies, waits for them, and re-layouts  9.22 us

profile of v2, /device:TPU:0, one launch (start us, length us, event | category | flops | bytes accessed | tf_op | source)
XLA Modules:
  0.0 102.5 jit_solution(17257258408160585568)
XLA Ops:
  0.6 90.8 %shard_map.82 = (f32[2048,256]{1,0:T(8,128)}, f32[2048,256]{1,0:T(8,128)}, f32[1,1]{1,0:T(1,128)}, f32[2048,256]{1,0:T(8,128)}, f32[2048,256]{1,0:T(8,128)}, /*index=5*/f32[256,256]{1,0:T(8,128)}) custom-call(bf16[2048,256]{1,0:T(8,128)(2,1)} %z1.1, bf16[2048,256]{1,0:T(8,128)(2,1)} %z2.1, bf16[256,256]{1,0:T(8,128)(2,1)} %c_ref.1), custom_call_target="tpu_custom_call" | custom-call | tf_op jit(solution)/shard_map/pallas_call | solution.py:459
  91.5 0.0 copy-start.2
  91.5 3.2 %copy.15 = f32[2048,256]{1,0:T(8,128)} copy(f32[2048,256]{1,0:T(8,128)} %get-tuple-element.24) | data formatting | bytes 4194304
  94.7 0.0 copy-done.2
  94.7 0.0 copy-start.1
  94.7 1.3 %copy.16 = f32[2048,256]{1,0:T(8,128)} copy(f32[2048,256]{1,0:T(8,128)S(1)} %copy-done.2) | data formatting | bytes 4194304
  96.7 0.3 copy-done.1
  97.0 0.0 copy-start
  97.0 1.3 %copy.18 = f32[2048,256]{1,0:T(8,128)} copy(f32[2048,256]{1,0:T(8,128)S(1)} %copy-done.1) | data formatting | bytes 4194304
  98.4 1.0 %copy-done = f32[2048,256]{1,0:T(8,128)S(1)} copy-done((f32[2048,256]{1,0:T(8,128)S(1)}, f32[2048,256]{1,0:T(8,128)}, u32[]{:S(2)}) %copy-start) | copy-done | bytes 2097176
  99.4 0.0 copy-start.3
  99.4 1.3 %copy.19 = f32[2048,256]{1,0:T(8,128)} copy(f32[2048,256]{1,0:T(8,128)S(1)} %copy-done) | data formatting | bytes 4194304
  100.7 0.0 copy-done.3
  100.7 0.7 copy.20
Async XLA Ops:
  91.5 3.2 %copy-start.2 = (f32[2048,256]{1,0:T(8,128)S(1)}, f32[2048,256]{1,0:T(8,128)}, u32[]{:S(2)}) copy-start(f32[2048,256]{1,0:T(8,128)} %get-tuple-element.25) | copy-start | bytes 6291460
  94.7 2.3 %copy-start.1 = (f32[2048,256]{1,0:T(8,128)S(1)}, f32[2048,256]{1,0:T(8,128)}, u32[]{:S(2)}) copy-start(f32[2048,256]{1,0:T(8,128)} %get-tuple-element.27) | copy-start | bytes 6291460
  97.0 2.3 %copy-start = (f32[2048,256]{1,0:T(8,128)S(1)}, f32[2048,256]{1,0:T(8,128)}, u32[]{:S(2)}) copy-start(f32[2048,256]{1,0:T(8,128)} %get-tuple-element.28) | copy-start | bytes 6291460
  99.4 1.3 %copy-start.3 = (f32[256,256]{1,0:T(8,128)S(1)}, f32[256,256]{1,0:T(8,128)}, u32[]{:S(2)}) copy-start(f32[256,256]{1,0:T(8,128)} %get-tuple-element.29) | copy-start | bytes 786436

commit v3 on v0

v3 whole, which is shorter than its diff:
```python
import functools
import re

import jax
import jax.numpy as jnp
from jax import lax
from jax.experimental import pallas as pl
from jax.experimental.pallas import tpu as pltpu
from jax.sharding import PartitionSpec as P

EPSILON = 0.05
TEMP_TAU = 0.1
ITERS = 3
LINE = 4
AXES = 3
MESH = pl.DeviceIdType.MESH
F32 = jnp.float32
BF16 = jnp.bfloat16
LANES = 128
SUM_CUTS = (0, 1408, 2816, 4096)
C_CUTS = (0, 80, 160, 256)
G_CUTS = (0, 24, 48, 64)
AG_SEMS = 27
DISTS = (2, 1, 3)


def _nt(a, b):
    return lax.dot_general(a, b, (((1,), (1,)), ((), ())), preferred_element_type=F32)


def _nn(a, b):
    return jnp.dot(a, b, preferred_element_type=F32)


def _col_to_row(s):
    r = lax.broadcasted_iota(jnp.int32, (LANES, LANES), 0)
    c = lax.broadcasted_iota(jnp.int32, (LANES, LANES), 1)
    return jnp.sum(jnp.where(r == c, s, 0.0), axis=0, keepdims=True)


def _row_to_col(row, n=LANES, shift=0):
    r = lax.broadcasted_iota(jnp.int32, (n, LANES), 0)
    c = lax.broadcasted_iota(jnp.int32, (n, LANES), 1)
    return jnp.sum(jnp.where(c == r + shift, row, 0.0), axis=1, keepdims=True)


def _parts(cuts):
    return tuple(zip(cuts[:-1], cuts[1:]))


class _Env:
    def __init__(self):
        self.me = lax.axis_index('proto')
        self.core = lax.axis_index('data')
        me = self.me
        self.pos = [lax.rem(me, LINE), lax.rem(lax.div(me, LINE), LINE), lax.div(me, LINE * LINE)]
        self.stride = [1, LINE, LINE * LINE]
        self.pending = []
        self.partner = (me, 1 - self.core)

    def p(self, axis, d):
        return self.pos[axis] if d == 0 else lax.rem(self.pos[axis] + d, LINE)

    def peer(self, axis, d):
        return (self.me + (self.p(axis, d) - self.pos[axis]) * self.stride[axis], self.core)

    def remote(self, src, dst, ss, rs, dev):
        cp = pltpu.make_async_remote_copy(src, dst, ss, rs, device_id=dev, device_id_type=MESH)
        cp.start()
        self.pending.append(cp)
        return cp

    def arrived(self, ref, rs):
        pltpu.make_async_remote_copy(ref, ref, rs, rs, device_id=self.partner, device_id_type=MESH).wait_recv()

    def drain(self):
        for cp in self.pending:
            cp.wait_send()
        self.pending = []


class _Gather:
    def __init__(self, env, buf, cuts, ssem, rsem, twin=None):
        self.env, self.buf, self.parts = env, buf, _parts(cuts)
        self.ssem, self.rsem, self.twin = ssem, rsem, twin

    def at(self, j, i0, i1, i2):
        ids = [None] * AXES
        for axis, i in zip((j, j + 1, j + 2), (i0, i1, i2)):
            ids[axis % AXES] = slice(None) if i is None else i
        r0, r1 = self.parts[j]
        return self.buf.at[ids[2], ids[1], ids[0], r0:r1, :]

    def p(self, j, level, d):
        return self.env.p((j + level) % AXES, d)

    def send(self, j, k, ref, level, d, src=None):
        i = j * AG_SEMS + k
        self.env.remote(ref if src is None else src, ref, self.ssem.at[i], self.rsem.at[i],
                        self.env.peer((j + level) % AXES, d))

    def recv(self, j, k, ref):
        self.env.arrived(ref, self.rsem.at[j * AG_SEMS + k])

    def s1_send(self, src=None):
        for d in DISTS:
            for j, (r0, r1) in enumerate(self.parts):
                ref = self.at(j, self.p(j, 0, 0), self.p(j, 1, 0), self.p(j, 2, 0))
                self.send(j, d - 1, ref, 0, d, None if src is None else src.at[r0:r1, :])

    def s1_recv(self):
        for d in (1, 3, 2):
            for j in range(AXES):
                self.recv(j, d - 1, self.at(j, self.p(j, 0, LINE - d), self.p(j, 1, 0), self.p(j, 2, 0)))

    def chunk(self, j, level, k, m):
        if level == 1:
            return self.at(j, self.p(j, 0, k), self.p(j, 1, m), self.p(j, 2, 0))
        return self.at(j, None, self.p(j, 1, k), self.p(j, 2, m))

    def a_send(self, level, k):
        base = 12 * level - 9
        for j in range(AXES):
            ref = self.chunk(j, level, k, 0)
            self.send(j, base + k, ref, level, 1)
            self.send(j, base + LINE + k, ref, level, 3)

    def a_recv(self, level, k):
        base = 12 * level - 9
        for j in range(AXES):
            self.recv(j, base + k, self.chunk(j, level, k, 3))
            self.recv(j, base + LINE + k, self.chunk(j, level, k, 1))

    def b_send(self, level, k):
        base = 12 * level - 1
        d = 1 if k < 2 else 3
        for j in range(AXES):
            self.send(j, base + k, self.chunk(j, level, k, LINE - d), level, d)

    def b_recv(self, level, k):
        base = 12 * level - 1
        for j in range(AXES):
            self.recv(j, base + k, self.chunk(j, level, k, 2))

    def t_send(self, k, m):
        ts, tr = self.twin
        for j in range(AXES):
            i = (j * LINE + k) * LINE + m
            ref = self.chunk(j, 2, k, m)
            self.env.remote(ref, ref, ts.at[i], tr.at[i], self.env.partner)

    def t_recv(self):
        for j in range(AXES):
            for k in range(LINE):
                for m in range(LINE):
                    self.env.arrived(self.chunk(j, 2, k, m), self.twin[1].at[(j * LINE + k) * LINE + m])

    def run(self, ops):
        for op in re.findall('[a-zA-Z][0-9]*', ops):
            args = [int(c) for c in op[1:]]
            {'S': self.s1_send, 's': self.s1_recv, 'A': self.a_send, 'a': self.a_recv,
             'B': self.b_send, 'b': self.b_recv, 'T': self.t_send, 'U': self.t_recv}[op[0]](*args)


def write_kernel(mine, code1, code2, gfull, gp, o1, o2, g1, g2, og, sem):
    pairs = [(code1, o1), (code2, o2), (gp, og)]
    for view, out in enumerate((g1, g2)):
        pairs.append((gfull.at[:, view * mine:(view + 1) * mine, :], out))
    copies = [pltpu.make_async_copy(src, dst, sem.at[i]) for i, (src, dst) in enumerate(pairs)]
    for cp in copies:
        cp.start()
    for cp in copies:
        cp.wait()


def step_kernel(total_rows, total_protos, z1h, z2h, ch,
                code1, code2, loss_out, gfull, gp_out,
                z1, z2, y1, y2, c_ref, f_scr, e_scr, cfull, lrow, frow, vall, zr, dall,
                cacc, vb, ub, stage, csend, crecv, first, later, lossb, losst, dacc, drecv, dz, cst,
                lsem, c_ssem, c_rsem, s_ssem, s_rsem, a_ssem, a_rsem, t_ssem, t_rsem,
                v_ssem, v_rsem, g_ssem, g_rsem, l_ssem, l_rsem, x_ssem, x_rsem, o_sem):
    env = _Env()
    me, core, pos, partner = env.me, env.core, env.pos, env.partner
    remote = env.remote
    rows, cols = z1.shape[0], c_ref.shape[0]
    mine = zr.shape[0] // 2
    blocks = LINE ** AXES
    fscale = 1.0 / (2 * total_rows * TEMP_TAU)
    zs, ys = (z1, z2), (y1, y2)
    chunks = rows // cols

    barrier = pltpu.get_barrier_semaphore()
    pl.semaphore_signal(barrier, inc=1, device_id=partner, device_id_type=MESH)
    for axis in range(AXES):
        for d in DISTS:
            pl.semaphore_signal(barrier, inc=1, device_id=env.peer(axis, d), device_id_type=MESH)
    loads = [pltpu.make_async_copy(src, dst, lsem.at[i]) for i, (src, dst) in enumerate(
        ((ch, c_ref), (z1h, z1), (z2h, z2), (ch, cfull.at[pos[2], pos[1], pos[0]])))]
    gc = _Gather(env, cfull, C_CUTS, a_ssem, a_rsem, (t_ssem, t_rsem))
    gg = _Gather(env, gfull, G_CUTS, g_ssem, g_rsem)
    for cp in loads[:3]:
        cp.start()

    def scores(view):
        cacc[view] = jnp.zeros((cols, LANES), F32)

        def body(i, _):
            n0 = pl.multiple_of(i * cols, cols)
            s = _nt(c_ref[...], zs[view][pl.ds(n0, cols), :])
            f = jnp.exp(s * (1.0 / TEMP_TAU))
            stage[0, 2 + view:3 + view, pl.ds(n0, cols)] = jnp.sum(f, axis=0, keepdims=True)
            e = f * f
            f_scr[view, :, pl.ds(n0, cols)] = f
            e_scr[view, :, pl.ds(n0, cols)] = e
            cacc[view] += e[:, :LANES] + e[:, LANES:]
            return 0
        lax.fori_loop(0, chunks, body, 0, unroll=2)
        zr[view * mine:(view + 1) * mine, :] = zs[view][pl.ds(pl.multiple_of(me * mine, mine), mine), :]

    def other_scores(view):
        def body(i, _):
            n0 = pl.multiple_of(i * cols, cols)
            f = jnp.exp(_nt(c_ref[...], ys[view][pl.ds(n0, cols), :]) * (1.0 / TEMP_TAU))
            e_scr[view, :, pl.ds(rows + n0, cols)] = f * f
            return 0
        lax.fori_loop(0, chunks, body, 0, unroll=2)

    def row_scores(lo, hi):
        def body(q, _):
            z_, y_, x_ = block(q)
            l = _nt(zr[...], cfull[z_, y_, x_]) * (1.0 / TEMP_TAU)
            lrow[q] = l
            frow[q] = jnp.exp(l)
            return 0
        lax.fori_loop(lo, hi, body, 0, unroll=2)

    def block(q):
        return lax.div(q, LINE * LINE), lax.rem(lax.div(q, LINE), LINE), lax.rem(q, LINE)

    def column_sums(it):
        for view in range(2):
            for h in range(2):
                k = 2 * view + h
                s = jnp.sum(cacc[view, h * LANES:(h + 1) * LANES, :], axis=1, keepdims=True)
                csend[it, k:k + 1, :] = _col_to_row(s)

    def spread(vrow):
        for view in range(2):
            for h in range(2):
                k = 2 * view + h
                vb[view, h * LANES:(h + 1) * LANES, :] = jnp.broadcast_to(
                    _row_to_col(vrow[k:k + 1, :]), (LANES, LANES))

    def exchange():
        cp = remote(csend.at[0], crecv.at[0], c_ssem.at[0], c_rsem.at[0], partner)
        cp.wait_recv()
        return csend[0] + crecv[0]

    def row_sums(it, width):
        step = 4 * LANES
        for view in range(2):
            def body(j, _, view=view):
                acc = [jnp.zeros((8, LANES), F32) for _ in range(4)]
                offs = [pl.multiple_of(j * step + t * LANES, LANES) for t in range(4)]
                for g in range(0, cols, 8):
                    w = vb[view, g:g + 8, :]
                    for t, l0 in enumerate(offs):
                        acc[t] = acc[t] + e_scr[view, g:g + 8, pl.ds(l0, LANES)] * w
                for t, l0 in enumerate(offs):
                    stage[it, view:view + 1, pl.ds(l0, LANES)] = jnp.sum(acc[t], axis=0, keepdims=True)
                return 0
            lax.fori_loop(0, width // step, body, 0)

    def weighted_columns():
        for view in range(2):
            def body(g, _, view=view):
                for gi in range(2):
                    k0 = pl.multiple_of(g * 16 + gi * 8, 8)
                    acc = [None] * 4
                    for t in range(2 * rows // LANES):
                        ls = slice(t * LANES, (t + 1) * LANES)
                        x = e_scr[view, pl.ds(k0, 8), ls] * ub[view, :, ls]
                        acc[t % 4] = x if acc[t % 4] is None else acc[t % 4] + x
                    cacc[view, pl.ds(k0, 8), :] = (acc[0] + acc[1]) + (acc[2] + acc[3])
                return 0
            lax.fori_loop(0, cols // 16, body, 0)

    def v_refs(st, d):
        ids = [pos[2], pos[1], pos[0]][:AXES - st]
        ids[-1] = env.p(st, d)
        return vall.at[tuple(ids)]

    def vsend(st):
        for d in DISTS:
            i = st * AXES + d - 1
            remote(v_refs(st, 0), v_refs(st, 0), v_ssem.at[i], v_rsem.at[i], env.peer(st, d))

    def vrecv(st):
        for d in DISTS:
            env.arrived(v_refs(st, LINE - d), v_rsem.at[st * AXES + d - 1])

    def hidden(slot):
        if slot in (0, 1):
            env.arrived(ys[slot], x_rsem.at[slot])
            other_scores(slot)
        elif slot == 6:
            gc.t_recv()
            row_scores(0, 20)
        elif slot == 7:
            row_scores(20, 42)
        elif slot == 8:
            row_scores(42, blocks)

    @pl.when(core == 1)
    def _():
        loads[0].wait()
        for view in range(2):
            loads[1 + view].wait()
            scores(view)
        pl.semaphore_wait(barrier, 1 + AXES * (LINE - 1))
        column_sums(0)
        total = exchange()
        for it in range(ITERS):
            last = it == ITERS - 1
            vrow = 1.0 / (float(total_protos) * total)
            if last:
                vall[pos[2], pos[1], pos[0]] = vrow
                vsend(0)
            spread(vrow)
            row_sums(it, rows if it == 0 else 2 * rows)
            buf = first if it == 0 else later.at[it - 1]
            if it == 0:
                env.arrived(stage.at[0, :, rows:], x_rsem.at[2])
            for j, (l0, l1) in enumerate(_parts(SUM_CUTS)):
                buf[0, pos[j], :, l0:l1] = stage[it, :buf.shape[2], l0:l1]
            for st in range(AXES):
                for d in DISTS:
                    for j, (l0, l1) in enumerate(_parts(SUM_CUTS)):
                        ax = (st + j) % AXES
                        i = ((it * AXES + st) * AXES + j) * (LINE - 1) + d - 1
                        src = buf.at[st, pos[ax], :, l0:l1]
                        remote(src, src, s_ssem.at[i], s_rsem.at[i], env.peer(ax, d))
                hidden(it * AXES + st)
                if last:
                    vrecv(st)
                    if st < AXES - 1:
                        vsend(st + 1)
                for j, (l0, l1) in enumerate(_parts(SUM_CUTS)):
                    ax = (st + j) % AXES
                    for d in DISTS:
                        i = ((it * AXES + st) * AXES + j) * (LINE - 1) + d - 1
                        env.arrived(buf.at[st, env.p(ax, LINE - d), :, l0:l1], s_rsem.at[i])
                    tot = (buf[st, 0, :, l0:l1] + buf[st, 1, :, l0:l1]) + (buf[st, 2, :, l0:l1] + buf[st, 3, :, l0:l1])
                    if st < AXES - 1:
                        buf[st + 1, pos[(st + 1 + j) % AXES], :, l0:l1] = tot
                        continue
                    if it == 0:
                        dall[2:4, l0:l1] = tot[2:4]
                    if last:
                        dall[0:2, l0:l1] = tot
                    else:
                        u = 1.0 / (float(total_rows) * tot)
                        for view in range(2):
                            ub[view, :, l0:l1] = jnp.broadcast_to(u[view:view + 1], (8, l1 - l0))
            if not last:
                weighted_columns()
                column_sums(it + 1)
                total = csend[it + 1]
        remote(dall.at[:, rows:], dall.at[:, :rows], x_ssem.at[3], x_rsem.at[3], partner)
        remote(vall, vall, x_ssem.at[4], x_rsem.at[4], partner)
        env.drain()

    @pl.when(core == 0)
    def _():
        loads[3].start()
        loads[0].wait()
        loads[3].wait()
        pl.semaphore_wait(barrier, 1 + AXES * (LINE - 1))
        gc.run('S')
        loads[1].wait()
        remote(z1, y1, x_ssem.at[0], x_rsem.at[0], partner)
        scores(0)
        gc.run('sA10A11A12A13A20T00')
        loads[2].wait()
        scores(1)
        column_sums(0)
        vrow = 1.0 / (float(total_protos) * exchange())
        spread(vrow)
        row_sums(0, rows)
        remote(stage.at[0, :, :rows], stage.at[0, :, rows:], x_ssem.at[2], x_rsem.at[2], partner)
        remote(z2, y2, x_ssem.at[1], x_rsem.at[1], partner)
        gc.run('a10B10a11B11a12B12a13B13A21A23T10T30')
        gc.run('a20B20T01T03b10b11b12b13A22T20')
        gc.run('a21B21T11T13a23B23T31T33')
        gc.run('b20T02b21T12b23T32')
        gc.run('a22B22T21T23b22T22')
        row_scores(0, blocks)
        env.arrived(dall.at[:, :rows], x_rsem.at[3])
        env.arrived(vall, x_rsem.at[4])
        env.drain()

    tile = pl.multiple_of(lax.div(me * mine, LANES) * LANES, LANES)
    shift = lax.rem(me * mine, LANES)
    dv = dall[:, pl.ds(tile, LANES)]
    col = [_row_to_col(dv[i:i + 1, :], mine, shift) for i in range(4)]
    rc = jnp.broadcast_to(1.0 / jnp.concatenate(col[0:2], axis=0), (2 * mine, LANES))
    den = jnp.concatenate(col[2:4], axis=0)
    dc = jnp.broadcast_to(1.0 / den, (2 * mine, LANES))
    ld = jnp.broadcast_to(jnp.log(den), (2 * mine, LANES))

    def code_rows(q, h):
        z_, y_, x_ = block(q)
        f = frow[q, :, h * LANES:(h + 1) * LANES]
        v0 = jnp.broadcast_to(vall[z_, y_, x_, h:h + 1, :], (mine, LANES))
        v1 = jnp.broadcast_to(vall[z_, y_, x_, 2 + h:3 + h, :], (mine, LANES))
        return f, f * f * (rc * jnp.concatenate([v0, v1], axis=0))

    def dzbody(i, acc):
        hs = []
        for x_ in range(LINE):
            for h in range(2):
                f, code = code_rows(i * LINE + x_, h)
                other = jnp.concatenate([code[mine:], code[:mine]], axis=0)
                hs.append(((f * dc - other) * fscale).astype(BF16))
        cl = cfull[lax.div(i, LINE), lax.rem(i, LINE)].reshape(LINE * cols, cols)
        return acc + _nn(jnp.concatenate(hs, axis=1), cl)

    dz[...] = lax.fori_loop(0, LINE * LINE, dzbody, jnp.zeros((2 * mine, cols), F32), unroll=2)

    own = pltpu.make_async_copy(dz, gfull.at[pos[2], pos[1], pos[0]], o_sem.at[0])
    own.start()
    gg.s1_send(dz)
    spread(vall[pos[2], pos[1], pos[0]])
    dacc[...] = jnp.zeros((cols, cols), F32)

    def out_copy(view, i):
        n0 = pl.multiple_of(i * cols, cols)
        return pltpu.make_async_copy(cst.at[view, pl.ds(n0, cols), :], (code1, code2)[view].at[pl.ds(n0, cols), :],
                                     o_sem.at[2 + view * chunks + i])

    def columns(i):
        def body(i, _):
            n0 = pl.multiple_of(i * cols, cols)
            inv = 1.0 / dall[:, pl.ds(n0, cols)]
            code, prob = [], []
            for view in range(2):
                w = jnp.concatenate([vb[view], vb[view]], axis=1)
                code.append(e_scr[view, :, pl.ds(n0, cols)] * w * inv[view:view + 1, :])
                prob.append(f_scr[view, :, pl.ds(n0, cols)] * inv[2 + view:3 + view, :])
            for view in range(2):
                h = ((prob[view] - code[1 - view]) * fscale).astype(BF16)
                dacc[...] += _nn(h, zs[view][pl.ds(n0, cols), :])
                cst[view, pl.ds(n0, cols), :] = code[view].T
                out_copy(view, i).start()
            return 0
        lax.fori_loop(i * 2, i * 2 + 2, body, 0)

    def lbody(q, acc):
        for h in range(2):
            f, code = code_rows(q, h)
            lp = lrow[q, :, h * LANES:(h + 1) * LANES] - ld
            other = jnp.concatenate([code[mine:], code[:mine]], axis=0)
            acc = acc + other * lp
        return acc
    part = lax.fori_loop(0, blocks, lbody, jnp.zeros((2 * mine, LANES), F32), unroll=2)
    lossb[0, pos[0]] = jnp.sum(part.reshape(2 * mine // 8, 8, LANES), axis=0)

    def loss_send(st):
        ref = lossb.at[st, pos[st]]
        for d in DISTS:
            i = st * AXES + d - 1
            remote(ref, ref, l_ssem.at[i], l_rsem.at[i], env.peer(st, d))

    def loss_recv(st):
        for d in DISTS:
            env.arrived(lossb.at[st, env.p(st, LINE - d)], l_rsem.at[st * AXES + d - 1])
        return (lossb[st, 0] + lossb[st, 1]) + (lossb[st, 2] + lossb[st, 3])

    own.wait()
    gg.run('sA10A11A12A13')
    loss_send(0)
    gg.run('A20')
    columns(0)
    gg.run('a10B10a11B11a12B12a13B13A21A23')
    lossb[1, pos[1]] = loss_recv(0)
    loss_send(1)
    columns(1)
    gg.run('b10b11b12b13A22a20B20')
    lossb[2, pos[2]] = loss_recv(1)
    loss_send(2)
    columns(2)
    gg.run('a21B21a23B23')
    columns(3)
    losst[0] = loss_recv(2)
    lcp = remote(losst.at[0], losst.at[1], l_ssem.at[9], l_rsem.at[9], partner)
    dcp = remote(dacc, drecv, l_ssem.at[10], l_rsem.at[10], partner)
    gg.run('a22B22')
    lcp.wait_recv()
    loss_out[...] = jnp.sum(losst[0] + losst[1], keepdims=True) * (-1.0 / (2 * total_rows))
    dcp.wait_recv()
    drecv[...] = dacc[...] + drecv[...]
    gpc = pltpu.make_async_copy(drecv, gp_out, o_sem.at[1])
    gpc.start()
    gg.run('b20b21b23b22')
    gpc.wait()
    for view in range(2):
        for i in range(chunks):
            out_copy(view, i).wait()
    env.drain()


def solution(mesh):
    proto_size = mesh.shape['proto']
    data_size = mesh.shape['data']

    def local_step(emb_one, emb_two, protos):
        rows, dim = emb_one.shape
        cols = protos.shape[0]
        total_rows = rows * data_size
        total_protos = cols * proto_size
        mine = rows // proto_size
        vm = pl.BlockSpec(memory_space=pltpu.VMEM)
        hbm = pl.BlockSpec(memory_space=pltpu.HBM)
        free = pl.BlockSpec(memory_space=pl.ANY)
        nsem = ITERS * AXES * AXES * (LINE - 1)
        dma = lambda n: pltpu.SemaphoreType.DMA((n,))
        grid3 = (LINE,) * AXES
        sds = jax.ShapeDtypeStruct
        code = sds((rows, cols), F32)
        zbuf = pltpu.VMEM((rows, dim), BF16)
        square = pltpu.VMEM((cols, dim), F32)
        rowbuf = pltpu.VMEM((proto_size, 2 * mine, cols), F32)
        small = pltpu.VMEM((ITERS, 4, LANES), F32)
        spread = pltpu.VMEM((2, cols, LANES), F32)
        args = [pltpu.with_memory_space_constraint(a, pltpu.HBM) for a in (emb_one, emb_two, protos)]
        code1, code2, loss, gall, gp = pl.pallas_call(
            functools.partial(step_kernel, total_rows, total_protos),
            out_shape=(code, code, sds((1, 1), F32),
                       sds(grid3 + (2 * mine, dim), F32), sds((cols, dim), F32)),
            in_specs=[hbm] * 3,
            out_specs=(free, free, vm, free, free),
            scratch_shapes=[
                zbuf, zbuf, zbuf, zbuf, pltpu.VMEM((cols, dim), BF16),
                pltpu.VMEM((2, cols, rows), F32),
                pltpu.VMEM((2, cols, 2 * rows), F32),
                pltpu.VMEM(grid3 + (cols, dim), BF16),
                rowbuf, rowbuf,
                pltpu.VMEM(grid3 + (4, LANES), F32),
                pltpu.VMEM((2 * mine, dim), BF16),
                pltpu.VMEM((4, total_rows), F32),
                spread, spread,
                pltpu.VMEM((2, 8, total_rows), F32),
                pltpu.VMEM((ITERS, 4, total_rows), F32),
                small, small,
                pltpu.VMEM((AXES, LINE, 4, total_rows), F32),
                pltpu.VMEM((ITERS - 1, AXES, LINE, 2, total_rows), F32),
                pltpu.VMEM((AXES, LINE, 8, LANES), F32),
                pltpu.VMEM((2, 8, LANES), F32),
                square, square,
                pltpu.VMEM((2 * mine, dim), F32),
                pltpu.VMEM((2, rows, cols), F32),
                dma(4), dma(ITERS), dma(ITERS), dma(nsem), dma(nsem),
                dma(AXES * AG_SEMS), dma(AXES * AG_SEMS), dma(48), dma(48),
                dma(9), dma(9), dma(AXES * AG_SEMS), dma(AXES * AG_SEMS), dma(11), dma(11),
                dma(5), dma(5), dma(2 + 2 * rows // cols),
            ],
            compiler_params=pltpu.CompilerParams(collective_id=0, has_side_effects=True,
                                                 vmem_limit_bytes=44 * 2 ** 20),
        )(*args)
        blocked = sds((proto_size, mine, dim), F32)
        o1, o2, g1, g2, og = pl.pallas_call(
            functools.partial(write_kernel, mine),
            out_shape=(code, code, blocked, blocked, sds((cols, dim), F32)),
            in_specs=[vm] * 4,
            out_specs=(hbm,) * 5,
            scratch_shapes=[dma(5)],
            compiler_params=pltpu.CompilerParams(vmem_limit_bytes=2 ** 20),
        )(code1, code2, gall.reshape(proto_size, 2 * mine, dim), gp)
        return o1, o2, loss[0, 0], g1.reshape(rows, dim), g2.reshape(rows, dim), og

    return jax.shard_map(
        local_step, mesh=mesh,
        in_specs=(P('data', None), P('data', None), P('proto', None)),
        out_specs=(P('data', 'proto'), P('data', 'proto'), P(), P('data', None), P('data', None), P('proto', None)),
        check_vma=False)
```

time: 1620 us -> 86.6 us (0.05)
  blocking collectives: 1470 us -> 0 us
  waiting for transfers between devices: 85.6 us -> 0 us
  Pallas kernels: 0 us -> 84.1 us
  other arithmetic: 25.6 us -> 0 us
    psum x12 -> x0, blocking collectives: 1470 us -> none  [the longest x6 1390 us: view_terms(): row_sum = lax.psum(jnp.sum(transport, axis=1, keepdims=True), 'proto')]
    psum x2 -> x0, waiting for transfers between devices: 85.6 us -> none  [the longest x1 85.6 us: local_step(): lax.psum(jnp.einsum('nk,kd->nd', logit_grad_one, protos, preferred_elemen...]
    pallas_call x0 -> x2, Pallas kernels: none -> 84.1 us  [the longest x1 80.6 us: local_step(): pl.pallas_call(functools.partial(step_kernel, total_rows, total_protos),...]
    reduce_sum x11 -> x0, other arithmetic: 16.7 us -> none  [the longest x4 6 us: view_terms(): row_sum = lax.psum(jnp.sum(transport, axis=1, keepdims=True), 'proto')]
  transfers between devices with their start and end apart: 2 -> 0, of which waited for: 1 -> 0; matrix products, arithmetic and copies ran while one was open for 1% -> 0% of each run, Pallas kernels for 0% -> 0%
where the time goes in v3:
time: 86.6 us; the launch traced here: 86.5 us
  Pallas kernels  84.1 us (97%)
  between operations  2.41 us (3%)
    pallas_call x1, Pallas kernels, local_step(): pl.pallas_call(functools.partial(step_kernel, total_rows, total_protos),...  80.6 us
    pallas_call x1, Pallas kernels, local_step(): pl.pallas_call(functools.partial(write_kernel, mine), out_shape=(code, co...  3.46 us

profile of v3, /device:TPU:0, one launch (start us, length us, event | category | flops | bytes accessed | tf_op | source)
XLA Modules:
  0.0 86.5 jit_solution(6220557557922008388)
XLA Ops:
  0.6 80.6 %shard_map.82 = (f32[2048,256]{1,0:T(8,128)S(1)}, f32[2048,256]{1,0:T(8,128)S(1)}, f32[1,1]{1,0:T(1,128)}, f32[4,4,4,64,256]{4,3,2,1,0:T(8,128)S(1)}, f32[256,256]{1,0:T(8,128)S(1)}) custom-call(bf16[2048,256]{1,0:T(8,128)(2,1)} %z1h.1, bf16[2048,256]{1,0:T(8,128)(2,1)} %z2h.1, bf16[256,256]{1,0:T(8,128)(2,1)} %ch.1), custom_call_target="tpu_custom_call" | custom-call | tf_op jit(solution)/shard_map/pallas_call | solution.py:536
  81.2 3.5 %shard_map.83 = (f32[2048,256]{1,0:T(8,128)}, f32[2048,256]{1,0:T(8,128)}, f32[64,32,256]{2,1,0:T(8,128)}, f32[64,32,256]{2,1,0:T(8,128)}, f32[256,256]{1,0:T(8,128)}) custom-call(f32[2048,256]{1,0:T(8,128)S(1)} %get-tuple-element.16.code1, f32[2048,256]{1,0:T(8,128)S(1)} %get-tuple-element.17.code2, f32[64,64,256]{2,1,0:T(8,128)S(1)} %bitcast.4, ...), custom_call_target="tpu_custom_call" | custom-call | tf_op jit(solution)/shard_map/pallas_call | solution.py:571

commit v4 on v3

--- a/solution.py
+++ b/solution.py
@@ -20,7 +20,7 @@
 SUM_CUTS = (0, 1408, 2816, 4096)
 C_CUTS = (0, 80, 160, 256)
 G_CUTS = (0, 24, 48, 64)
-AG_SEMS = 27
+AG_SEMS = 19
 DISTS = (2, 1, 3)
 
 
@@ -67,8 +67,11 @@
     def remote(self, src, dst, ss, rs, dev):
         cp = pltpu.make_async_remote_copy(src, dst, ss, rs, device_id=dev, device_id_type=MESH)
         cp.start()
-        self.pending.append(cp)
         return cp
+
+    def sent(self, ref, ss):
+        self.pending.append(pltpu.make_async_remote_copy(ref, ref, ss, ss, device_id=self.partner,
+                                                         device_id_type=MESH))
 
     def arrived(self, ref, rs):
         pltpu.make_async_remote_copy(ref, ref, rs, rs, device_id=self.partner, device_id_type=MESH).wait_recv()
@@ -76,7 +79,7 @@
     def drain(self):
         for cp in self.pending:
             cp.wait_send()
-        self.pending = []
+        self.pending.clear()
 
 
 class _Gather:
@@ -94,24 +97,33 @@
     def p(self, j, level, d):
         return self.env.p((j + level) % AXES, d)
 
-    def send(self, j, k, ref, level, d, src=None):
-        i = j * AG_SEMS + k
-        self.env.remote(ref if src is None else src, ref, self.ssem.at[i], self.rsem.at[i],
+    def send(self, j, group, k, ref, level, d, src=None):
+        self.env.remote(ref if src is None else src, ref, self.ssem.at[group], self.rsem.at[k],
                         self.env.peer((j + level) % AXES, d))
 
-    def recv(self, j, k, ref):
-        self.env.arrived(ref, self.rsem.at[j * AG_SEMS + k])
+    def some(self, blocks):
+        for level in range(AXES):
+            width = LINE ** level
+            if blocks <= width * (LINE - 1):
+                lead = (0,) * (AXES - 1 - level)
+                return self.buf.at[lead + (pl.ds(0, blocks // width),)]
+
+    def recv(self, k, blocks):
+        self.env.arrived(self.some(blocks), self.rsem.at[k])
+
+    def all_sent(self):
+        for group, blocks in enumerate((3, 8, 4, 32, 16)):
+            self.env.sent(self.some(blocks), self.ssem.at[group])
 
     def s1_send(self, src=None):
         for d in DISTS:
             for j, (r0, r1) in enumerate(self.parts):
                 ref = self.at(j, self.p(j, 0, 0), self.p(j, 1, 0), self.p(j, 2, 0))
-                self.send(j, d - 1, ref, 0, d, None if src is None else src.at[r0:r1, :])
+                self.send(j, 0, d - 1, ref, 0, d, None if src is None else src.at[r0:r1, :])
 
     def s1_recv(self):
         for d in (1, 3, 2):
-            for j in range(AXES):
-                self.recv(j, d - 1, self.at(j, self.p(j, 0, LINE - d), self.p(j, 1, 0), self.p(j, 2, 0)))
+            self.recv(d - 1, 1)
 
     def chunk(self, j, level, k, m):
         if level == 1:
@@ -119,41 +131,30 @@
         return self.at(j, None, self.p(j, 1, k), self.p(j, 2, m))
 
     def a_send(self, level, k):
-        base = 12 * level - 9
         for j in range(AXES):
             ref = self.chunk(j, level, k, 0)
-            self.send(j, base + k, ref, level, 1)
-            self.send(j, base + LINE + k, ref, level, 3)
+            for d in (1, 3):
+                self.send(j, 2 * level - 1, 8 * level - 5 + k, ref, level, d)
 
     def a_recv(self, level, k):
-        base = 12 * level - 9
-        for j in range(AXES):
-            self.recv(j, base + k, self.chunk(j, level, k, 3))
-            self.recv(j, base + LINE + k, self.chunk(j, level, k, 1))
+        self.recv(8 * level - 5 + k, 2 * LINE ** (level - 1))
 
     def b_send(self, level, k):
-        base = 12 * level - 1
         d = 1 if k < 2 else 3
         for j in range(AXES):
-            self.send(j, base + k, self.chunk(j, level, k, LINE - d), level, d)
+            self.send(j, 2 * level, 8 * level - 1 + k, self.chunk(j, level, k, LINE - d), level, d)
 
     def b_recv(self, level, k):
-        base = 12 * level - 1
-        for j in range(AXES):
-            self.recv(j, base + k, self.chunk(j, level, k, 2))
+        self.recv(8 * level - 1 + k, LINE ** (level - 1))
 
     def t_send(self, k, m):
         ts, tr = self.twin
         for j in range(AXES):
-            i = (j * LINE + k) * LINE + m
             ref = self.chunk(j, 2, k, m)
-            self.env.remote(ref, ref, ts.at[i], tr.at[i], self.env.partner)
+            self.env.remote(ref, ref, ts.at[0], tr.at[0], self.env.partner)
 
     def t_recv(self):
-        for j in range(AXES):
-            for k in range(LINE):
-                for m in range(LINE):
-                    self.env.arrived(self.chunk(j, 2, k, m), self.twin[1].at[(j * LINE + k) * LINE + m])
+        self.env.arrived(self.buf, self.twin[1].at[0])
 
     def run(self, ops):
         for op in re.findall('[a-zA-Z][0-9]*', ops):
@@ -253,15 +254,16 @@
 
     def exchange():
         cp = remote(csend.at[0], crecv.at[0], c_ssem.at[0], c_rsem.at[0], partner)
-        cp.wait_recv()
+        cp.wait()
         return csend[0] + crecv[0]
 
     def row_sums(it, width):
-        step = 4 * LANES
+        wide = 8
+        step = wide * LANES
         for view in range(2):
             def body(j, _, view=view):
-                acc = [jnp.zeros((8, LANES), F32) for _ in range(4)]
-                offs = [pl.multiple_of(j * step + t * LANES, LANES) for t in range(4)]
+                acc = [jnp.zeros((8, LANES), F32) for _ in range(wide)]
+                offs = [pl.multiple_of(j * step + t * LANES, LANES) for t in range(wide)]
                 for g in range(0, cols, 8):
                     w = vb[view, g:g + 8, :]
                     for t, l0 in enumerate(offs):
@@ -285,19 +287,16 @@
                 return 0
             lax.fori_loop(0, cols // 16, body, 0)
 
-    def v_refs(st, d):
-        ids = [pos[2], pos[1], pos[0]][:AXES - st]
-        ids[-1] = env.p(st, d)
-        return vall.at[tuple(ids)]
-
     def vsend(st):
+        ref = vall.at[(pos[2], pos[1], pos[0])[:AXES - st]]
         for d in DISTS:
-            i = st * AXES + d - 1
-            remote(v_refs(st, 0), v_refs(st, 0), v_ssem.at[i], v_rsem.at[i], env.peer(st, d))
+            remote(ref, ref, v_ssem.at[st], v_rsem.at[st], env.peer(st, d))
+
+    def v_some(st):
+        return vall.at[(0,) * (AXES - 1 - st) + (pl.ds(0, LINE - 1),)]
 
     def vrecv(st):
-        for d in DISTS:
-            env.arrived(v_refs(st, LINE - d), v_rsem.at[st * AXES + d - 1])
+        env.arrived(v_some(st), v_rsem.at[st])
 
     def hidden(slot):
         if slot in (0, 1):
@@ -334,22 +333,19 @@
             for j, (l0, l1) in enumerate(_parts(SUM_CUTS)):
                 buf[0, pos[j], :, l0:l1] = stage[it, :buf.shape[2], l0:l1]
             for st in range(AXES):
+                i = it * AXES + st
                 for d in DISTS:
                     for j, (l0, l1) in enumerate(_parts(SUM_CUTS)):
                         ax = (st + j) % AXES
-                        i = ((it * AXES + st) * AXES + j) * (LINE - 1) + d - 1
                         src = buf.at[st, pos[ax], :, l0:l1]
                         remote(src, src, s_ssem.at[i], s_rsem.at[i], env.peer(ax, d))
-                hidden(it * AXES + st)
+                hidden(i)
                 if last:
                     vrecv(st)
                     if st < AXES - 1:
                         vsend(st + 1)
+                env.arrived(buf.at[st, :LINE - 1], s_rsem.at[i])
                 for j, (l0, l1) in enumerate(_parts(SUM_CUTS)):
-                    ax = (st + j) % AXES
-                    for d in DISTS:
-                        i = ((it * AXES + st) * AXES + j) * (LINE - 1) + d - 1
-                        env.arrived(buf.at[st, env.p(ax, LINE - d), :, l0:l1], s_rsem.at[i])
                     tot = (buf[st, 0, :, l0:l1] + buf[st, 1, :, l0:l1]) + (buf[st, 2, :, l0:l1] + buf[st, 3, :, l0:l1])
                     if st < AXES - 1:
                         buf[st + 1, pos[(st + 1 + j) % AXES], :, l0:l1] = tot
@@ -368,7 +364,6 @@
                 total = csend[it + 1]
         remote(dall.at[:, rows:], dall.at[:, :rows], x_ssem.at[3], x_rsem.at[3], partner)
         remote(vall, vall, x_ssem.at[4], x_rsem.at[4], partner)
-        env.drain()
 
     @pl.when(core == 0)
     def _():
@@ -380,7 +375,6 @@
         loads[1].wait()
         remote(z1, y1, x_ssem.at[0], x_rsem.at[0], partner)
         scores(0)
-        gc.run('sA10A11A12A13A20T00')
         loads[2].wait()
         scores(1)
         column_sums(0)
@@ -389,6 +383,7 @@
         row_sums(0, rows)
         remote(stage.at[0, :, :rows], stage.at[0, :, rows:], x_ssem.at[2], x_rsem.at[2], partner)
         remote(z2, y2, x_ssem.at[1], x_rsem.at[1], partner)
+        gc.run('A10sA11A12A13A20T00')
         gc.run('a10B10a11B11a12B12a13B13A21A23T10T30')
         gc.run('a20B20T01T03b10b11b12b13A22T20')
         gc.run('a21B21T11T13a23B23T31T33')
@@ -397,6 +392,10 @@
         row_scores(0, blocks)
         env.arrived(dall.at[:, :rows], x_rsem.at[3])
         env.arrived(vall, x_rsem.at[4])
+        gc.all_sent()
+        for i, ref in enumerate((z1, z2, stage.at[0, :, :rows])):
+            env.sent(ref, x_ssem.at[i])
+        env.sent(cfull, t_ssem.at[0])
         env.drain()
 
     tile = pl.multiple_of(lax.div(me * mine, LANES) * LANES, LANES)
@@ -430,13 +429,15 @@
     own = pltpu.make_async_copy(dz, gfull.at[pos[2], pos[1], pos[0]], o_sem.at[0])
     own.start()
     gg.s1_send(dz)
+    own.wait()
+    gg.run('A10')
     spread(vall[pos[2], pos[1], pos[0]])
     dacc[...] = jnp.zeros((cols, cols), F32)
 
     def out_copy(view, i):
         n0 = pl.multiple_of(i * cols, cols)
         return pltpu.make_async_copy(cst.at[view, pl.ds(n0, cols), :], (code1, code2)[view].at[pl.ds(n0, cols), :],
-                                     o_sem.at[2 + view * chunks + i])
+                                     o_sem.at[2 + view])
 
     def columns(i):
         def body(i, _):
@@ -468,16 +469,14 @@
     def loss_send(st):
         ref = lossb.at[st, pos[st]]
         for d in DISTS:
-            i = st * AXES + d - 1
-            remote(ref, ref, l_ssem.at[i], l_rsem.at[i], env.peer(st, d))
+            remote(ref, ref, l_ssem.at[st], l_rsem.at[st], env.peer(st, d))
+        env.sent(lossb.at[st, :LINE - 1], l_ssem.at[st])
 
     def loss_recv(st):
-        for d in DISTS:
-            env.arrived(lossb.at[st, env.p(st, LINE - d)], l_rsem.at[st * AXES + d - 1])
+        env.arrived(lossb.at[st, :LINE - 1], l_rsem.at[st])
         return (lossb[st, 0] + lossb[st, 1]) + (lossb[st, 2] + lossb[st, 3])
 
-    own.wait()
-    gg.run('sA10A11A12A13')
+    gg.run('sA11A12A13')
     loss_send(0)
     gg.run('A20')
     columns(0)
@@ -492,8 +491,8 @@
     gg.run('a21B21a23B23')
     columns(3)
     losst[0] = loss_recv(2)
-    lcp = remote(losst.at[0], losst.at[1], l_ssem.at[9], l_rsem.at[9], partner)
-    dcp = remote(dacc, drecv, l_ssem.at[10], l_rsem.at[10], partner)
+    lcp = remote(losst.at[0], losst.at[1], l_ssem.at[3], l_rsem.at[3], partner)
+    dcp = remote(dacc, drecv, l_ssem.at[4], l_rsem.at[4], partner)
     gg.run('a22B22')
     lcp.wait_recv()
     loss_out[...] = jnp.sum(losst[0] + losst[1], keepdims=True) * (-1.0 / (2 * total_rows))
@@ -503,10 +502,24 @@
     gpc.start()
     gg.run('b20b21b23b22')
     gpc.wait()
-    for view in range(2):
-        for i in range(chunks):
-            out_copy(view, i).wait()
+    for view, out in enumerate((code1, code2)):
+        pltpu.make_async_copy(cst.at[view], out, o_sem.at[2 + view]).wait()
+    gg.all_sent()
+    env.sent(losst.at[0], l_ssem.at[3])
+    env.sent(dacc, l_ssem.at[4])
     env.drain()
+
+    @pl.when(core == 1)
+    def _():
+        for it in range(ITERS):
+            for st in range(AXES):
+                buf = first if it == 0 else later.at[it - 1]
+                env.sent(buf.at[st, :LINE - 1], s_ssem.at[it * AXES + st])
+        for st in range(AXES):
+            env.sent(v_some(st), v_ssem.at[st])
+        env.sent(dall.at[:, rows:], x_ssem.at[3])
+        env.sent(vall, x_ssem.at[4])
+        env.drain()
 
 
 def solution(mesh):
@@ -522,7 +535,7 @@
         vm = pl.BlockSpec(memory_space=pltpu.VMEM)
         hbm = pl.BlockSpec(memory_space=pltpu.HBM)
         free = pl.BlockSpec(memory_space=pl.ANY)
-        nsem = ITERS * AXES * AXES * (LINE - 1)
+        nsem = ITERS * AXES
         dma = lambda n: pltpu.SemaphoreType.DMA((n,))
         grid3 = (LINE,) * AXES
         sds = jax.ShapeDtypeStruct
@@ -559,10 +572,10 @@
                 square, square,
                 pltpu.VMEM((2 * mine, dim), F32),
                 pltpu.VMEM((2, rows, cols), F32),
-                dma(4), dma(ITERS), dma(ITERS), dma(nsem), dma(nsem),
-                dma(AXES * AG_SEMS), dma(AXES * AG_SEMS), dma(48), dma(48),
-                dma(9), dma(9), dma(AXES * AG_SEMS), dma(AXES * AG_SEMS), dma(11), dma(11),
-                dma(5), dma(5), dma(2 + 2 * rows // cols),
+                dma(4), dma(1), dma(1), dma(nsem), dma(nsem),
+                dma(5), dma(AG_SEMS), dma(1), dma(1),
+                dma(AXES), dma(AXES), dma(5), dma(AG_SEMS), dma(5), dma(5),
+                dma(5), dma(5), dma(4),
             ],
             compiler_params=pltpu.CompilerParams(collective_id=0, has_side_effects=True,
                                                  vmem_limit_bytes=44 * 2 ** 20),

time: 86.6 us -> 80.2 us (0.926)
  Pallas kernels: 84.1 us -> 77.6 us
    pallas_call x1, Pallas kernels: 80.6 us -> 74.2 us  [local_step(): pl.pallas_call(functools.partial(step_kernel, total_rows, total_protos),...]
where the time goes in v4:
time: 80.2 us; the launch traced here: 80 us
  Pallas kernels  77.6 us (97%)
  between operations  2.41 us (3%)
    pallas_call x1, Pallas kernels, local_step(): pl.pallas_call(functools.partial(step_kernel, total_rows, total_protos),...  74.2 us
    pallas_call x1, Pallas kernels, local_step(): pl.pallas_call(functools.partial(write_kernel, mine), out_shape=(code, co...  3.46 us

profile of v4, /device:TPU:0, one launch (start us, length us, event | category | flops | bytes accessed | tf_op | source)
XLA Modules:
  0.0 80.0 jit_solution(7661266904195256423)
XLA Ops:
  0.6 74.2 %shard_map.82 = (f32[2048,256]{1,0:T(8,128)S(1)}, f32[2048,256]{1,0:T(8,128)S(1)}, f32[1,1]{1,0:T(1,128)}, f32[4,4,4,64,256]{4,3,2,1,0:T(8,128)S(1)}, f32[256,256]{1,0:T(8,128)S(1)}) custom-call(bf16[2048,256]{1,0:T(8,128)(2,1)} %z1h.1, bf16[2048,256]{1,0:T(8,128)(2,1)} %z2h.1, bf16[256,256]{1,0:T(8,128)(2,1)} %ch.1), custom_call_target="tpu_custom_call" | custom-call | tf_op jit(solution)/shard_map/pallas_call | solution.py:549
  74.8 3.5 %shard_map.83 = (f32[2048,256]{1,0:T(8,128)}, f32[2048,256]{1,0:T(8,128)}, f32[64,32,256]{2,1,0:T(8,128)}, f32[64,32,256]{2,1,0:T(8,128)}, f32[256,256]{1,0:T(8,128)}) custom-call(f32[2048,256]{1,0:T(8,128)S(1)} %get-tuple-element.16.code1, f32[2048,256]{1,0:T(8,128)S(1)} %get-tuple-element.17.code2, f32[64,64,256]{2,1,0:T(8,128)S(1)} %bitcast.4, ...), custom_call_target="tpu_custom_call" | custom-call | tf_op jit(solution)/shard_map/pallas_call | solution.py:584

commit v5 on v4

--- a/solution.py
+++ b/solution.py
@@ -136,6 +136,19 @@
             for d in (1, 3):
                 self.send(j, 2 * level - 1, 8 * level - 5 + k, ref, level, d)
 
+    def piece_send(self, *offsets):
+        for k in offsets:
+            for j in range(AXES):
+                ref = self.chunk(j, 1, k, 0)
+                for d in (1, 3):
+                    self.send(j, 3, 11, ref, 2, d)
+
+    def own_piece(self):
+        self.piece_send(0)
+
+    def other_pieces(self):
+        self.piece_send(1, 3, 2)
+
     def a_recv(self, level, k):
         self.recv(8 * level - 5 + k, 2 * LINE ** (level - 1))
 
@@ -160,7 +173,7 @@
         for op in re.findall('[a-zA-Z][0-9]*', ops):
             args = [int(c) for c in op[1:]]
             {'S': self.s1_send, 's': self.s1_recv, 'A': self.a_send, 'a': self.a_recv,
-             'B': self.b_send, 'b': self.b_recv, 'T': self.t_send, 'U': self.t_recv}[op[0]](*args)
+             'B': self.b_send, 'b': self.b_recv, 'T': self.t_send, 'P': self.own_piece, 'Q': self.other_pieces}[op[0]](*args)
 
 
 def write_kernel(mine, code1, code2, gfull, gp, o1, o2, g1, g2, og, sem):
@@ -188,7 +201,7 @@
     blocks = LINE ** AXES
     fscale = 1.0 / (2 * total_rows * TEMP_TAU)
     zs, ys = (z1, z2), (y1, y2)
-    chunks = rows // cols
+    chunks, groups = rows // cols, cols // 8
 
     barrier = pltpu.get_barrier_semaphore()
     pl.semaphore_signal(barrier, inc=1, device_id=partner, device_id_type=MESH)
@@ -212,17 +225,17 @@
             stage[0, 2 + view:3 + view, pl.ds(n0, cols)] = jnp.sum(f, axis=0, keepdims=True)
             e = f * f
             f_scr[view, :, pl.ds(n0, cols)] = f
-            e_scr[view, :, pl.ds(n0, cols)] = e
+            e_scr[view, :, :, pl.ds(n0, cols)] = e.reshape(groups, 8, cols)
             cacc[view] += e[:, :LANES] + e[:, LANES:]
             return 0
-        lax.fori_loop(0, chunks, body, 0, unroll=2)
+        lax.fori_loop(0, chunks, body, 0, unroll=4)
         zr[view * mine:(view + 1) * mine, :] = zs[view][pl.ds(pl.multiple_of(me * mine, mine), mine), :]
 
     def other_scores(view):
         def body(i, _):
             n0 = pl.multiple_of(i * cols, cols)
             f = jnp.exp(_nt(c_ref[...], ys[view][pl.ds(n0, cols), :]) * (1.0 / TEMP_TAU))
-            e_scr[view, :, pl.ds(rows + n0, cols)] = f * f
+            e_scr[view, :, :, pl.ds(rows + n0, cols)] = (f * f).reshape(groups, 8, cols)
             return 0
         lax.fori_loop(0, chunks, body, 0, unroll=2)
 
@@ -233,7 +246,7 @@
             lrow[q] = l
             frow[q] = jnp.exp(l)
             return 0
-        lax.fori_loop(lo, hi, body, 0, unroll=2)
+        lax.fori_loop(lo, hi, body, 0, unroll=4)
 
     def block(q):
         return lax.div(q, LINE * LINE), lax.rem(lax.div(q, LINE), LINE), lax.rem(q, LINE)
@@ -258,34 +271,28 @@
         return csend[0] + crecv[0]
 
     def row_sums(it, width):
-        wide = 8
-        step = wide * LANES
+        tiles = [slice(l, l + LANES) for l in range(0, width, LANES)]
         for view in range(2):
-            def body(j, _, view=view):
-                acc = [jnp.zeros((8, LANES), F32) for _ in range(wide)]
-                offs = [pl.multiple_of(j * step + t * LANES, LANES) for t in range(wide)]
-                for g in range(0, cols, 8):
-                    w = vb[view, g:g + 8, :]
-                    for t, l0 in enumerate(offs):
-                        acc[t] = acc[t] + e_scr[view, g:g + 8, pl.ds(l0, LANES)] * w
-                for t, l0 in enumerate(offs):
-                    stage[it, view:view + 1, pl.ds(l0, LANES)] = jnp.sum(acc[t], axis=0, keepdims=True)
+            def body(g, acc, view=view):
+                w = vb[view, pl.ds(pl.multiple_of(g * 8, 8), 8), :]
+                return tuple(a + e_scr[view, g, :, ls] * w for a, ls in zip(acc, tiles))
+            acc = lax.fori_loop(0, groups, body, tuple(jnp.zeros((8, LANES), F32) for _ in tiles), unroll=4)
+            for a, ls in zip(acc, tiles):
+                stage[it, view:view + 1, ls] = jnp.sum(a, axis=0, keepdims=True)
+
+    def weighted_columns():
+        tiles = [slice(l, l + LANES) for l in range(0, 2 * rows, LANES)]
+        for view in range(2):
+            us = [ub[view, :, ls] for ls in tiles]
+
+            def body(g, _, view=view, us=us):
+                acc = [None] * 4
+                for t, ls in enumerate(tiles):
+                    x = e_scr[view, g, :, ls] * us[t]
+                    acc[t % 4] = x if acc[t % 4] is None else acc[t % 4] + x
+                cacc[view, pl.ds(pl.multiple_of(g * 8, 8), 8), :] = (acc[0] + acc[1]) + (acc[2] + acc[3])
                 return 0
-            lax.fori_loop(0, width // step, body, 0)
-
-    def weighted_columns():
-        for view in range(2):
-            def body(g, _, view=view):
-                for gi in range(2):
-                    k0 = pl.multiple_of(g * 16 + gi * 8, 8)
-                    acc = [None] * 4
-                    for t in range(2 * rows // LANES):
-                        ls = slice(t * LANES, (t + 1) * LANES)
-                        x = e_scr[view, pl.ds(k0, 8), ls] * ub[view, :, ls]
-                        acc[t % 4] = x if acc[t % 4] is None else acc[t % 4] + x
-                    cacc[view, pl.ds(k0, 8), :] = (acc[0] + acc[1]) + (acc[2] + acc[3])
-                return 0
-            lax.fori_loop(0, cols // 16, body, 0)
+            lax.fori_loop(0, groups, body, 0, unroll=4)
 
     def vsend(st):
         ref = vall.at[(pos[2], pos[1], pos[0])[:AXES - st]]
@@ -299,16 +306,16 @@
         env.arrived(v_some(st), v_rsem.at[st])
 
     def hidden(slot):
-        if slot in (0, 1):
-            env.arrived(ys[slot], x_rsem.at[slot])
-            other_scores(slot)
+        if slot in (1, 2):
+            env.arrived(ys[slot - 1], x_rsem.at[slot - 1])
+            other_scores(slot - 1)
         elif slot == 6:
             gc.t_recv()
             row_scores(0, 20)
         elif slot == 7:
-            row_scores(20, 42)
+            row_scores(20, 44)
         elif slot == 8:
-            row_scores(42, blocks)
+            row_scores(44, blocks)
 
     @pl.when(core == 1)
     def _():
@@ -369,12 +376,11 @@
     def _():
         loads[3].start()
         loads[0].wait()
+        loads[1].wait()
+        scores(0)
         loads[3].wait()
         pl.semaphore_wait(barrier, 1 + AXES * (LINE - 1))
-        gc.run('S')
-        loads[1].wait()
-        remote(z1, y1, x_ssem.at[0], x_rsem.at[0], partner)
-        scores(0)
+        gc.run('SA10P')
         loads[2].wait()
         scores(1)
         column_sums(0)
@@ -382,13 +388,13 @@
         spread(vrow)
         row_sums(0, rows)
         remote(stage.at[0, :, :rows], stage.at[0, :, rows:], x_ssem.at[2], x_rsem.at[2], partner)
-        remote(z2, y2, x_ssem.at[1], x_rsem.at[1], partner)
-        gc.run('A10sA11A12A13A20T00')
-        gc.run('a10B10a11B11a12B12a13B13A21A23T10T30')
-        gc.run('a20B20T01T03b10b11b12b13A22T20')
-        gc.run('a21B21T11T13a23B23T31T33')
-        gc.run('b20T02b21T12b23T32')
-        gc.run('a22B22T21T23b22T22')
+        for i in range(2):
+            remote(zs[i], ys[i], x_ssem.at[i], x_rsem.at[i], partner)
+        gc.run('sA11A13A12QT00')
+        gc.run('a10B10a11B11a13B13a12B12A21A23')
+        gc.run('a20B20b10b11b13b12A22T10T30T20')
+        gc.run('a21B21a23B23T01T03T11T13T31T33')
+        gc.run('a22B22T21T23b20T02b21T12b23T32b22T22')
         row_scores(0, blocks)
         env.arrived(dall.at[:, :rows], x_rsem.at[3])
         env.arrived(vall, x_rsem.at[4])
@@ -424,13 +430,13 @@
         cl = cfull[lax.div(i, LINE), lax.rem(i, LINE)].reshape(LINE * cols, cols)
         return acc + _nn(jnp.concatenate(hs, axis=1), cl)
 
-    dz[...] = lax.fori_loop(0, LINE * LINE, dzbody, jnp.zeros((2 * mine, cols), F32), unroll=2)
+    dz[...] = lax.fori_loop(0, LINE * LINE, dzbody, jnp.zeros((2 * mine, cols), F32), unroll=4)
 
     own = pltpu.make_async_copy(dz, gfull.at[pos[2], pos[1], pos[0]], o_sem.at[0])
     own.start()
     gg.s1_send(dz)
     own.wait()
-    gg.run('A10')
+    gg.run('A10P')
     spread(vall[pos[2], pos[1], pos[0]])
     dacc[...] = jnp.zeros((cols, cols), F32)
 
@@ -446,7 +452,7 @@
             code, prob = [], []
             for view in range(2):
                 w = jnp.concatenate([vb[view], vb[view]], axis=1)
-                code.append(e_scr[view, :, pl.ds(n0, cols)] * w * inv[view:view + 1, :])
+                code.append(e_scr[view, :, :, pl.ds(n0, cols)].reshape(cols, cols) * w * inv[view:view + 1, :])
                 prob.append(f_scr[view, :, pl.ds(n0, cols)] * inv[2 + view:3 + view, :])
             for view in range(2):
                 h = ((prob[view] - code[1 - view]) * fscale).astype(BF16)
@@ -454,7 +460,7 @@
                 cst[view, pl.ds(n0, cols), :] = code[view].T
                 out_copy(view, i).start()
             return 0
-        lax.fori_loop(i * 2, i * 2 + 2, body, 0)
+        lax.fori_loop(i * 2, i * 2 + 2, body, 0, unroll=True)
 
     def lbody(q, acc):
         for h in range(2):
@@ -463,7 +469,7 @@
             other = jnp.concatenate([code[mine:], code[:mine]], axis=0)
             acc = acc + other * lp
         return acc
-    part = lax.fori_loop(0, blocks, lbody, jnp.zeros((2 * mine, LANES), F32), unroll=2)
+    part = lax.fori_loop(0, blocks, lbody, jnp.zeros((2 * mine, LANES), F32), unroll=4)
     lossb[0, pos[0]] = jnp.sum(part.reshape(2 * mine // 8, 8, LANES), axis=0)
 
     def loss_send(st):
@@ -476,15 +482,14 @@
         env.arrived(lossb.at[st, :LINE - 1], l_rsem.at[st])
         return (lossb[st, 0] + lossb[st, 1]) + (lossb[st, 2] + lossb[st, 3])
 
-    gg.run('sA11A12A13')
+    gg.run('sA11A13A12Q')
     loss_send(0)
-    gg.run('A20')
     columns(0)
-    gg.run('a10B10a11B11a12B12a13B13A21A23')
+    gg.run('a10B10a11B11a13B13a12B12A21A23')
     lossb[1, pos[1]] = loss_recv(0)
     loss_send(1)
     columns(1)
-    gg.run('b10b11b12b13A22a20B20')
+    gg.run('a20B20b10b11b13b12A22')
     lossb[2, pos[2]] = loss_recv(1)
     loss_send(2)
     columns(2)
@@ -555,7 +560,7 @@
             scratch_shapes=[
                 zbuf, zbuf, zbuf, zbuf, pltpu.VMEM((cols, dim), BF16),
                 pltpu.VMEM((2, cols, rows), F32),
-                pltpu.VMEM((2, cols, 2 * rows), F32),
+                pltpu.VMEM((2, cols // 8, 8, total_rows), F32),
                 pltpu.VMEM(grid3 + (cols, dim), BF16),
                 rowbuf, rowbuf,
                 pltpu.VMEM(grid3 + (4, LANES), F32),

time: 80.2 us -> 75.7 us (0.944)
  Pallas kernels: 77.6 us -> 73.1 us
    pallas_call x1, Pallas kernels: 74.2 us -> 69.7 us  [local_step(): pl.pallas_call(functools.partial(step_kernel, total_rows, total_protos),...]
where the time goes in v5:
time: 75.7 us; the launch traced here: 75.5 us
  Pallas kernels  73.1 us (97%)
  between operations  2.41 us (3%)
    pallas_call x1, Pallas kernels, local_step(): pl.pallas_call(functools.partial(step_kernel, total_rows, total_protos),...  69.7 us
    pallas_call x1, Pallas kernels, local_step(): pl.pallas_call(functools.partial(write_kernel, mine), out_shape=(code, co...  3.46 us

profile of v5, /device:TPU:0, one launch (start us, length us, event | category | flops | bytes accessed | tf_op | source)
XLA Modules:
  0.0 75.5 jit_solution(2827999530024807546)
XLA Ops:
  0.6 69.7 %shard_map.82 = (f32[2048,256]{1,0:T(8,128)S(1)}, f32[2048,256]{1,0:T(8,128)S(1)}, f32[1,1]{1,0:T(1,128)}, f32[4,4,4,64,256]{4,3,2,1,0:T(8,128)S(1)}, f32[256,256]{1,0:T(8,128)S(1)}) custom-call(bf16[2048,256]{1,0:T(8,128)(2,1)} %z1h.1, bf16[2048,256]{1,0:T(8,128)(2,1)} %z2h.1, bf16[256,256]{1,0:T(8,128)(2,1)} %ch.1), custom_call_target="tpu_custom_call" | custom-call | tf_op jit(solution)/shard_map/pallas_call | solution.py:554
  70.3 3.5 %shard_map.83 = (f32[2048,256]{1,0:T(8,128)}, f32[2048,256]{1,0:T(8,128)}, f32[64,32,256]{2,1,0:T(8,128)}, f32[64,32,256]{2,1,0:T(8,128)}, f32[256,256]{1,0:T(8,128)}) custom-call(f32[2048,256]{1,0:T(8,128)S(1)} %get-tuple-element.16.code1, f32[2048,256]{1,0:T(8,128)S(1)} %get-tuple-element.17.code2, f32[64,64,256]{2,1,0:T(8,128)S(1)} %bitcast.4, ...), custom_call_target="tpu_custom_call" | custom-call | tf_op jit(solution)/shard_map/pallas_call | solution.py:589

commit v6 on v5

--- a/solution.py
+++ b/solution.py
@@ -20,7 +20,7 @@
 SUM_CUTS = (0, 1408, 2816, 4096)
 C_CUTS = (0, 80, 160, 256)
 G_CUTS = (0, 24, 48, 64)
-AG_SEMS = 19
+AG_SEMS = 27
 DISTS = (2, 1, 3)
 
 
@@ -130,18 +130,30 @@
             return self.at(j, self.p(j, 0, k), self.p(j, 1, m), self.p(j, 2, 0))
         return self.at(j, None, self.p(j, 1, k), self.p(j, 2, m))
 
+    def slot(self, level, k, d):
+        return 12 * level - 9 + k + LINE * (d // 2)
+
     def a_send(self, level, k):
         for j in range(AXES):
             ref = self.chunk(j, level, k, 0)
             for d in (1, 3):
-                self.send(j, 2 * level - 1, 8 * level - 5 + k, ref, level, d)
+                self.send(j, 2 * level - 1, self.slot(level, k, d), ref, level, d)
+
+    def way(self, k):
+        return 1 if k < 2 else 3
+
+    def f_recv(self, level, k):
+        self.recv(self.slot(level, k, self.way(k)), LINE ** (level - 1))
+
+    def g_recv(self, level, k):
+        self.recv(self.slot(level, k, LINE - self.way(k)), LINE ** (level - 1))
 
     def piece_send(self, *offsets):
         for k in offsets:
             for j in range(AXES):
                 ref = self.chunk(j, 1, k, 0)
                 for d in (1, 3):
-                    self.send(j, 3, 11, ref, 2, d)
+                    self.send(j, 3, self.slot(2, 0, d), ref, 2, d)
 
     def own_piece(self):
         self.piece_send(0)
@@ -149,16 +161,13 @@
     def other_pieces(self):
         self.piece_send(1, 3, 2)
 
-    def a_recv(self, level, k):
-        self.recv(8 * level - 5 + k, 2 * LINE ** (level - 1))
-
     def b_send(self, level, k):
-        d = 1 if k < 2 else 3
+        d = self.way(k)
         for j in range(AXES):
-            self.send(j, 2 * level, 8 * level - 1 + k, self.chunk(j, level, k, LINE - d), level, d)
+            self.send(j, 2 * level, self.slot(level, k, 5), self.chunk(j, level, k, LINE - d), level, d)
 
     def b_recv(self, level, k):
-        self.recv(8 * level - 1 + k, LINE ** (level - 1))
+        self.recv(self.slot(level, k, 5), LINE ** (level - 1))
 
     def t_send(self, k, m):
         ts, tr = self.twin
@@ -172,7 +181,7 @@
     def run(self, ops):
         for op in re.findall('[a-zA-Z][0-9]*', ops):
             args = [int(c) for c in op[1:]]
-            {'S': self.s1_send, 's': self.s1_recv, 'A': self.a_send, 'a': self.a_recv,
+            {'S': self.s1_send, 's': self.s1_recv, 'A': self.a_send, 'f': self.f_recv, 'g': self.g_recv,
              'B': self.b_send, 'b': self.b_recv, 'T': self.t_send, 'P': self.own_piece, 'Q': self.other_pieces}[op[0]](*args)
 
 
@@ -190,7 +199,7 @@
 def step_kernel(total_rows, total_protos, z1h, z2h, ch,
                 code1, code2, loss_out, gfull, gp_out,
                 z1, z2, y1, y2, c_ref, f_scr, e_scr, cfull, lrow, frow, vall, zr, dall,
-                cacc, vb, ub, stage, csend, crecv, first, later, lossb, losst, dacc, drecv, dz, cst,
+                cacc, vb, ub, stage, csend, crecv, sums, lossb, losst, dacc, drecv, dz, cst,
                 lsem, c_ssem, c_rsem, s_ssem, s_rsem, a_ssem, a_rsem, t_ssem, t_rsem,
                 v_ssem, v_rsem, g_ssem, g_rsem, l_ssem, l_rsem, x_ssem, x_rsem, o_sem):
     env = _Env()
@@ -228,7 +237,7 @@
             e_scr[view, :, :, pl.ds(n0, cols)] = e.reshape(groups, 8, cols)
             cacc[view] += e[:, :LANES] + e[:, LANES:]
             return 0
-        lax.fori_loop(0, chunks, body, 0, unroll=4)
+        lax.fori_loop(0, chunks, body, 0, unroll=8)
         zr[view * mine:(view + 1) * mine, :] = zs[view][pl.ds(pl.multiple_of(me * mine, mine), mine), :]
 
     def other_scores(view):
@@ -266,9 +275,7 @@
                     _row_to_col(vrow[k:k + 1, :]), (LANES, LANES))
 
     def exchange():
-        cp = remote(csend.at[0], crecv.at[0], c_ssem.at[0], c_rsem.at[0], partner)
-        cp.wait()
-        return csend[0] + crecv[0]
+        return remote(csend.at[0], crecv.at[0], c_ssem.at[0], c_rsem.at[0], partner)
 
     def row_sums(it, width):
         tiles = [slice(l, l + LANES) for l in range(0, width, LANES)]
@@ -305,17 +312,50 @@
     def vrecv(st):
         env.arrived(v_some(st), v_rsem.at[st])
 
+    def load_sums(it, value):
+        for j, (l0, l1) in enumerate(_parts(SUM_CUTS)):
+            sums[it, 0, pos[j], :, l0:l1] = value[:, l0:l1]
+
+    def send_sums(it, st):
+        for d in DISTS:
+            for j, (l0, l1) in enumerate(_parts(SUM_CUTS)):
+                ax = (st + j) % AXES
+                src = sums.at[it, st, pos[ax], :, l0:l1]
+                remote(src, src, s_ssem.at[it * AXES + st], s_rsem.at[it * AXES + st], env.peer(ax, d))
+
+    def recv_sums(it, st):
+        env.arrived(sums.at[it, st, :LINE - 1], s_rsem.at[it * AXES + st])
+        tot = []
+        for j, (l0, l1) in enumerate(_parts(SUM_CUTS)):
+            s = [sums[it, st, i, :, l0:l1] for i in range(LINE)]
+            t = (s[0] + s[1]) + (s[2] + s[3])
+            tot.append(t)
+            if st < AXES - 1:
+                sums[it, st + 1, pos[(st + 1 + j) % AXES], :, l0:l1] = t
+        return tot
+
+    def denominators(st):
+        if st == 0:
+            load_sums(ITERS, stage[0, 2:4])
+        else:
+            tot = recv_sums(ITERS, st - 1)
+        if st < AXES:
+            send_sums(ITERS, st)
+            return
+        for (l0, l1), t in zip(_parts(SUM_CUTS), tot):
+            dall[2:4, l0:l1] = t
+
     def hidden(slot):
         if slot in (1, 2):
             env.arrived(ys[slot - 1], x_rsem.at[slot - 1])
             other_scores(slot - 1)
-        elif slot == 6:
+        elif slot == 7:
             gc.t_recv()
-            row_scores(0, 20)
-        elif slot == 7:
-            row_scores(20, 44)
+            row_scores(0, blocks // 2)
         elif slot == 8:
-            row_scores(44, blocks)
+            row_scores(blocks // 2, blocks)
+        if slot in (3, 4, 5, 6):
+            denominators(slot - 3)
 
     @pl.when(core == 1)
     def _():
@@ -325,7 +365,8 @@
             scores(view)
         pl.semaphore_wait(barrier, 1 + AXES * (LINE - 1))
         column_sums(0)
-        total = exchange()
+        exchange().wait()
+        total = csend[0] + crecv[0]
         for it in range(ITERS):
             last = it == ITERS - 1
             vrow = 1.0 / (float(total_protos) * total)
@@ -334,35 +375,24 @@
                 vsend(0)
             spread(vrow)
             row_sums(it, rows if it == 0 else 2 * rows)
-            buf = first if it == 0 else later.at[it - 1]
             if it == 0:
                 env.arrived(stage.at[0, :, rows:], x_rsem.at[2])
-            for j, (l0, l1) in enumerate(_parts(SUM_CUTS)):
-                buf[0, pos[j], :, l0:l1] = stage[it, :buf.shape[2], l0:l1]
+            load_sums(it, stage[it, 0:2])
             for st in range(AXES):
-                i = it * AXES + st
-                for d in DISTS:
-                    for j, (l0, l1) in enumerate(_parts(SUM_CUTS)):
-                        ax = (st + j) % AXES
-                        src = buf.at[st, pos[ax], :, l0:l1]
-                        remote(src, src, s_ssem.at[i], s_rsem.at[i], env.peer(ax, d))
-                hidden(i)
+                send_sums(it, st)
+                hidden(it * AXES + st)
                 if last:
                     vrecv(st)
                     if st < AXES - 1:
                         vsend(st + 1)
-                env.arrived(buf.at[st, :LINE - 1], s_rsem.at[i])
-                for j, (l0, l1) in enumerate(_parts(SUM_CUTS)):
-                    tot = (buf[st, 0, :, l0:l1] + buf[st, 1, :, l0:l1]) + (buf[st, 2, :, l0:l1] + buf[st, 3, :, l0:l1])
-                    if st < AXES - 1:
-                        buf[st + 1, pos[(st + 1 + j) % AXES], :, l0:l1] = tot
-                        continue
-                    if it == 0:
-                        dall[2:4, l0:l1] = tot[2:4]
+                tot = recv_sums(it, st)
+                if st < AXES - 1:
+                    continue
+                for (l0, l1), t in zip(_parts(SUM_CUTS), tot):
                     if last:
-                        dall[0:2, l0:l1] = tot
+                        dall[0:2, l0:l1] = t
                     else:
-                        u = 1.0 / (float(total_rows) * tot)
+                        u = 1.0 / (float(total_rows) * t)
                         for view in range(2):
                             ub[view, :, l0:l1] = jnp.broadcast_to(u[view:view + 1], (8, l1 - l0))
             if not last:
@@ -376,25 +406,26 @@
     def _():
         loads[3].start()
         loads[0].wait()
-        loads[1].wait()
-        scores(0)
+        for view in range(2):
+            loads[1 + view].wait()
+            scores(view)
+        column_sums(0)
         loads[3].wait()
         pl.semaphore_wait(barrier, 1 + AXES * (LINE - 1))
+        cp = exchange()
         gc.run('SA10P')
-        loads[2].wait()
-        scores(1)
-        column_sums(0)
-        vrow = 1.0 / (float(total_protos) * exchange())
+        cp.wait()
+        vrow = 1.0 / (float(total_protos) * (csend[0] + crecv[0]))
         spread(vrow)
         row_sums(0, rows)
         remote(stage.at[0, :, :rows], stage.at[0, :, rows:], x_ssem.at[2], x_rsem.at[2], partner)
         for i in range(2):
             remote(zs[i], ys[i], x_ssem.at[i], x_rsem.at[i], partner)
         gc.run('sA11A13A12QT00')
-        gc.run('a10B10a11B11a13B13a12B12A21A23')
-        gc.run('a20B20b10b11b13b12A22T10T30T20')
-        gc.run('a21B21a23B23T01T03T11T13T31T33')
-        gc.run('a22B22T21T23b20T02b21T12b23T32b22T22')
+        gc.run('f10B10f11B11f13B13f12B12g10g11A21g13g12A23')
+        gc.run('f20B20b10b11b13b12A22T10T30T20')
+        gc.run('f21B21f23B23g20g21g23T01T03T11T13T31T33')
+        gc.run('f22B22g22T21T23b20T02b21T12b23T32b22T22')
         row_scores(0, blocks)
         env.arrived(dall.at[:, :rows], x_rsem.at[3])
         env.arrived(vall, x_rsem.at[4])
@@ -485,27 +516,27 @@
     gg.run('sA11A13A12Q')
     loss_send(0)
     columns(0)
-    gg.run('a10B10a11B11a13B13a12B12A21A23')
+    gg.run('f10B10f11B11f13B13f12B12g10g11A21g13g12A23')
     lossb[1, pos[1]] = loss_recv(0)
     loss_send(1)
     columns(1)
-    gg.run('a20B20b10b11b13b12A22')
+    gg.run('f20B20b10b11b13b12A22')
     lossb[2, pos[2]] = loss_recv(1)
     loss_send(2)
     columns(2)
-    gg.run('a21B21a23B23')
+    gg.run('f21B21f23B23')
     columns(3)
     losst[0] = loss_recv(2)
     lcp = remote(losst.at[0], losst.at[1], l_ssem.at[3], l_rsem.at[3], partner)
     dcp = remote(dacc, drecv, l_ssem.at[4], l_rsem.at[4], partner)
-    gg.run('a22B22')
+    gg.run('f22B22')
     lcp.wait_recv()
     loss_out[...] = jnp.sum(losst[0] + losst[1], keepdims=True) * (-1.0 / (2 * total_rows))
     dcp.wait_recv()
     drecv[...] = dacc[...] + drecv[...]
     gpc = pltpu.make_async_copy(drecv, gp_out, o_sem.at[1])
     gpc.start()
-    gg.run('b20b21b23b22')
+    gg.run('g20g21g23g22b20b21b23b22')
     gpc.wait()
     for view, out in enumerate((code1, code2)):
         pltpu.make_async_copy(cst.at[view], out, o_sem.at[2 + view]).wait()
@@ -516,10 +547,9 @@
 
     @pl.when(core == 1)
     def _():
-        for it in range(ITERS):
+        for it in range(ITERS + 1):
             for st in range(AXES):
-                buf = first if it == 0 else later.at[it - 1]
-                env.sent(buf.at[st, :LINE - 1], s_ssem.at[it * AXES + st])
+                env.sent(sums.at[it, st, :LINE - 1], s_ssem.at[it * AXES + st])
         for st in range(AXES):
             env.sent(v_some(st), v_ssem.at[st])
         env.sent(dall.at[:, rows:], x_ssem.at[3])
@@ -540,7 +570,7 @@
         vm = pl.BlockSpec(memory_space=pltpu.VMEM)
         hbm = pl.BlockSpec(memory_space=pltpu.HBM)
         free = pl.BlockSpec(memory_space=pl.ANY)
-        nsem = ITERS * AXES
+        nsem = (ITERS + 1) * AXES
         dma = lambda n: pltpu.SemaphoreType.DMA((n,))
         grid3 = (LINE,) * AXES
         sds = jax.ShapeDtypeStruct
@@ -570,8 +600,7 @@
                 pltpu.VMEM((2, 8, total_rows), F32),
                 pltpu.VMEM((ITERS, 4, total_rows), F32),
                 small, small,
-                pltpu.VMEM((AXES, LINE, 4, total_rows), F32),
-                pltpu.VMEM((ITERS - 1, AXES, LINE, 2, total_rows), F32),
+                pltpu.VMEM((ITERS + 1, AXES, LINE, 2, total_rows), F32),
                 pltpu.VMEM((AXES, LINE, 8, LANES), F32),
                 pltpu.VMEM((2, 8, LANES), F32),
                 square, square,

time: 75.7 us -> 73.9 us (0.976)
  Pallas kernels: 73.1 us -> 71.3 us
    pallas_call x1, Pallas kernels: 69.7 us -> 67.9 us  [local_step(): pl.pallas_call(functools.partial(step_kernel, total_rows, total_protos),...]
where the time goes in v6:
time: 73.9 us; the launch traced here: 73.7 us
  Pallas kernels  71.3 us (96%)
  between operations  2.41 us (3%)
    pallas_call x1, Pallas kernels, local_step(): pl.pallas_call(functools.partial(step_kernel, total_rows, total_protos),...  67.9 us
    pallas_call x1, Pallas kernels, local_step(): pl.pallas_call(functools.partial(write_kernel, mine), out_shape=(code, co...  3.46 us

profile of v6, /device:TPU:0, one launch (start us, length us, event | category | flops | bytes accessed | tf_op | source)
XLA Modules:
  0.0 73.7 jit_solution(13527196012090698385)
XLA Ops:
  0.6 67.9 %shard_map.82 = (f32[2048,256]{1,0:T(8,128)S(1)}, f32[2048,256]{1,0:T(8,128)S(1)}, f32[1,1]{1,0:T(1,128)}, f32[4,4,4,64,256]{4,3,2,1,0:T(8,128)S(1)}, f32[256,256]{1,0:T(8,128)S(1)}) custom-call(bf16[2048,256]{1,0:T(8,128)(2,1)} %z1h.1, bf16[2048,256]{1,0:T(8,128)(2,1)} %z2h.1, bf16[256,256]{1,0:T(8,128)(2,1)} %ch.1), custom_call_target="tpu_custom_call" | custom-call | tf_op jit(solution)/shard_map/pallas_call | solution.py:584
  68.5 3.5 %shard_map.83 = (f32[2048,256]{1,0:T(8,128)}, f32[2048,256]{1,0:T(8,128)}, f32[64,32,256]{2,1,0:T(8,128)}, f32[64,32,256]{2,1,0:T(8,128)}, f32[256,256]{1,0:T(8,128)}) custom-call(f32[2048,256]{1,0:T(8,128)S(1)} %get-tuple-element.16.code1, f32[2048,256]{1,0:T(8,128)S(1)} %get-tuple-element.17.code2, f32[64,64,256]{2,1,0:T(8,128)S(1)} %bitcast.4, ...), custom_call_target="tpu_custom_call" | custom-call | tf_op jit(solution)/shard_map/pallas_call | solution.py:618

commit v7 on v6

--- a/solution.py
+++ b/solution.py
@@ -19,7 +19,7 @@
 LANES = 128
 SUM_CUTS = (0, 1408, 2816, 4096)
 C_CUTS = (0, 80, 160, 256)
-G_CUTS = (0, 24, 48, 64)
+G_CUTS = ((0, 40, 88, 128), (0, 40, 80, 128))
 AG_SEMS = 27
 DISTS = (2, 1, 3)
 
@@ -186,9 +186,14 @@
 
 
 def write_kernel(mine, code1, code2, gfull, gp, o1, o2, g1, g2, og, sem):
-    pairs = [(code1, o1), (code2, o2), (gp, og)]
-    for view, out in enumerate((g1, g2)):
-        pairs.append((gfull.at[:, view * mine:(view + 1) * mine, :], out))
+    half = code1.shape[0] // 2
+    pairs = [(gp, og)]
+    for h in range(2):
+        for src, dst in ((code1, o1), (code2, o2)):
+            pairs.append((src.at[h * half:(h + 1) * half, :], dst.at[h * half:(h + 1) * half, :]))
+        for view, dst in enumerate((g1, g2)):
+            r = (2 * h + view) * mine
+            pairs.append((gfull.at[:, r:r + mine, :], dst.at[:, :, h * LANES:(h + 1) * LANES]))
     copies = [pltpu.make_async_copy(src, dst, sem.at[i]) for i, (src, dst) in enumerate(pairs)]
     for cp in copies:
         cp.start()
@@ -201,7 +206,7 @@
                 z1, z2, y1, y2, c_ref, f_scr, e_scr, cfull, lrow, frow, vall, zr, dall,
                 cacc, vb, ub, stage, csend, crecv, sums, lossb, losst, dacc, drecv, dz, cst,
                 lsem, c_ssem, c_rsem, s_ssem, s_rsem, a_ssem, a_rsem, t_ssem, t_rsem,
-                v_ssem, v_rsem, g_ssem, g_rsem, l_ssem, l_rsem, x_ssem, x_rsem, o_sem):
+                v_ssem, v_rsem, l_ssem, l_rsem, x_ssem, x_rsem, o_sem):
     env = _Env()
     me, core, pos, partner = env.me, env.core, env.pos, env.partner
     remote = env.remote
@@ -220,7 +225,15 @@
     loads = [pltpu.make_async_copy(src, dst, lsem.at[i]) for i, (src, dst) in enumerate(
         ((ch, c_ref), (z1h, z1), (z2h, z2), (ch, cfull.at[pos[2], pos[1], pos[0]])))]
     gc = _Gather(env, cfull, C_CUTS, a_ssem, a_rsem, (t_ssem, t_rsem))
-    gg = _Gather(env, gfull, G_CUTS, g_ssem, g_rsem)
+    gg = [_Gather(env, gfull, cuts, a_ssem, a_rsem) for cuts in G_CUTS]
+
+    def by_core(fn):
+        for c in range(2):
+            pl.when(core == c)(functools.partial(fn, c))
+
+    def grun(ops):
+        by_core(lambda c: gg[c].run(ops))
+
     for cp in loads[:3]:
         cp.start()
 
@@ -321,7 +334,7 @@
             for j, (l0, l1) in enumerate(_parts(SUM_CUTS)):
                 ax = (st + j) % AXES
                 src = sums.at[it, st, pos[ax], :, l0:l1]
-                remote(src, src, s_ssem.at[it * AXES + st], s_rsem.at[it * AXES + st], env.peer(ax, d))
+                remote(src, src, s_ssem.at[0], s_rsem.at[it * AXES + st], env.peer(ax, d))
 
     def recv_sums(it, st):
         env.arrived(sums.at[it, st, :LINE - 1], s_rsem.at[it * AXES + st])
@@ -461,13 +474,14 @@
         cl = cfull[lax.div(i, LINE), lax.rem(i, LINE)].reshape(LINE * cols, cols)
         return acc + _nn(jnp.concatenate(hs, axis=1), cl)
 
-    dz[...] = lax.fori_loop(0, LINE * LINE, dzbody, jnp.zeros((2 * mine, cols), F32), unroll=4)
+    rowgrad = lax.fori_loop(0, LINE * LINE, dzbody, jnp.zeros((2 * mine, cols), F32), unroll=4)
+    dz[...] = jnp.concatenate([rowgrad[:, :LANES], rowgrad[:, LANES:]], axis=0)
 
     own = pltpu.make_async_copy(dz, gfull.at[pos[2], pos[1], pos[0]], o_sem.at[0])
     own.start()
-    gg.s1_send(dz)
+    by_core(lambda c: gg[c].s1_send(dz))
     own.wait()
-    gg.run('A10P')
+    grun('A10P')
     spread(vall[pos[2], pos[1], pos[0]])
     dacc[...] = jnp.zeros((cols, cols), F32)
 
@@ -513,43 +527,41 @@
         env.arrived(lossb.at[st, :LINE - 1], l_rsem.at[st])
         return (lossb[st, 0] + lossb[st, 1]) + (lossb[st, 2] + lossb[st, 3])
 
-    gg.run('sA11A13A12Q')
     loss_send(0)
+    grun('sA11A13A12Q')
     columns(0)
-    gg.run('f10B10f11B11f13B13f12B12g10g11A21g13g12A23')
     lossb[1, pos[1]] = loss_recv(0)
     loss_send(1)
+    grun('f10B10f11B11f13B13f12B12g10g11A21g13g12A23')
     columns(1)
-    gg.run('f20B20b10b11b13b12A22')
     lossb[2, pos[2]] = loss_recv(1)
     loss_send(2)
+    grun('f20B20b10b11b13b12A22')
     columns(2)
-    gg.run('f21B21f23B23')
+    grun('f21B21f23B23')
     columns(3)
+    dcp = remote(dacc, drecv, l_ssem.at[4], l_rsem.at[4], partner)
+    grun('f22B22')
     losst[0] = loss_recv(2)
     lcp = remote(losst.at[0], losst.at[1], l_ssem.at[3], l_rsem.at[3], partner)
-    dcp = remote(dacc, drecv, l_ssem.at[4], l_rsem.at[4], partner)
-    gg.run('f22B22')
     lcp.wait_recv()
     loss_out[...] = jnp.sum(losst[0] + losst[1], keepdims=True) * (-1.0 / (2 * total_rows))
     dcp.wait_recv()
     drecv[...] = dacc[...] + drecv[...]
     gpc = pltpu.make_async_copy(drecv, gp_out, o_sem.at[1])
     gpc.start()
-    gg.run('g20g21g23g22b20b21b23b22')
+    grun('g20g21g23g22b20b21b23b22')
     gpc.wait()
     for view, out in enumerate((code1, code2)):
         pltpu.make_async_copy(cst.at[view], out, o_sem.at[2 + view]).wait()
-    gg.all_sent()
+    gg[0].all_sent()
     env.sent(losst.at[0], l_ssem.at[3])
     env.sent(dacc, l_ssem.at[4])
     env.drain()
 
     @pl.when(core == 1)
     def _():
-        for it in range(ITERS + 1):
-            for st in range(AXES):
-                env.sent(sums.at[it, st, :LINE - 1], s_ssem.at[it * AXES + st])
+        env.sent(sums.at[:, :, :LINE - 1], s_ssem.at[0])
         for st in range(AXES):
             env.sent(v_some(st), v_ssem.at[st])
         env.sent(dall.at[:, rows:], x_ssem.at[3])
@@ -573,6 +585,7 @@
         nsem = (ITERS + 1) * AXES
         dma = lambda n: pltpu.SemaphoreType.DMA((n,))
         grid3 = (LINE,) * AXES
+        packed = (2 * mine * dim // LANES, LANES)
         sds = jax.ShapeDtypeStruct
         code = sds((rows, cols), F32)
         zbuf = pltpu.VMEM((rows, dim), BF16)
@@ -584,7 +597,7 @@
         code1, code2, loss, gall, gp = pl.pallas_call(
             functools.partial(step_kernel, total_rows, total_protos),
             out_shape=(code, code, sds((1, 1), F32),
-                       sds(grid3 + (2 * mine, dim), F32), sds((cols, dim), F32)),
+                       sds(grid3 + packed, F32), sds((cols, dim), F32)),
             in_specs=[hbm] * 3,
             out_specs=(free, free, vm, free, free),
             scratch_shapes=[
@@ -604,11 +617,11 @@
                 pltpu.VMEM((AXES, LINE, 8, LANES), F32),
                 pltpu.VMEM((2, 8, LANES), F32),
                 square, square,
-                pltpu.VMEM((2 * mine, dim), F32),
+                pltpu.VMEM(packed, F32),
                 pltpu.VMEM((2, rows, cols), F32),
-                dma(4), dma(1), dma(1), dma(nsem), dma(nsem),
+                dma(4), dma(1), dma(1), dma(1), dma(nsem),
                 dma(5), dma(AG_SEMS), dma(1), dma(1),
-                dma(AXES), dma(AXES), dma(5), dma(AG_SEMS), dma(5), dma(5),
+                dma(AXES), dma(AXES), dma(5), dma(5),
                 dma(5), dma(5), dma(4),
             ],
             compiler_params=pltpu.CompilerParams(collective_id=0, has_side_effects=True,
@@ -620,9 +633,9 @@
             out_shape=(code, code, blocked, blocked, sds((cols, dim), F32)),
             in_specs=[vm] * 4,
             out_specs=(hbm,) * 5,
-            scratch_shapes=[dma(5)],
+            scratch_shapes=[dma(9)],
             compiler_params=pltpu.CompilerParams(vmem_limit_bytes=2 ** 20),
-        )(code1, code2, gall.reshape(proto_size, 2 * mine, dim), gp)
+        )(code1, code2, gall.reshape((proto_size,) + packed), gp)
         return o1, o2, loss[0, 0], g1.reshape(rows, dim), g2.reshape(rows, dim), og
 
     return jax.shard_map(

time: 73.9 us -> 70.6 us (0.955)
  Pallas kernels: 71.3 us -> 68.1 us
    pallas_call x1, Pallas kernels: 67.9 us -> 64.6 us  [local_step(): pl.pallas_call(functools.partial(step_kernel, total_rows, total_protos),...]
where the time goes in v7:
time: 70.6 us; the launch traced here: 70.5 us
  Pallas kernels  68.1 us (96%)
  between operations  2.41 us (3%)
    pallas_call x1, Pallas kernels, local_step(): pl.pallas_call(functools.partial(step_kernel, total_rows, total_protos),...  64.6 us
    pallas_call x1, Pallas kernels, local_step(): pl.pallas_call(functools.partial(write_kernel, mine), out_shape=(code, co...  3.46 us

profile of v7, /device:TPU:0, one launch (start us, length us, event | category | flops | bytes accessed | tf_op | source)
XLA Modules:
  0.0 70.5 jit_solution(2372045616265821204)
XLA Ops:
  0.6 64.6 %shard_map.82 = (f32[2048,256]{1,0:T(8,128)S(1)}, f32[2048,256]{1,0:T(8,128)S(1)}, f32[1,1]{1,0:T(1,128)}, f32[4,4,4,128,128]{4,3,2,1,0:T(8,128)S(1)}, f32[256,256]{1,0:T(8,128)S(1)}) custom-call(bf16[2048,256]{1,0:T(8,128)(2,1)} %z1h.1, bf16[2048,256]{1,0:T(8,128)(2,1)} %z2h.1, bf16[256,256]{1,0:T(8,128)(2,1)} %ch.1), custom_call_target="tpu_custom_call" | custom-call | tf_op jit(solution)/shard_map/pallas_call | solution.py:597
  65.3 3.5 %shard_map.83 = (f32[2048,256]{1,0:T(8,128)}, f32[2048,256]{1,0:T(8,128)}, f32[64,32,256]{2,1,0:T(8,128)}, f32[64,32,256]{2,1,0:T(8,128)}, f32[256,256]{1,0:T(8,128)}) custom-call(f32[2048,256]{1,0:T(8,128)S(1)} %get-tuple-element.16.code1, f32[2048,256]{1,0:T(8,128)S(1)} %get-tuple-element.17.code2, f32[64,128,128]{2,1,0:T(8,128)S(1)} %bitcast.4, ...), custom_call_target="tpu_custom_call" | custom-call | tf_op jit(solution)/shard_map/pallas_call | solution.py:631

commit v8 on v7

--- a/solution.py
+++ b/solution.py
@@ -8,7 +8,6 @@
 from jax.experimental.pallas import tpu as pltpu
 from jax.sharding import PartitionSpec as P
 
-EPSILON = 0.05
 TEMP_TAU = 0.1
 ITERS = 3
 LINE = 4
@@ -22,6 +21,7 @@
 G_CUTS = ((0, 40, 88, 128), (0, 40, 80, 128))
 AG_SEMS = 27
 DISTS = (2, 1, 3)
+WAYS = (1, 3)
 
 
 def _nt(a, b):
@@ -59,7 +59,7 @@
         self.partner = (me, 1 - self.core)
 
     def p(self, axis, d):
-        return self.pos[axis] if d == 0 else lax.rem(self.pos[axis] + d, LINE)
+        return self.pos[axis] if isinstance(d, int) and d == 0 else lax.rem(self.pos[axis] + d, LINE)
 
     def peer(self, axis, d):
         return (self.me + (self.p(axis, d) - self.pos[axis]) * self.stride[axis], self.core)
@@ -83,9 +83,9 @@
 
 
 class _Gather:
-    def __init__(self, env, buf, cuts, ssem, rsem, twin=None):
+    def __init__(self, env, buf, cuts, ssem, rsem, twin=None, rows=None):
         self.env, self.buf, self.parts = env, buf, _parts(cuts)
-        self.ssem, self.rsem, self.twin = ssem, rsem, twin
+        self.ssem, self.rsem, self.twin, self.rows = ssem, rsem, twin, rows
 
     def at(self, j, i0, i1, i2):
         ids = [None] * AXES
@@ -122,7 +122,7 @@
                 self.send(j, 0, d - 1, ref, 0, d, None if src is None else src.at[r0:r1, :])
 
     def s1_recv(self):
-        for d in (1, 3, 2):
+        for d in DISTS:
             self.recv(d - 1, 1)
 
     def chunk(self, j, level, k, m):
@@ -136,7 +136,7 @@
     def a_send(self, level, k):
         for j in range(AXES):
             ref = self.chunk(j, level, k, 0)
-            for d in (1, 3):
+            for d in WAYS:
                 self.send(j, 2 * level - 1, self.slot(level, k, d), ref, level, d)
 
     def way(self, k):
@@ -152,7 +152,7 @@
         for k in offsets:
             for j in range(AXES):
                 ref = self.chunk(j, 1, k, 0)
-                for d in (1, 3):
+                for d in WAYS:
                     self.send(j, 3, self.slot(2, 0, d), ref, 2, d)
 
     def own_piece(self):
@@ -173,16 +173,18 @@
         ts, tr = self.twin
         for j in range(AXES):
             ref = self.chunk(j, 2, k, m)
-            self.env.remote(ref, ref, ts.at[0], tr.at[0], self.env.partner)
-
-    def t_recv(self):
-        self.env.arrived(self.buf, self.twin[1].at[0])
+            i = (k == 2) + (m == 2)
+            self.env.remote(ref, ref, ts.at[0], tr.at[i], self.env.partner)
+
+    def t_recv(self, group):
+        part = (self.buf.at[:3, :3], self.buf.at[:3, :2], self.buf.at[0, 0])[group]
+        self.env.arrived(part, self.twin[1].at[group])
 
     def run(self, ops):
         for op in re.findall('[a-zA-Z][0-9]*', ops):
             args = [int(c) for c in op[1:]]
             {'S': self.s1_send, 's': self.s1_recv, 'A': self.a_send, 'f': self.f_recv, 'g': self.g_recv,
-             'B': self.b_send, 'b': self.b_recv, 'T': self.t_send, 'P': self.own_piece, 'Q': self.other_pieces}[op[0]](*args)
+             'B': self.b_send, 'b': self.b_recv, 'T': self.t_send, 'R': self.rows, 'U': self.t_recv, 'P': self.own_piece, 'Q': self.other_pieces}[op[0]](*args)
 
 
 def write_kernel(mine, code1, code2, gfull, gp, o1, o2, g1, g2, og, sem):
@@ -204,14 +206,15 @@
 def step_kernel(total_rows, total_protos, z1h, z2h, ch,
                 code1, code2, loss_out, gfull, gp_out,
                 z1, z2, y1, y2, c_ref, f_scr, e_scr, cfull, lrow, frow, vall, zr, dall,
-                cacc, vb, ub, stage, csend, crecv, sums, lossb, losst, dacc, drecv, dz, cst,
+                cacc, vb, ub, stage, csend, crecv, sums, lossb, losst, dacc, drecv, dz, cst, vsrc,
                 lsem, c_ssem, c_rsem, s_ssem, s_rsem, a_ssem, a_rsem, t_ssem, t_rsem,
-                v_ssem, v_rsem, l_ssem, l_rsem, x_ssem, x_rsem, o_sem):
+                v_ssem, v_rsem, g_ssem, g_rsem, l_ssem, l_rsem, x_ssem, x_rsem, o_sem):
     env = _Env()
     me, core, pos, partner = env.me, env.core, env.pos, env.partner
     remote = env.remote
     rows, cols = z1.shape[0], c_ref.shape[0]
-    mine = zr.shape[0] // 2
+    both = zr.shape[0]
+    mine = both // 2
     blocks = LINE ** AXES
     fscale = 1.0 / (2 * total_rows * TEMP_TAU)
     zs, ys = (z1, z2), (y1, y2)
@@ -224,8 +227,7 @@
             pl.semaphore_signal(barrier, inc=1, device_id=env.peer(axis, d), device_id_type=MESH)
     loads = [pltpu.make_async_copy(src, dst, lsem.at[i]) for i, (src, dst) in enumerate(
         ((ch, c_ref), (z1h, z1), (z2h, z2), (ch, cfull.at[pos[2], pos[1], pos[0]])))]
-    gc = _Gather(env, cfull, C_CUTS, a_ssem, a_rsem, (t_ssem, t_rsem))
-    gg = [_Gather(env, gfull, cuts, a_ssem, a_rsem) for cuts in G_CUTS]
+    gg = [_Gather(env, gfull, cuts, g_ssem, g_rsem) for cuts in G_CUTS]
 
     def by_core(fn):
         for c in range(2):
@@ -261,14 +263,41 @@
             return 0
         lax.fori_loop(0, chunks, body, 0, unroll=2)
 
-    def row_scores(lo, hi):
-        def body(q, _):
-            z_, y_, x_ = block(q)
-            l = _nt(zr[...], cfull[z_, y_, x_]) * (1.0 / TEMP_TAU)
-            lrow[q] = l
-            frow[q] = jnp.exp(l)
+    def score_block(offsets):
+        z_, y_, x_ = (env.p(axis, d) for axis, d in zip((2, 1, 0), offsets))
+        q = (z_ * LINE + y_) * LINE + x_
+        l = _nt(zr[...], cfull[z_, y_, x_]) * (1.0 / TEMP_TAU)
+        lrow[q] = l
+        frow[q] = jnp.exp(l)
+
+    def near(i):
+        return i + lax.div(i, 2)
+
+    def row_scores(piece):
+        def spot(axis, d, rest):
+            rest = list(rest)
+            rest.insert(axis, d)
+            score_block(rest)
+
+        def body(i, _):
+            a, b = near(lax.div(i, 3)), near(lax.rem(i, 3))
+            if piece < 3:
+                spot(0, near(jnp.int32(piece)), (a, b))
+            elif piece < 6:
+                spot(piece - 3, 2, (a, b))
             return 0
-        lax.fori_loop(lo, hi, body, 0, unroll=4)
+
+        def last(i, _):
+            for axis in range(AXES):
+                spot(axis, near(i), (2, 2))
+            return 0
+        if piece < 6:
+            lax.fori_loop(0, 9, body, 0, unroll=True)
+        else:
+            lax.fori_loop(0, 3, last, 0, unroll=True)
+            score_block((2, 2, 2))
+
+    gc = _Gather(env, cfull, C_CUTS, a_ssem, a_rsem, (t_ssem, t_rsem), row_scores)
 
     def block(q):
         return lax.div(q, LINE * LINE), lax.rem(lax.div(q, LINE), LINE), lax.rem(q, LINE)
@@ -306,24 +335,27 @@
             us = [ub[view, :, ls] for ls in tiles]
 
             def body(g, _, view=view, us=us):
-                acc = [None] * 4
-                for t, ls in enumerate(tiles):
-                    x = e_scr[view, g, :, ls] * us[t]
-                    acc[t % 4] = x if acc[t % 4] is None else acc[t % 4] + x
-                cacc[view, pl.ds(pl.multiple_of(g * 8, 8), 8), :] = (acc[0] + acc[1]) + (acc[2] + acc[3])
+                terms = [e_scr[view, g, :, ls] * u for ls, u in zip(tiles, us)]
+                chains = [sum(terms[t::LINE][1:], terms[t]) for t in range(LINE)]
+                cacc[view, pl.ds(pl.multiple_of(g * 8, 8), 8), :] = (chains[0] + chains[1]) + (chains[2] + chains[3])
                 return 0
             lax.fori_loop(0, groups, body, 0, unroll=4)
 
-    def vsend(st):
-        ref = vall.at[(pos[2], pos[1], pos[0])[:AXES - st]]
-        for d in DISTS:
-            remote(ref, ref, v_ssem.at[st], v_rsem.at[st], env.peer(st, d))
-
-    def v_some(st):
-        return vall.at[(0,) * (AXES - 1 - st) + (pl.ds(0, LINE - 1),)]
-
-    def vrecv(st):
-        env.arrived(v_some(st), v_rsem.at[st])
+    def at_offset(oz, oy, ox):
+        return (env.p(2, oz) * LINE + env.p(1, oy)) * LINE + env.p(0, ox)
+
+    def broadcast_v():
+        dst = vall.at[pos[2], pos[1], pos[0]]
+        pltpu.make_async_copy(vsrc, dst, v_rsem.at[0]).start()
+        order = DISTS + (0,)
+        for oz in order:
+            for oy in order:
+                for ox in order:
+                    there = at_offset(oz, oy, ox)
+                    remote(vsrc, dst, v_ssem.at[3], v_rsem.at[0], (there, 0))
+                    if oz or oy or ox:
+                        group = 0 if oz else 1 if oy else 2
+                        remote(vsrc, dst, v_ssem.at[group], v_rsem.at[0], (there, 1))
 
     def load_sums(it, value):
         for j, (l0, l1) in enumerate(_parts(SUM_CUTS)):
@@ -362,13 +394,10 @@
         if slot in (1, 2):
             env.arrived(ys[slot - 1], x_rsem.at[slot - 1])
             other_scores(slot - 1)
-        elif slot == 7:
-            gc.t_recv()
-            row_scores(0, blocks // 2)
-        elif slot == 8:
-            row_scores(blocks // 2, blocks)
         if slot in (3, 4, 5, 6):
             denominators(slot - 3)
+        if slot == 6:
+            gc.run('U0R0R1R2U1R3R4R5U2R6')
 
     @pl.when(core == 1)
     def _():
@@ -384,8 +413,8 @@
             last = it == ITERS - 1
             vrow = 1.0 / (float(total_protos) * total)
             if last:
-                vall[pos[2], pos[1], pos[0]] = vrow
-                vsend(0)
+                vsrc[...] = vrow
+                broadcast_v()
             spread(vrow)
             row_sums(it, rows if it == 0 else 2 * rows)
             if it == 0:
@@ -394,26 +423,20 @@
             for st in range(AXES):
                 send_sums(it, st)
                 hidden(it * AXES + st)
+                tot = recv_sums(it, st)
                 if last:
-                    vrecv(st)
-                    if st < AXES - 1:
-                        vsend(st + 1)
-                tot = recv_sums(it, st)
+                    send_sums(it, 1)
+                    break
                 if st < AXES - 1:
                     continue
                 for (l0, l1), t in zip(_parts(SUM_CUTS), tot):
-                    if last:
-                        dall[0:2, l0:l1] = t
-                    else:
-                        u = 1.0 / (float(total_rows) * t)
-                        for view in range(2):
-                            ub[view, :, l0:l1] = jnp.broadcast_to(u[view:view + 1], (8, l1 - l0))
+                    u = 1.0 / (float(total_rows) * t)
+                    for view in range(2):
+                        ub[view, :, l0:l1] = jnp.broadcast_to(u[view:view + 1], (8, l1 - l0))
             if not last:
                 weighted_columns()
                 column_sums(it + 1)
                 total = csend[it + 1]
-        remote(dall.at[:, rows:], dall.at[:, :rows], x_ssem.at[3], x_rsem.at[3], partner)
-        remote(vall, vall, x_ssem.at[4], x_rsem.at[4], partner)
 
     @pl.when(core == 0)
     def _():
@@ -437,44 +460,57 @@
         gc.run('sA11A13A12QT00')
         gc.run('f10B10f11B11f13B13f12B12g10g11A21g13g12A23')
         gc.run('f20B20b10b11b13b12A22T10T30T20')
-        gc.run('f21B21f23B23g20g21g23T01T03T11T13T31T33')
-        gc.run('f22B22g22T21T23b20T02b21T12b23T32b22T22')
-        row_scores(0, blocks)
-        env.arrived(dall.at[:, :rows], x_rsem.at[3])
-        env.arrived(vall, x_rsem.at[4])
+        gc.run('f21B21f23B23g20g21g23T01T03T11T13T31T33R0')
+        gc.run('f22B22R1g22T21T23b20T02b21T12R2')
+        gc.run('b23T32R3b22T22R4R5R6')
         gc.all_sent()
         for i, ref in enumerate((z1, z2, stage.at[0, :, :rows])):
             env.sent(ref, x_ssem.at[i])
         env.sent(cfull, t_ssem.at[0])
         env.drain()
 
-    tile = pl.multiple_of(lax.div(me * mine, LANES) * LANES, LANES)
-    shift = lax.rem(me * mine, LANES)
-    dv = dall[:, pl.ds(tile, LANES)]
-    col = [_row_to_col(dv[i:i + 1, :], mine, shift) for i in range(4)]
-    rc = jnp.broadcast_to(1.0 / jnp.concatenate(col[0:2], axis=0), (2 * mine, LANES))
-    den = jnp.concatenate(col[2:4], axis=0)
-    dc = jnp.broadcast_to(1.0 / den, (2 * mine, LANES))
-    ld = jnp.broadcast_to(jnp.log(den), (2 * mine, LANES))
-
-    def code_rows(q, h):
+    env.arrived(vall, v_rsem.at[0])
+
+    def lanes(h):
+        return slice(h * LANES, (h + 1) * LANES)
+
+    def table(q):
+        return lax.div(q, blocks // 2), pl.ds(pl.multiple_of(lax.rem(q, blocks // 2) * both, both), both)
+
+    def sumbody(q, acc):
         z_, y_, x_ = block(q)
-        f = frow[q, :, h * LANES:(h + 1) * LANES]
-        v0 = jnp.broadcast_to(vall[z_, y_, x_, h:h + 1, :], (mine, LANES))
-        v1 = jnp.broadcast_to(vall[z_, y_, x_, 2 + h:3 + h, :], (mine, LANES))
-        return f, f * f * (rc * jnp.concatenate([v0, v1], axis=0))
+        view, part = table(q)
+        for h in range(2):
+            f = frow[q, :, lanes(h)]
+            v0 = jnp.broadcast_to(vall[z_, y_, x_, h:h + 1, :], (mine, LANES))
+            v1 = jnp.broadcast_to(vall[z_, y_, x_, 2 + h:3 + h, :], (mine, LANES))
+            t = f * f * jnp.concatenate([v0, v1], axis=0)
+            cst[view, part, lanes(h)] = t
+            acc = (acc[0] + t, acc[1] + f)
+        return acc
+
+    zero = jnp.zeros((both, LANES), F32)
+    rsum, den = (jnp.sum(a, axis=1, keepdims=True)
+                 for a in lax.fori_loop(0, blocks, sumbody, (zero, zero), unroll=4))
+    rc = jnp.broadcast_to(1.0 / rsum, (both, LANES))
+    dc = jnp.broadcast_to(1.0 / den, (both, LANES))
+    ld = jnp.broadcast_to(jnp.log(den), (both, LANES))
+
+    def other_codes(q, h):
+        view, part = table(q)
+        code = cst[view, part, lanes(h)] * rc
+        return jnp.concatenate([code[mine:], code[:mine]], axis=0)
 
     def dzbody(i, acc):
         hs = []
         for x_ in range(LINE):
             for h in range(2):
-                f, code = code_rows(i * LINE + x_, h)
-                other = jnp.concatenate([code[mine:], code[:mine]], axis=0)
-                hs.append(((f * dc - other) * fscale).astype(BF16))
+                q = i * LINE + x_
+                hs.append(((frow[q, :, lanes(h)] * dc - other_codes(q, h)) * fscale).astype(BF16))
         cl = cfull[lax.div(i, LINE), lax.rem(i, LINE)].reshape(LINE * cols, cols)
         return acc + _nn(jnp.concatenate(hs, axis=1), cl)
 
-    rowgrad = lax.fori_loop(0, LINE * LINE, dzbody, jnp.zeros((2 * mine, cols), F32), unroll=4)
+    rowgrad = lax.fori_loop(0, LINE * LINE, dzbody, jnp.zeros((both, cols), F32), unroll=4)
     dz[...] = jnp.concatenate([rowgrad[:, :LANES], rowgrad[:, LANES:]], axis=0)
 
     own = pltpu.make_async_copy(dz, gfull.at[pos[2], pos[1], pos[0]], o_sem.at[0])
@@ -482,6 +518,12 @@
     by_core(lambda c: gg[c].s1_send(dz))
     own.wait()
     grun('A10P')
+
+    @pl.when(core == 1)
+    def _():
+        recv_sums(ITERS - 1, 1)
+        send_sums(ITERS - 1, 2)
+
     spread(vall[pos[2], pos[1], pos[0]])
     dacc[...] = jnp.zeros((cols, cols), F32)
 
@@ -509,13 +551,10 @@
 
     def lbody(q, acc):
         for h in range(2):
-            f, code = code_rows(q, h)
-            lp = lrow[q, :, h * LANES:(h + 1) * LANES] - ld
-            other = jnp.concatenate([code[mine:], code[:mine]], axis=0)
-            acc = acc + other * lp
+            acc = acc + other_codes(q, h) * (lrow[q, :, lanes(h)] - ld)
         return acc
-    part = lax.fori_loop(0, blocks, lbody, jnp.zeros((2 * mine, LANES), F32), unroll=4)
-    lossb[0, pos[0]] = jnp.sum(part.reshape(2 * mine // 8, 8, LANES), axis=0)
+    part = lax.fori_loop(0, blocks, lbody, jnp.zeros((both, LANES), F32), unroll=4)
+    lossb[0, pos[0]] = jnp.sum(part.reshape(both // 8, 8, LANES), axis=0)
 
     def loss_send(st):
         ref = lossb.at[st, pos[st]]
@@ -529,14 +568,22 @@
 
     loss_send(0)
     grun('sA11A13A12Q')
-    columns(0)
+
+    @pl.when(core == 1)
+    def _():
+        for (l0, l1), t in zip(_parts(SUM_CUTS), recv_sums(ITERS - 1, AXES - 1)):
+            dall[0:2, l0:l1] = t
+        remote(dall.at[:, rows:], dall.at[:, :rows], x_ssem.at[3], x_rsem.at[3], partner)
+
     lossb[1, pos[1]] = loss_recv(0)
     loss_send(1)
     grun('f10B10f11B11f13B13f12B12g10g11A21g13g12A23')
-    columns(1)
     lossb[2, pos[2]] = loss_recv(1)
     loss_send(2)
+    pl.when(core == 0)(lambda: env.arrived(dall.at[:, :rows], x_rsem.at[3]))
+    columns(0)
     grun('f20B20b10b11b13b12A22')
+    columns(1)
     columns(2)
     grun('f21B21f23B23')
     columns(3)
@@ -562,10 +609,9 @@
     @pl.when(core == 1)
     def _():
         env.sent(sums.at[:, :, :LINE - 1], s_ssem.at[0])
-        for st in range(AXES):
-            env.sent(v_some(st), v_ssem.at[st])
+        for i, ref in enumerate((vall.at[:LINE - 1], vall.at[0, :LINE - 1], vall.at[0, 0, :LINE - 1], vall)):
+            env.sent(ref, v_ssem.at[i])
         env.sent(dall.at[:, rows:], x_ssem.at[3])
-        env.sent(vall, x_ssem.at[4])
         env.drain()
 
 
@@ -584,13 +630,15 @@
         free = pl.BlockSpec(memory_space=pl.ANY)
         nsem = (ITERS + 1) * AXES
         dma = lambda n: pltpu.SemaphoreType.DMA((n,))
+        one, few, many = dma(1), dma(5), dma(AG_SEMS)
+        pair = 2 * mine
         grid3 = (LINE,) * AXES
-        packed = (2 * mine * dim // LANES, LANES)
+        packed = (pair * dim // LANES, LANES)
         sds = jax.ShapeDtypeStruct
         code = sds((rows, cols), F32)
         zbuf = pltpu.VMEM((rows, dim), BF16)
         square = pltpu.VMEM((cols, dim), F32)
-        rowbuf = pltpu.VMEM((proto_size, 2 * mine, cols), F32)
+        rowbuf = pltpu.VMEM((proto_size, pair, cols), F32)
         small = pltpu.VMEM((ITERS, 4, LANES), F32)
         spread = pltpu.VMEM((2, cols, LANES), F32)
         args = [pltpu.with_memory_space_constraint(a, pltpu.HBM) for a in (emb_one, emb_two, protos)]
@@ -607,7 +655,7 @@
                 pltpu.VMEM(grid3 + (cols, dim), BF16),
                 rowbuf, rowbuf,
                 pltpu.VMEM(grid3 + (4, LANES), F32),
-                pltpu.VMEM((2 * mine, dim), BF16),
+                pltpu.VMEM((pair, dim), BF16),
                 pltpu.VMEM((4, total_rows), F32),
                 spread, spread,
                 pltpu.VMEM((2, 8, total_rows), F32),
@@ -619,10 +667,9 @@
                 square, square,
                 pltpu.VMEM(packed, F32),
                 pltpu.VMEM((2, rows, cols), F32),
-                dma(4), dma(1), dma(1), dma(1), dma(nsem),
-                dma(5), dma(AG_SEMS), dma(1), dma(1),
-                dma(AXES), dma(AXES), dma(5), dma(5),
-                dma(5), dma(5), dma(4),
+                pltpu.VMEM((4, LANES), F32),
+                few, one, one, one, dma(nsem),
+                few, many, one, few, few, one, few, many, few, few, few, few, few,
             ],
             compiler_params=pltpu.CompilerParams(collective_id=0, has_side_effects=True,
                                                  vmem_limit_bytes=44 * 2 ** 20),

time: 70.6 us -> 66.9 us (0.948)
  Pallas kernels: 68.1 us -> 64.4 us
    pallas_call x1, Pallas kernels: 64.6 us -> 60.9 us  [local_step(): pl.pallas_call(functools.partial(step_kernel, total_rows, total_protos),...]
where the time goes in v8:
time: 66.9 us; the launch traced here: 66.8 us
  Pallas kernels  64.4 us (96%)
  between operations  2.41 us (4%)
    pallas_call x1, Pallas kernels, local_step(): pl.pallas_call(functools.partial(step_kernel, total_rows, total_protos),...  60.9 us
    pallas_call x1, Pallas kernels, local_step(): pl.pallas_call(functools.partial(write_kernel, mine), out_shape=(code, co...  3.46 us

profile of v8, /device:TPU:0, one launch (start us, length us, event | category | flops | bytes accessed | tf_op | source)
XLA Modules:
  0.0 66.8 jit_solution(982654187426279609)
XLA Ops:
  0.6 60.9 %shard_map.82 = (f32[2048,256]{1,0:T(8,128)S(1)}, f32[2048,256]{1,0:T(8,128)S(1)}, f32[1,1]{1,0:T(1,128)}, f32[4,4,4,128,128]{4,3,2,1,0:T(8,128)S(1)}, f32[256,256]{1,0:T(8,128)S(1)}) custom-call(bf16[2048,256]{1,0:T(8,128)(2,1)} %z1h.1, bf16[2048,256]{1,0:T(8,128)(2,1)} %z2h.1, bf16[256,256]{1,0:T(8,128)(2,1)} %ch.1), custom_call_target="tpu_custom_call" | custom-call | tf_op jit(solution)/shard_map/pallas_call | solution.py:645
  61.6 3.5 %shard_map.83 = (f32[2048,256]{1,0:T(8,128)}, f32[2048,256]{1,0:T(8,128)}, f32[64,32,256]{2,1,0:T(8,128)}, f32[64,32,256]{2,1,0:T(8,128)}, f32[256,256]{1,0:T(8,128)}) custom-call(f32[2048,256]{1,0:T(8,128)S(1)} %get-tuple-element.16.code1, f32[2048,256]{1,0:T(8,128)S(1)} %get-tuple-element.17.code2, f32[64,128,128]{2,1,0:T(8,128)S(1)} %bitcast.4, ...), custom_call_target="tpu_custom_call" | custom-call | tf_op jit(solution)/shard_map/pallas_call | solution.py:678

commit v9 on v8

--- a/solution.py
+++ b/solution.py
@@ -16,8 +16,10 @@
 F32 = jnp.float32
 BF16 = jnp.bfloat16
 LANES = 128
+VIEWS = (0, 1)
+SCALE = 1.0 / TEMP_TAU
 SUM_CUTS = (0, 1408, 2816, 4096)
-C_CUTS = (0, 80, 160, 256)
+C_CUTS = (0, 88, 168, 256)
 G_CUTS = ((0, 40, 88, 128), (0, 40, 80, 128))
 AG_SEMS = 27
 DISTS = (2, 1, 3)
@@ -190,7 +192,7 @@
 def write_kernel(mine, code1, code2, gfull, gp, o1, o2, g1, g2, og, sem):
     half = code1.shape[0] // 2
     pairs = [(gp, og)]
-    for h in range(2):
+    for h in VIEWS:
         for src, dst in ((code1, o1), (code2, o2)):
             pairs.append((src.at[h * half:(h + 1) * half, :], dst.at[h * half:(h + 1) * half, :]))
         for view, dst in enumerate((g1, g2)):
@@ -207,7 +209,7 @@
                 code1, code2, loss_out, gfull, gp_out,
                 z1, z2, y1, y2, c_ref, f_scr, e_scr, cfull, lrow, frow, vall, zr, dall,
                 cacc, vb, ub, stage, csend, crecv, sums, lossb, losst, dacc, drecv, dz, cst, vsrc,
-                lsem, c_ssem, c_rsem, s_ssem, s_rsem, a_ssem, a_rsem, t_ssem, t_rsem,
+                lsem, c_ssem, c_rsem, s_ssem, a_ssem, a_rsem, t_ssem, t_rsem,
                 v_ssem, v_rsem, g_ssem, g_rsem, l_ssem, l_rsem, x_ssem, x_rsem, o_sem):
     env = _Env()
     me, core, pos, partner = env.me, env.core, env.pos, env.partner
@@ -220,24 +222,24 @@
     zs, ys = (z1, z2), (y1, y2)
     chunks, groups = rows // cols, cols // 8
 
+    loads = [pltpu.make_async_copy(src, dst, lsem.at[i]) for i, (src, dst) in enumerate(
+        ((ch, c_ref), (z1h, z1), (z2h, z2), (ch, cfull.at[pos[2], pos[1], pos[0]])))]
+    gg = [_Gather(env, gfull, cuts, g_ssem, g_rsem) for cuts in G_CUTS]
+
+    def by_core(fn):
+        for c in VIEWS:
+            pl.when(core == c)(functools.partial(fn, c))
+
+    def grun(ops):
+        by_core(lambda c: gg[c].run(ops))
+
+    for cp in loads[:3]:
+        cp.start()
     barrier = pltpu.get_barrier_semaphore()
     pl.semaphore_signal(barrier, inc=1, device_id=partner, device_id_type=MESH)
     for axis in range(AXES):
         for d in DISTS:
             pl.semaphore_signal(barrier, inc=1, device_id=env.peer(axis, d), device_id_type=MESH)
-    loads = [pltpu.make_async_copy(src, dst, lsem.at[i]) for i, (src, dst) in enumerate(
-        ((ch, c_ref), (z1h, z1), (z2h, z2), (ch, cfull.at[pos[2], pos[1], pos[0]])))]
-    gg = [_Gather(env, gfull, cuts, g_ssem, g_rsem) for cuts in G_CUTS]
-
-    def by_core(fn):
-        for c in range(2):
-            pl.when(core == c)(functools.partial(fn, c))
-
-    def grun(ops):
-        by_core(lambda c: gg[c].run(ops))
-
-    for cp in loads[:3]:
-        cp.start()
 
     def scores(view):
         cacc[view] = jnp.zeros((cols, LANES), F32)
@@ -245,7 +247,7 @@
         def body(i, _):
             n0 = pl.multiple_of(i * cols, cols)
             s = _nt(c_ref[...], zs[view][pl.ds(n0, cols), :])
-            f = jnp.exp(s * (1.0 / TEMP_TAU))
+            f = jnp.exp(s * SCALE)
             stage[0, 2 + view:3 + view, pl.ds(n0, cols)] = jnp.sum(f, axis=0, keepdims=True)
             e = f * f
             f_scr[view, :, pl.ds(n0, cols)] = f
@@ -258,7 +260,7 @@
     def other_scores(view):
         def body(i, _):
             n0 = pl.multiple_of(i * cols, cols)
-            f = jnp.exp(_nt(c_ref[...], ys[view][pl.ds(n0, cols), :]) * (1.0 / TEMP_TAU))
+            f = jnp.exp(_nt(c_ref[...], ys[view][pl.ds(n0, cols), :]) * SCALE)
             e_scr[view, :, :, pl.ds(rows + n0, cols)] = (f * f).reshape(groups, 8, cols)
             return 0
         lax.fori_loop(0, chunks, body, 0, unroll=2)
@@ -266,7 +268,7 @@
     def score_block(offsets):
         z_, y_, x_ = (env.p(axis, d) for axis, d in zip((2, 1, 0), offsets))
         q = (z_ * LINE + y_) * LINE + x_
-        l = _nt(zr[...], cfull[z_, y_, x_]) * (1.0 / TEMP_TAU)
+        l = _nt(zr[...], cfull[z_, y_, x_]) * SCALE
         lrow[q] = l
         frow[q] = jnp.exp(l)
 
@@ -303,15 +305,15 @@
         return lax.div(q, LINE * LINE), lax.rem(lax.div(q, LINE), LINE), lax.rem(q, LINE)
 
     def column_sums(it):
-        for view in range(2):
-            for h in range(2):
+        for view in VIEWS:
+            for h in VIEWS:
                 k = 2 * view + h
                 s = jnp.sum(cacc[view, h * LANES:(h + 1) * LANES, :], axis=1, keepdims=True)
                 csend[it, k:k + 1, :] = _col_to_row(s)
 
     def spread(vrow):
-        for view in range(2):
-            for h in range(2):
+        for view in VIEWS:
+            for h in VIEWS:
                 k = 2 * view + h
                 vb[view, h * LANES:(h + 1) * LANES, :] = jnp.broadcast_to(
                     _row_to_col(vrow[k:k + 1, :]), (LANES, LANES))
@@ -321,7 +323,7 @@
 
     def row_sums(it, width):
         tiles = [slice(l, l + LANES) for l in range(0, width, LANES)]
-        for view in range(2):
+        for view in VIEWS:
             def body(g, acc, view=view):
                 w = vb[view, pl.ds(pl.multiple_of(g * 8, 8), 8), :]
                 return tuple(a + e_scr[view, g, :, ls] * w for a, ls in zip(acc, tiles))
@@ -331,7 +333,7 @@
 
     def weighted_columns():
         tiles = [slice(l, l + LANES) for l in range(0, 2 * rows, LANES)]
-        for view in range(2):
+        for view in VIEWS:
             us = [ub[view, :, ls] for ls in tiles]
 
             def body(g, _, view=view, us=us):
@@ -357,19 +359,33 @@
                         group = 0 if oz else 1 if oy else 2
                         remote(vsrc, dst, v_ssem.at[group], v_rsem.at[0], (there, 1))
 
-    def load_sums(it, value):
-        for j, (l0, l1) in enumerate(_parts(SUM_CUTS)):
-            sums[it, 0, pos[j], :, l0:l1] = value[:, l0:l1]
+    def within(lo, hi):
+        return [(j, max(l0, lo), min(l1, hi)) for j, (l0, l1) in enumerate(_parts(SUM_CUTS)) if l0 < hi and l1 > lo]
+
+    def load_sums(it, part, hi):
+        for j, l0, l1 in within(0, hi):
+            sums[it, 0, pos[j], :, l0:l1] = stage[part + (slice(l0, l1),)]
 
     def send_sums(it, st):
         for d in DISTS:
-            for j, (l0, l1) in enumerate(_parts(SUM_CUTS)):
+            for j, l0, l1 in within(0, rows if it + st == 0 else total_rows):
                 ax = (st + j) % AXES
                 src = sums.at[it, st, pos[ax], :, l0:l1]
-                remote(src, src, s_ssem.at[0], s_rsem.at[it * AXES + st], env.peer(ax, d))
+                remote(src, src, s_ssem.at[2 if it else min(st, 1)], a_rsem.at[it * AXES + st], env.peer(ax, d))
+
+    def send_first():
+        for d in DISTS + (0,):
+            for j, l0, l1 in within(rows, total_rows):
+                src = sums.at[0, 0, pos[j], :, l0:l1]
+                if d:
+                    remote(src, src, x_ssem.at[3], a_rsem.at[0], (env.peer(j, d)[0], 1))
+                else:
+                    remote(src, src, x_ssem.at[3], x_rsem.at[3], partner)
 
     def recv_sums(it, st):
-        env.arrived(sums.at[it, st, :LINE - 1], s_rsem.at[it * AXES + st])
+        if it + st == 0:
+            env.arrived(sums.at[0, 0, 0, :, rows:], x_rsem.at[3])
+        env.arrived(sums.at[it, st, :LINE - 1], a_rsem.at[it * AXES + st])
         tot = []
         for j, (l0, l1) in enumerate(_parts(SUM_CUTS)):
             s = [sums[it, st, i, :, l0:l1] for i in range(LINE)]
@@ -381,7 +397,8 @@
 
     def denominators(st):
         if st == 0:
-            load_sums(ITERS, stage[0, 2:4])
+            env.arrived(stage.at[0, :, rows:], x_rsem.at[2])
+            load_sums(ITERS, (0, slice(2, 4)), total_rows)
         else:
             tot = recv_sums(ITERS, st - 1)
         if st < AXES:
@@ -402,7 +419,7 @@
     @pl.when(core == 1)
     def _():
         loads[0].wait()
-        for view in range(2):
+        for view in VIEWS:
             loads[1 + view].wait()
             scores(view)
         pl.semaphore_wait(barrier, 1 + AXES * (LINE - 1))
@@ -417,9 +434,7 @@
                 broadcast_v()
             spread(vrow)
             row_sums(it, rows if it == 0 else 2 * rows)
-            if it == 0:
-                env.arrived(stage.at[0, :, rows:], x_rsem.at[2])
-            load_sums(it, stage[it, 0:2])
+            load_sums(it, (it, slice(0, 2)), rows if it == 0 else total_rows)
             for st in range(AXES):
                 send_sums(it, st)
                 hidden(it * AXES + st)
@@ -431,7 +446,7 @@
                     continue
                 for (l0, l1), t in zip(_parts(SUM_CUTS), tot):
                     u = 1.0 / (float(total_rows) * t)
-                    for view in range(2):
+                    for view in VIEWS:
                         ub[view, :, l0:l1] = jnp.broadcast_to(u[view:view + 1], (8, l1 - l0))
             if not last:
                 weighted_columns()
@@ -442,20 +457,24 @@
     def _():
         loads[3].start()
         loads[0].wait()
-        for view in range(2):
+        for view in VIEWS:
             loads[1 + view].wait()
             scores(view)
         column_sums(0)
         loads[3].wait()
         pl.semaphore_wait(barrier, 1 + AXES * (LINE - 1))
         cp = exchange()
-        gc.run('SA10P')
+        gc.run('S')
         cp.wait()
         vrow = 1.0 / (float(total_protos) * (csend[0] + crecv[0]))
         spread(vrow)
         row_sums(0, rows)
+        for j, l0, l1 in within(rows, total_rows):
+            sums[0, 0, pos[j], :, l0:l1] = stage[0, 0:2, l0 - rows:l1 - rows]
+        send_first()
+        gc.run('A10P')
         remote(stage.at[0, :, :rows], stage.at[0, :, rows:], x_ssem.at[2], x_rsem.at[2], partner)
-        for i in range(2):
+        for i in VIEWS:
             remote(zs[i], ys[i], x_ssem.at[i], x_rsem.at[i], partner)
         gc.run('sA11A13A12QT00')
         gc.run('f10B10f11B11f13B13f12B12g10g11A21g13g12A23')
@@ -464,7 +483,7 @@
         gc.run('f22B22R1g22T21T23b20T02b21T12R2')
         gc.run('b23T32R3b22T22R4R5R6')
         gc.all_sent()
-        for i, ref in enumerate((z1, z2, stage.at[0, :, :rows])):
+        for i, ref in enumerate((z1, z2, stage.at[0, :, :rows], sums.at[0, 0, :2])):
             env.sent(ref, x_ssem.at[i])
         env.sent(cfull, t_ssem.at[0])
         env.drain()
@@ -480,7 +499,7 @@
     def sumbody(q, acc):
         z_, y_, x_ = block(q)
         view, part = table(q)
-        for h in range(2):
+        for h in VIEWS:
             f = frow[q, :, lanes(h)]
             v0 = jnp.broadcast_to(vall[z_, y_, x_, h:h + 1, :], (mine, LANES))
             v1 = jnp.broadcast_to(vall[z_, y_, x_, 2 + h:3 + h, :], (mine, LANES))
@@ -504,7 +523,7 @@
     def dzbody(i, acc):
         hs = []
         for x_ in range(LINE):
-            for h in range(2):
+            for h in VIEWS:
                 q = i * LINE + x_
                 hs.append(((frow[q, :, lanes(h)] * dc - other_codes(q, h)) * fscale).astype(BF16))
         cl = cfull[lax.div(i, LINE), lax.rem(i, LINE)].reshape(LINE * cols, cols)
@@ -517,7 +536,6 @@
     own.start()
     by_core(lambda c: gg[c].s1_send(dz))
     own.wait()
-    grun('A10P')
 
     @pl.when(core == 1)
     def _():
@@ -537,11 +555,11 @@
             n0 = pl.multiple_of(i * cols, cols)
             inv = 1.0 / dall[:, pl.ds(n0, cols)]
             code, prob = [], []
-            for view in range(2):
+            for view in VIEWS:
                 w = jnp.concatenate([vb[view], vb[view]], axis=1)
                 code.append(e_scr[view, :, :, pl.ds(n0, cols)].reshape(cols, cols) * w * inv[view:view + 1, :])
                 prob.append(f_scr[view, :, pl.ds(n0, cols)] * inv[2 + view:3 + view, :])
-            for view in range(2):
+            for view in VIEWS:
                 h = ((prob[view] - code[1 - view]) * fscale).astype(BF16)
                 dacc[...] += _nn(h, zs[view][pl.ds(n0, cols), :])
                 cst[view, pl.ds(n0, cols), :] = code[view].T
@@ -550,10 +568,11 @@
         lax.fori_loop(i * 2, i * 2 + 2, body, 0, unroll=True)
 
     def lbody(q, acc):
-        for h in range(2):
+        for h in VIEWS:
             acc = acc + other_codes(q, h) * (lrow[q, :, lanes(h)] - ld)
         return acc
     part = lax.fori_loop(0, blocks, lbody, jnp.zeros((both, LANES), F32), unroll=4)
+    grun('A10P')
     lossb[0, pos[0]] = jnp.sum(part.reshape(both // 8, 8, LANES), axis=0)
 
     def loss_send(st):
@@ -567,20 +586,20 @@
         return (lossb[st, 0] + lossb[st, 1]) + (lossb[st, 2] + lossb[st, 3])
 
     loss_send(0)
-    grun('sA11A13A12Q')
+    grun('sA11A13A12f10B10Q')
 
     @pl.when(core == 1)
     def _():
         for (l0, l1), t in zip(_parts(SUM_CUTS), recv_sums(ITERS - 1, AXES - 1)):
             dall[0:2, l0:l1] = t
-        remote(dall.at[:, rows:], dall.at[:, :rows], x_ssem.at[3], x_rsem.at[3], partner)
+        remote(dall.at[:, rows:], dall.at[:, :rows], x_ssem.at[3], x_rsem.at[4], partner)
 
     lossb[1, pos[1]] = loss_recv(0)
     loss_send(1)
-    grun('f10B10f11B11f13B13f12B12g10g11A21g13g12A23')
+    grun('f11B11f13B13f12B12g10g11A21g13g12A23')
     lossb[2, pos[2]] = loss_recv(1)
     loss_send(2)
-    pl.when(core == 0)(lambda: env.arrived(dall.at[:, :rows], x_rsem.at[3]))
+    pl.when(core == 0)(lambda: env.arrived(dall.at[:, :rows], x_rsem.at[4]))
     columns(0)
     grun('f20B20b10b11b13b12A22')
     columns(1)
@@ -608,7 +627,8 @@
 
     @pl.when(core == 1)
     def _():
-        env.sent(sums.at[:, :, :LINE - 1], s_ssem.at[0])
+        for i, ref in enumerate((sums.at[0, 0, :AXES, :, :rows], sums.at[0, 1:, :AXES], sums.at[1:, :, :AXES])):
+            env.sent(ref, s_ssem.at[i])
         for i, ref in enumerate((vall.at[:LINE - 1], vall.at[0, :LINE - 1], vall.at[0, 0, :LINE - 1], vall)):
             env.sent(ref, v_ssem.at[i])
         env.sent(dall.at[:, rows:], x_ssem.at[3])
@@ -628,7 +648,6 @@
         vm = pl.BlockSpec(memory_space=pltpu.VMEM)
         hbm = pl.BlockSpec(memory_space=pltpu.HBM)
         free = pl.BlockSpec(memory_space=pl.ANY)
-        nsem = (ITERS + 1) * AXES
         dma = lambda n: pltpu.SemaphoreType.DMA((n,))
         one, few, many = dma(1), dma(5), dma(AG_SEMS)
         pair = 2 * mine
@@ -668,7 +687,7 @@
                 pltpu.VMEM(packed, F32),
                 pltpu.VMEM((2, rows, cols), F32),
                 pltpu.VMEM((4, LANES), F32),
-                few, one, one, one, dma(nsem),
+                few, one, one, few,
                 few, many, one, few, few, one, few, many, few, few, few, few, few,
             ],
             compiler_params=pltpu.CompilerParams(collective_id=0, has_side_effects=True,

time: 66.9 us -> 65.9 us (0.985)
  Pallas kernels: 64.4 us -> 63.2 us
    pallas_call x1, Pallas kernels: 60.9 us -> 59.7 us  [local_step(): pl.pallas_call(functools.partial(step_kernel, total_rows, total_protos),...]
where the time goes in v9:
time: 65.9 us; the launch traced here: 65.6 us
  Pallas kernels  63.2 us (96%)
  between operations  2.41 us (4%)
    pallas_call x1, Pallas kernels, local_step(): pl.pallas_call(functools.partial(step_kernel, total_rows, total_protos),...  59.7 us
    pallas_call x1, Pallas kernels, local_step(): pl.pallas_call(functools.partial(write_kernel, mine), out_shape=(code, co...  3.46 us

profile of v9, /device:TPU:0, one launch (start us, length us, event | category | flops | bytes accessed | tf_op | source)
XLA Modules:
  0.0 65.6 jit_solution(4718432680088957918)
XLA Ops:
  0.6 59.7 %shard_map.82 = (f32[2048,256]{1,0:T(8,128)S(1)}, f32[2048,256]{1,0:T(8,128)S(1)}, f32[1,1]{1,0:T(1,128)}, f32[4,4,4,128,128]{4,3,2,1,0:T(8,128)S(1)}, f32[256,256]{1,0:T(8,128)S(1)}) custom-call(bf16[2048,256]{1,0:T(8,128)(2,1)} %z1h.1, bf16[2048,256]{1,0:T(8,128)(2,1)} %z2h.1, bf16[256,256]{1,0:T(8,128)(2,1)} %ch.1), custom_call_target="tpu_custom_call" | custom-call | tf_op jit(solution)/shard_map/pallas_call | solution.py:664
  60.4 3.5 %shard_map.83 = (f32[2048,256]{1,0:T(8,128)}, f32[2048,256]{1,0:T(8,128)}, f32[64,32,256]{2,1,0:T(8,128)}, f32[64,32,256]{2,1,0:T(8,128)}, f32[256,256]{1,0:T(8,128)}) custom-call(f32[2048,256]{1,0:T(8,128)S(1)} %get-tuple-element.16.code1, f32[2048,256]{1,0:T(8,128)S(1)} %get-tuple-element.17.code2, f32[64,128,128]{2,1,0:T(8,128)S(1)} %bitcast.4, ...), custom_call_target="tpu_custom_call" | custom-call | tf_op jit(solution)/shard_map/pallas_call | solution.py:697

commit v10 on v9

--- a/solution.py
+++ b/solution.py
@@ -21,7 +21,7 @@
 SUM_CUTS = (0, 1408, 2816, 4096)
 C_CUTS = (0, 88, 168, 256)
 G_CUTS = ((0, 40, 88, 128), (0, 40, 80, 128))
-AG_SEMS = 27
+AG_SEMS = 25
 DISTS = (2, 1, 3)
 WAYS = (1, 3)
 
@@ -121,11 +121,10 @@
         for d in DISTS:
             for j, (r0, r1) in enumerate(self.parts):
                 ref = self.at(j, self.p(j, 0, 0), self.p(j, 1, 0), self.p(j, 2, 0))
-                self.send(j, 0, d - 1, ref, 0, d, None if src is None else src.at[r0:r1, :])
+                self.send(j, 0, 0, ref, 0, d, None if src is None else src.at[r0:r1, :])
 
     def s1_recv(self):
-        for d in DISTS:
-            self.recv(d - 1, 1)
+        self.recv(0, 3)
 
     def chunk(self, j, level, k, m):
         if level == 1:
@@ -133,7 +132,7 @@
         return self.at(j, None, self.p(j, 1, k), self.p(j, 2, m))
 
     def slot(self, level, k, d):
-        return 12 * level - 9 + k + LINE * (d // 2)
+        return 1 + 12 * (level - 1) + k + LINE * (d // 2)
 
     def a_send(self, level, k):
         for j in range(AXES):
@@ -327,7 +326,7 @@
             def body(g, acc, view=view):
                 w = vb[view, pl.ds(pl.multiple_of(g * 8, 8), 8), :]
                 return tuple(a + e_scr[view, g, :, ls] * w for a, ls in zip(acc, tiles))
-            acc = lax.fori_loop(0, groups, body, tuple(jnp.zeros((8, LANES), F32) for _ in tiles), unroll=4)
+            acc = lax.fori_loop(0, groups, body, tuple(jnp.zeros((8, LANES), F32) for _ in tiles), unroll=8)
             for a, ls in zip(acc, tiles):
                 stage[it, view:view + 1, ls] = jnp.sum(a, axis=0, keepdims=True)
 
@@ -341,7 +340,7 @@
                 chains = [sum(terms[t::LINE][1:], terms[t]) for t in range(LINE)]
                 cacc[view, pl.ds(pl.multiple_of(g * 8, 8), 8), :] = (chains[0] + chains[1]) + (chains[2] + chains[3])
                 return 0
-            lax.fori_loop(0, groups, body, 0, unroll=4)
+            lax.fori_loop(0, groups, body, 0, unroll=8)
 
     def at_offset(oz, oy, ox):
         return (env.p(2, oz) * LINE + env.p(1, oy)) * LINE + env.p(0, ox)
@@ -354,10 +353,10 @@
             for oy in order:
                 for ox in order:
                     there = at_offset(oz, oy, ox)
-                    remote(vsrc, dst, v_ssem.at[3], v_rsem.at[0], (there, 0))
                     if oz or oy or ox:
                         group = 0 if oz else 1 if oy else 2
                         remote(vsrc, dst, v_ssem.at[group], v_rsem.at[0], (there, 1))
+                    remote(vsrc, dst, v_ssem.at[3], v_rsem.at[0], (there, 0))
 
     def within(lo, hi):
         return [(j, max(l0, lo), min(l1, hi)) for j, (l0, l1) in enumerate(_parts(SUM_CUTS)) if l0 < hi and l1 > lo]
@@ -411,9 +410,8 @@
         if slot in (1, 2):
             env.arrived(ys[slot - 1], x_rsem.at[slot - 1])
             other_scores(slot - 1)
-        if slot in (3, 4, 5, 6):
-            denominators(slot - 3)
         if slot == 6:
+            denominators(0)
             gc.run('U0R0R1R2U1R3R4R5U2R6')
 
     @pl.when(core == 1)
@@ -441,6 +439,7 @@
                 tot = recv_sums(it, st)
                 if last:
                     send_sums(it, 1)
+                    denominators(1)
                     break
                 if st < AXES - 1:
                     continue
@@ -510,7 +509,7 @@
 
     zero = jnp.zeros((both, LANES), F32)
     rsum, den = (jnp.sum(a, axis=1, keepdims=True)
-                 for a in lax.fori_loop(0, blocks, sumbody, (zero, zero), unroll=4))
+                 for a in lax.fori_loop(0, blocks, sumbody, (zero, zero), unroll=8))
     rc = jnp.broadcast_to(1.0 / rsum, (both, LANES))
     dc = jnp.broadcast_to(1.0 / den, (both, LANES))
     ld = jnp.broadcast_to(jnp.log(den), (both, LANES))
@@ -529,7 +528,7 @@
         cl = cfull[lax.div(i, LINE), lax.rem(i, LINE)].reshape(LINE * cols, cols)
         return acc + _nn(jnp.concatenate(hs, axis=1), cl)
 
-    rowgrad = lax.fori_loop(0, LINE * LINE, dzbody, jnp.zeros((both, cols), F32), unroll=4)
+    rowgrad = lax.fori_loop(0, LINE * LINE, dzbody, jnp.zeros((both, cols), F32), unroll=8)
     dz[...] = jnp.concatenate([rowgrad[:, :LANES], rowgrad[:, LANES:]], axis=0)
 
     own = pltpu.make_async_copy(dz, gfull.at[pos[2], pos[1], pos[0]], o_sem.at[0])
@@ -541,6 +540,7 @@
     def _():
         recv_sums(ITERS - 1, 1)
         send_sums(ITERS - 1, 2)
+        denominators(2)
 
     spread(vall[pos[2], pos[1], pos[0]])
     dacc[...] = jnp.zeros((cols, cols), F32)
@@ -592,6 +592,7 @@
     def _():
         for (l0, l1), t in zip(_parts(SUM_CUTS), recv_sums(ITERS - 1, AXES - 1)):
             dall[0:2, l0:l1] = t
+        denominators(AXES)
         remote(dall.at[:, rows:], dall.at[:, :rows], x_ssem.at[3], x_rsem.at[4], partner)
 
     lossb[1, pos[1]] = loss_recv(0)

time: 65.9 us -> 65.4 us (level)
  Pallas kernels: 63.2 us -> 62.3 us
    pallas_call x1, Pallas kernels: 59.7 us -> 58.8 us  [local_step(): pl.pallas_call(functools.partial(step_kernel, total_rows, total_protos),...]
where the time goes in v10:
time: 65.4 us; the launch traced here: 64.7 us
  Pallas kernels  62.3 us (95%)
  between operations  2.41 us (4%)
    pallas_call x1, Pallas kernels, local_step(): pl.pallas_call(functools.partial(step_kernel, total_rows, total_protos),...  58.8 us
    pallas_call x1, Pallas kernels, local_step(): pl.pallas_call(functools.partial(write_kernel, mine), out_shape=(code, co...  3.46 us

profile of v10, /device:TPU:0, one launch (start us, length us, event | category | flops | bytes accessed | tf_op | source)
XLA Modules:
  0.0 64.7 jit_solution(17339549321761515254)
XLA Ops:
  0.6 58.8 %shard_map.82 = (f32[2048,256]{1,0:T(8,128)S(1)}, f32[2048,256]{1,0:T(8,128)S(1)}, f32[1,1]{1,0:T(1,128)}, f32[4,4,4,128,128]{4,3,2,1,0:T(8,128)S(1)}, f32[256,256]{1,0:T(8,128)S(1)}) custom-call(bf16[2048,256]{1,0:T(8,128)(2,1)} %z1h.1, bf16[2048,256]{1,0:T(8,128)(2,1)} %z2h.1, bf16[256,256]{1,0:T(8,128)(2,1)} %ch.1), custom_call_target="tpu_custom_call" | custom-call | tf_op jit(solution)/shard_map/pallas_call | solution.py:665
  59.4 3.5 %shard_map.83 = (f32[2048,256]{1,0:T(8,128)}, f32[2048,256]{1,0:T(8,128)}, f32[64,32,256]{2,1,0:T(8,128)}, f32[64,32,256]{2,1,0:T(8,128)}, f32[256,256]{1,0:T(8,128)}) custom-call(f32[2048,256]{1,0:T(8,128)S(1)} %get-tuple-element.16.code1, f32[2048,256]{1,0:T(8,128)S(1)} %get-tuple-element.17.code2, f32[64,128,128]{2,1,0:T(8,128)S(1)} %bitcast.4, ...), custom_call_target="tpu_custom_call" | custom-call | tf_op jit(solution)/shard_map/pallas_call | solution.py:698

commit v11 on v10

--- a/solution.py
+++ b/solution.py
@@ -21,7 +21,7 @@
 SUM_CUTS = (0, 1408, 2816, 4096)
 C_CUTS = (0, 88, 168, 256)
 G_CUTS = ((0, 40, 88, 128), (0, 40, 80, 128))
-AG_SEMS = 25
+AG_SEMS = 22
 DISTS = (2, 1, 3)
 WAYS = (1, 3)
 
@@ -132,7 +132,7 @@
         return self.at(j, None, self.p(j, 1, k), self.p(j, 2, m))
 
     def slot(self, level, k, d):
-        return 1 + 12 * (level - 1) + k + LINE * (d // 2)
+        return 1 + 9 * (level - 1) + k + LINE * (d // 2)
 
     def a_send(self, level, k):
         for j in range(AXES):
@@ -165,10 +165,10 @@
     def b_send(self, level, k):
         d = self.way(k)
         for j in range(AXES):
-            self.send(j, 2 * level, self.slot(level, k, 5), self.chunk(j, level, k, LINE - d), level, d)
+            self.send(j, 2 * level, self.slot(level, k if level > 1 else 0, 5), self.chunk(j, level, k, LINE - d), level, d)
 
     def b_recv(self, level, k):
-        self.recv(self.slot(level, k, 5), LINE ** (level - 1))
+        self.recv(self.slot(level, k, 5), LINE)
 
     def t_send(self, k, m):
         ts, tr = self.twin
@@ -477,7 +477,7 @@
             remote(zs[i], ys[i], x_ssem.at[i], x_rsem.at[i], partner)
         gc.run('sA11A13A12QT00')
         gc.run('f10B10f11B11f13B13f12B12g10g11A21g13g12A23')
-        gc.run('f20B20b10b11b13b12A22T10T30T20')
+        gc.run('f20B20b10A22T10T30T20')
         gc.run('f21B21f23B23g20g21g23T01T03T11T13T31T33R0')
         gc.run('f22B22R1g22T21T23b20T02b21T12R2')
         gc.run('b23T32R3b22T22R4R5R6')
@@ -602,7 +602,7 @@
     loss_send(2)
     pl.when(core == 0)(lambda: env.arrived(dall.at[:, :rows], x_rsem.at[4]))
     columns(0)
-    grun('f20B20b10b11b13b12A22')
+    grun('f20B20b10A22')
     columns(1)
     columns(2)
     grun('f21B21f23B23')
@@ -650,7 +650,7 @@
         hbm = pl.BlockSpec(memory_space=pltpu.HBM)
         free = pl.BlockSpec(memory_space=pl.ANY)
         dma = lambda n: pltpu.SemaphoreType.DMA((n,))
-        one, few, many = dma(1), dma(5), dma(AG_SEMS)
+        one, four, few, many = dma(1), dma(4), dma(5), dma(AG_SEMS)
         pair = 2 * mine
         grid3 = (LINE,) * AXES
         packed = (pair * dim // LANES, LANES)
@@ -688,8 +688,8 @@
                 pltpu.VMEM(packed, F32),
                 pltpu.VMEM((2, rows, cols), F32),
                 pltpu.VMEM((4, LANES), F32),
-                few, one, one, few,
-                few, many, one, few, few, one, few, many, few, few, few, few, few,
+                four, one, one, four,
+                few, many, one, four, four, one, few, many, few, few, four, few, four,
             ],
             compiler_params=pltpu.CompilerParams(collective_id=0, has_side_effects=True,
                                                  vmem_limit_bytes=44 * 2 ** 20),

time: 65.4 us -> 65.3 us (level)
  no operation moved by 1% of the time
where the time goes in v11:
time: 65.3 us; the launch traced here: 64.6 us
  Pallas kernels  62.1 us (95%)
  between operations  2.41 us (4%)
    pallas_call x1, Pallas kernels, local_step(): pl.pallas_call(functools.partial(step_kernel, total_rows, total_protos),...  58.7 us
    pallas_call x1, Pallas kernels, local_step(): pl.pallas_call(functools.partial(write_kernel, mine), out_shape=(code, co...  3.46 us

profile of v11, /device:TPU:0, one launch (start us, length us, event | category | flops | bytes accessed | tf_op | source)
XLA Modules:
  0.0 64.6 jit_solution(3797698073061243741)
XLA Ops:
  0.6 58.7 %shard_map.82 = (f32[2048,256]{1,0:T(8,128)S(1)}, f32[2048,256]{1,0:T(8,128)S(1)}, f32[1,1]{1,0:T(1,128)}, f32[4,4,4,128,128]{4,3,2,1,0:T(8,128)S(1)}, f32[256,256]{1,0:T(8,128)S(1)}) custom-call(bf16[2048,256]{1,0:T(8,128)(2,1)} %z1h.1, bf16[2048,256]{1,0:T(8,128)(2,1)} %z2h.1, bf16[256,256]{1,0:T(8,128)(2,1)} %ch.1), custom_call_target="tpu_custom_call" | custom-call | tf_op jit(solution)/shard_map/pallas_call | solution.py:665
  59.3 3.5 %shard_map.83 = (f32[2048,256]{1,0:T(8,128)}, f32[2048,256]{1,0:T(8,128)}, f32[64,32,256]{2,1,0:T(8,128)}, f32[64,32,256]{2,1,0:T(8,128)}, f32[256,256]{1,0:T(8,128)}) custom-call(f32[2048,256]{1,0:T(8,128)S(1)} %get-tuple-element.16.code1, f32[2048,256]{1,0:T(8,128)S(1)} %get-tuple-element.17.code2, f32[64,128,128]{2,1,0:T(8,128)S(1)} %bitcast.4, ...), custom_call_target="tpu_custom_call" | custom-call | tf_op jit(solution)/shard_map/pallas_call | solution.py:698
